TPU v7x, 32 devices: a whole 2x2x4 slice. The times are simulated.
32 devices in a mesh: seq: 8 (over z, y), head: 4 (over x, core).
Axes of the slice: x: 2, y: 2, z: 4, core: 2. Of those that a mesh axis runs over, the one named last changes fastest.
Arguments:
- query_rows: bfloat16 [16384, 4096], P(('seq', 'head')), may hold values from -200 to 200
- key_rows: bfloat16 [16384, 512], P(('seq', 'head')), may hold values from -18 to 18
- value_rows: bfloat16 [16384, 512], P(('seq', 'head')), may hold values from -6 to 6
- random_table: int32 [128, 4, 3], replicated, may hold values from 0 to 127, as said below
- global_blocks: int32 [2], replicated, may hold values from 0 to 127
Outputs:
- attended: bfloat16 [16384, 4096], P(('seq', 'head'))
Inputs may be any that keep to these rules, and one draw needn't show every extreme that they name: `random_table`: for each of the 4 head groups and each aligned run of 16 query blocks (those of one index of seq), with the owner of block j being j // 16: at most 6 of the run's 3 * 16 entries name blocks of one owner, and they name at most 3 distinct blocks of one owner; both bounds are reached.
All inputs are finite; a program needn't handle non-finite values.
Results may differ from a plain program's by a relative error of at most 0.0029.
Values may be sent and summed in bfloat16 or wider, within the bound.
No kernel may reach another device: no remote copies, remote signals or barrier semaphores. Data moves between devices by JAX's collectives and lax.ppermute only.
A program may use at most 128 MiB of HBM per device.

v0:
```python
import functools
import math

import jax
import jax.numpy as jnp
from jax import lax
from jax.experimental import pallas as pl
from jax.experimental.pallas import tpu as pltpu
from jax.sharding import PartitionSpec as P


BLOCK = 128
HEAD_DIM = 128
GLOBALS = 2
RANDOM = 3
WINDOW = 3
MIB = 2**20
SOME_VMEM = 20 * MIB
MOST_VMEM = 60 * MIB


ANY = pl.BlockSpec(memory_space=pl.ANY)
SMEM = pl.BlockSpec(memory_space=pltpu.SMEM)
VMEM = pl.BlockSpec(memory_space=pltpu.VMEM)


def run_copies(copies):
    for copy in copies:
        copy.start()
    for copy in copies:
        copy.wait()


def pack_kernel(heads, order, key_ref, value_ref, *rest):
    outs, first, last = rest[:heads], rest[heads], rest[heads + 1]
    parts, edges, sem_in, sem_out, sem_edge_in, sem_edge_out = rest[heads + 2 :]
    rows = key_ref.shape[0]
    loads = []
    for r in range(heads):
        lanes = pl.ds(pl.multiple_of(order[r] * HEAD_DIM, HEAD_DIM), HEAD_DIM)
        for which, source in enumerate((key_ref, value_ref)):
            loads.append(
                pltpu.make_async_copy(
                    source.at[:, lanes], parts.at[r, which], sem_in.at[r, which]
                )
            )
    for which, source in enumerate((key_ref, value_ref)):
        for side, start in enumerate((0, rows - BLOCK)):
            loads.append(
                pltpu.make_async_copy(
                    source.at[start : start + BLOCK],
                    edges.at[side, which],
                    sem_edge_in.at[side, which],
                )
            )
    run_copies(loads)
    run_copies(
        [pltpu.make_async_copy(parts.at[r], outs[r], sem_out.at[r]) for r in range(heads)]
        + [
            pltpu.make_async_copy(edges.at[side], out, sem_edge_out.at[side])
            for side, out in enumerate((first, last))
        ]
    )


def pack(order, key_rows, value_rows):
    rows, columns = key_rows.shape
    heads = columns // HEAD_DIM
    part = jax.ShapeDtypeStruct((2, rows, HEAD_DIM), key_rows.dtype)
    edge = jax.ShapeDtypeStruct((2, BLOCK, columns), key_rows.dtype)
    return pl.pallas_call(
        functools.partial(pack_kernel, heads),
        in_specs=[SMEM, ANY, ANY],
        out_specs=[ANY] * (heads + 2),
        out_shape=[part] * heads + [edge] * 2,
        scratch_shapes=[
            pltpu.VMEM((heads, 2, rows, HEAD_DIM), key_rows.dtype),
            pltpu.VMEM((2, 2, BLOCK, columns), key_rows.dtype),
            pltpu.SemaphoreType.DMA((heads, 2)),
            pltpu.SemaphoreType.DMA((heads,)),
            pltpu.SemaphoreType.DMA((2, 2)),
            pltpu.SemaphoreType.DMA((2,)),
        ],
        compiler_params=pltpu.CompilerParams(vmem_limit_bytes=MOST_VMEM),
        name="pack",
    )(order, key_rows, value_rows)


def pick_kernel(heads, chunks, slots, order, sources, shared, *rest):
    parts, rest = rest[:heads], rest[heads:]
    outs, shared_ref, (run, sem_in, sem_out) = rest[:chunks], rest[chunks], rest[chunks + 1 :]
    rows = parts[0].shape[1]
    loads = []
    for r in range(heads):
        place = pl.ds(pl.multiple_of(order[r] * rows, BLOCK), rows)
        loads.append(pltpu.make_async_copy(parts[r], run.at[:, place], sem_in.at[r]))
    run_copies(loads)
    stores = []
    for chunk in range(chunks):
        for slot in range(slots):
            place = pl.ds(pl.multiple_of(sources[chunk * slots + slot] * BLOCK, BLOCK), BLOCK)
            stores.append(
                pltpu.make_async_copy(
                    run.at[:, place],
                    outs[chunk].at[:, slot * BLOCK : (slot + 1) * BLOCK],
                    sem_out.at[chunk, slot],
                )
            )
    for copy in stores:
        copy.start()
    for which in range(GLOBALS):
        place = pl.ds(pl.multiple_of(shared[2 * which] * BLOCK, BLOCK), BLOCK)
        block = run[:, place]
        shared_ref[:, which * BLOCK : (which + 1) * BLOCK] = jnp.where(
            shared[2 * which + 1] != 0, block, jnp.zeros_like(block)
        )
    for copy in stores:
        copy.wait()


def pick(order, sources, shared, parts, chunks, slots):
    heads = len(parts)
    rows, dtype = parts[0].shape[1], parts[0].dtype
    return pl.pallas_call(
        functools.partial(pick_kernel, heads, chunks, slots),
        in_specs=[SMEM, SMEM, SMEM] + [ANY] * heads,
        out_specs=[ANY] * chunks + [VMEM],
        out_shape=[jax.ShapeDtypeStruct((2, slots * BLOCK, HEAD_DIM), dtype)] * chunks
        + [jax.ShapeDtypeStruct((2, GLOBALS * BLOCK, HEAD_DIM), dtype)],
        scratch_shapes=[
            pltpu.VMEM((2, heads * rows, HEAD_DIM), dtype),
            pltpu.SemaphoreType.DMA((heads,)),
            pltpu.SemaphoreType.DMA((chunks, slots)),
        ],
        compiler_params=pltpu.CompilerParams(vmem_limit_bytes=SOME_VMEM),
        name="pick",
    )(order, sources, shared, *parts)


def join_kernel(count, *refs):
    sources, out_ref, sems = refs[:count], refs[count], refs[count + 1]
    copies, start = [], 0
    for place, source in enumerate(sources):
        size = source.shape[1]
        copies.append(
            pltpu.make_async_copy(source, out_ref.at[:, start : start + size], sems.at[place])
        )
        start += size
    run_copies(copies)


def join(arrays):
    rows = sum(array.shape[1] for array in arrays)
    shape = (2, rows, HEAD_DIM)
    return pl.pallas_call(
        functools.partial(join_kernel, len(arrays)),
        in_specs=[ANY] * len(arrays),
        out_specs=VMEM,
        out_shape=jax.ShapeDtypeStruct(shape, arrays[0].dtype),
        scratch_shapes=[pltpu.SemaphoreType.DMA((len(arrays),))],
        compiler_params=pltpu.CompilerParams(vmem_limit_bytes=SOME_VMEM),
        name="join",
    )(*arrays)


SCALE = math.log2(math.e) / math.sqrt(HEAD_DIM)
JOINED = 2
TOGETHER = 2


def stacked(ref, rows, head):
    return jnp.concatenate(
        [ref[rows, (head + j) * HEAD_DIM : (head + j + 1) * HEAD_DIM] for j in range(JOINED)],
        axis=0,
    )


def score_block(query, keys):
    return lax.dot_general(
        query, keys, (((1,), (1,)), ((), ())), preferred_element_type=jnp.float32
    )


def weighted(scores, top, values):
    weights = jnp.concatenate(
        [
            jnp.exp2((scores[:, start : start + HEAD_DIM] - top) * SCALE)
            for start in range(0, scores.shape[1], HEAD_DIM)
        ],
        axis=1,
    )
    both = jnp.concatenate([values, jnp.ones_like(values)], axis=1)
    mixed = jnp.dot(weights.astype(values.dtype), both, preferred_element_type=jnp.float32)
    return mixed[:, :HEAD_DIM], mixed[:, HEAD_DIM:]


def pipelined(tasks, scores_of, rest_of):
    scores = scores_of(*tasks[0])
    for place, task in enumerate(tasks):
        upcoming = scores_of(*tasks[place + 1]) if place + 1 < len(tasks) else None
        rest_of(*task, scores)
        scores = upcoming


def window_kernel(parts, order, flags, query_ref, *rest):
    locals_, (before_ref, after_ref), rest = rest[:parts], rest[parts : parts + 2], rest[parts + 2 :]
    out_ref, level_ref, held = rest
    part, step = pl.program_id(0), pl.program_id(1)
    _, width = query_ref.shape
    grouping = width // HEAD_DIM
    inner = locals_[0].shape[1]
    for r in range(parts):

        @pl.when((part == r) & (step == 0))
        def _(r=r):
            held[:, BLOCK : BLOCK + inner] = locals_[r][...]
            held[:, :BLOCK] = before_ref[...]
            held[:, BLOCK + inner :] = after_ref[...]

    def listed(which, unit):
        place = pl.ds(pl.multiple_of((step * TOGETHER + unit) * BLOCK, BLOCK), WINDOW * BLOCK)
        return held[which, place]

    def scores_of(unit, head):
        block = step * TOGETHER + unit
        scores = score_block(
            stacked(query_ref, slice(unit * BLOCK, (unit + 1) * BLOCK), head), listed(0, unit)
        )
        return jnp.concatenate(
            [
                jnp.where(flags[2 * block] != 0, scores[:, :BLOCK], -1e30),
                scores[:, BLOCK : 2 * BLOCK],
                jnp.where(flags[2 * block + 1] != 0, scores[:, 2 * BLOCK :], -1e30),
            ],
            axis=1,
        )

    def rest_of(unit, head, scores):
        top = jnp.broadcast_to(
            jnp.max(scores, axis=1, keepdims=True), (scores.shape[0], HEAD_DIM)
        )
        mixed, total = weighted(scores, top, listed(1, unit))
        mixed = mixed * (1.0 / total)
        level = top + jnp.log(total) * math.sqrt(HEAD_DIM)
        for j in range(JOINED):
            some = slice(j * BLOCK, (j + 1) * BLOCK)
            rows = slice(unit * BLOCK, (unit + 1) * BLOCK)
            lanes = slice((head + j) * HEAD_DIM, (head + j + 1) * HEAD_DIM)
            out_ref[0, rows, lanes] = mixed[some]
            level_ref[0, rows, lanes] = level[some]

    tasks = [(unit, head) for unit in range(TOGETHER) for head in range(0, grouping, JOINED)]
    pipelined(tasks, scores_of, rest_of)


def whole_block(array):
    return pl.BlockSpec(array.shape, lambda *_: (0,) * array.ndim)


def window_share(order, flags, queries, locals_, edges):
    rows, columns = queries.shape
    heads = edges[0].shape[2] // HEAD_DIM
    width = columns // heads
    blocks = rows // BLOCK
    parts = len(locals_)
    pairs = parts * blocks * (width // HEAD_DIM) * BLOCK * WINDOW * BLOCK
    some = TOGETHER * BLOCK
    edge = pl.BlockSpec((2, BLOCK, HEAD_DIM), lambda r, i, order, flags: (0, 0, order[r]))
    return pl.pallas_call(
        functools.partial(window_kernel, parts),
        grid_spec=pltpu.PrefetchScalarGridSpec(
            num_scalar_prefetch=2,
            grid=(parts, blocks // TOGETHER),
            in_specs=[pl.BlockSpec((some, width), lambda r, i, order, flags: (i, order[r]))]
            + [whole_block(array) for array in locals_]
            + [edge, edge],
            out_specs=[pl.BlockSpec((1, some, width), lambda r, i, order, flags: (r, i, 0))] * 2,
            scratch_shapes=[pltpu.VMEM((2, rows + 2 * BLOCK, HEAD_DIM), queries.dtype)],
        ),
        out_shape=[jax.ShapeDtypeStruct((parts, rows, width), jnp.float32)] * 2,
        compiler_params=pltpu.CompilerParams(vmem_limit_bytes=MOST_VMEM),
        cost_estimate=pl.CostEstimate(
            flops=4 * pairs * HEAD_DIM, bytes_accessed=8 * MIB, transcendentals=pairs
        ),
        name="window",
    )(order, flags, queries, *locals_, *edges)


LISTED = GLOBALS + RANDOM


def finish_kernel(counts, aliased, order, table, query_ref, mixed_ref, level_ref, *rest):
    sources, (out_ref, held) = rest[: sum(counts)], rest[sum(counts) + aliased :]
    part, step = pl.program_id(0), pl.program_id(1)
    grouping = query_ref.shape[1] // HEAD_DIM
    number = 0
    for r, count in enumerate(counts):

        @pl.when((part == r) & (step == 0))
        def _(mine=sources[number : number + count]):
            start = 0
            for source in mine:
                held[:, start : start + source.shape[1]] = source[...]
                start += source.shape[1]

        number += count
    base = (part * pl.num_programs(1) + step) * TOGETHER * LISTED

    def listed(which, unit):
        return jnp.concatenate(
            [
                held[
                    which,
                    pl.ds(pl.multiple_of(table[base + unit * LISTED + n] * BLOCK, BLOCK), BLOCK),
                ]
                for n in range(LISTED)
            ],
            axis=0,
        )

    def scores_of(unit, head):
        return score_block(
            stacked(query_ref, slice(unit * BLOCK, (unit + 1) * BLOCK), head), listed(0, unit)
        )

    def rest_of(unit, head, scores):
        rows = slice(unit * BLOCK, (unit + 1) * BLOCK)
        level = stacked(level_ref.at[0], rows, head)
        top = jnp.maximum(level, jnp.max(scores, axis=1, keepdims=True))
        mixed, total = weighted(scores, top, listed(1, unit))
        kept = jnp.exp2((level - top) * SCALE)
        inverse = 1.0 / (total + kept)
        mixed = (mixed + stacked(mixed_ref.at[0], rows, head) * kept) * inverse
        for j in range(JOINED):
            lanes = slice((head + j) * HEAD_DIM, (head + j + 1) * HEAD_DIM)
            out_ref[rows, lanes] = mixed[j * BLOCK : (j + 1) * BLOCK].astype(out_ref.dtype)

    tasks = [(unit, head) for unit in range(TOGETHER) for head in range(0, grouping, JOINED)]
    pipelined(tasks, scores_of, rest_of)


def finish(order, table, queries, share, parts, output):
    rows, columns = queries.shape
    width = share[0].shape[2]
    blocks = rows // BLOCK
    arrays = [array for part in parts for array in part]
    pairs = len(parts) * blocks * (width // HEAD_DIM) * BLOCK * LISTED * BLOCK
    some = TOGETHER * BLOCK
    spec = pl.BlockSpec((some, width), lambda r, i, order, table: (i, order[r]))
    aliased = [] if output is None else [output]
    operands = (order, table, queries, *share, *arrays, *aliased)
    return pl.pallas_call(
        functools.partial(finish_kernel, [len(part) for part in parts], len(aliased)),
        grid_spec=pltpu.PrefetchScalarGridSpec(
            num_scalar_prefetch=2,
            grid=(len(parts), blocks // TOGETHER),
            in_specs=[
                spec,
            ]
            + [pl.BlockSpec((1, some, width), lambda r, i, order, table: (r, i, 0))] * 2
            + [whole_block(array) for array in arrays]
            + [ANY] * len(aliased),
            out_specs=spec,
            scratch_shapes=[
                pltpu.VMEM(
                    (2, sum(array.shape[1] for array in parts[0]), HEAD_DIM), queries.dtype
                ),
            ],
        ),
        out_shape=jax.ShapeDtypeStruct((rows, columns), queries.dtype),
        input_output_aliases={len(operands) - 1: 0} if aliased else {},
        compiler_params=pltpu.CompilerParams(vmem_limit_bytes=MOST_VMEM),
        cost_estimate=pl.CostEstimate(
            flops=4 * pairs * HEAD_DIM, bytes_accessed=8 * MIB, transcendentals=pairs
        ),
        name="finish",
    )(*operands)


def plan(random_table, seq_index, head_index, seq_count, heads, my_blocks, slots):
    blocks = random_table.shape[0]
    run_blocks = blocks // seq_count
    by_run = random_table.reshape(seq_count, run_blocks, heads, RANDOM)
    mine = lax.dynamic_index_in_dim(by_run, head_index, 2, keepdims=False)
    mine = mine.reshape(seq_count, run_blocks * RANDOM) - seq_index * run_blocks
    local = jnp.arange(run_blocks, dtype=jnp.int32)
    named = jnp.any(mine[:, None, :] == local[:, None], axis=2)
    rank = jnp.sum(named[:, None, :] & (local[None, :] < local[:, None]), axis=2)
    hit = named[:, None, :] & (rank[:, None, :] == jnp.arange(slots)[:, None])
    sources = jnp.sum(jnp.where(hit, local, 0), axis=2).astype(jnp.int32)
    run = lax.dynamic_index_in_dim(by_run, seq_index, 0, keepdims=False)
    run = run.transpose(1, 0, 2).reshape(heads, run_blocks * RANDOM)
    order_of = jnp.arange(run_blocks * RANDOM)
    earlier = order_of[None, :] < order_of[:, None]
    first = ~jnp.any((run[:, :, None] == run[:, None, :]) & earlier, axis=2)
    start = head_index * my_blocks * RANDOM
    wanted = lax.dynamic_slice_in_dim(run, start, my_blocks * RANDOM, 1)
    same = (wanted[:, :, None] // run_blocks) == (run[:, None, :] // run_blocks)
    below = run[:, None, :] < wanted[:, :, None]
    slot = jnp.sum(same & below & first[:, None, :], axis=2).astype(jnp.int32)
    return sources, wanted // run_blocks, slot


def on_device(query_rows, key_rows, value_rows, random_table, global_blocks):
    seq_count, heads = lax.axis_size("seq"), lax.axis_size("head")
    seq_index, head_index = lax.axis_index("seq"), lax.axis_index("head")
    rows = key_rows.shape[0]
    my_blocks = rows // BLOCK
    run_blocks = my_blocks * heads
    slots = max(1, (RANDOM * run_blocks + 2 * seq_count - 1) // (2 * seq_count))
    order = head_index ^ jnp.arange(heads, dtype=jnp.int32)
    chunk_of = seq_index ^ jnp.arange(seq_count, dtype=jnp.int32)

    def across(array, axis, bit):
        count = lax.axis_size(axis)
        return lax.ppermute(array, axis, [(i, i ^ bit) for i in range(count)])

    *parts, first, last = pack(order, key_rows, value_rows)
    arrived = [parts[0]] + [across(parts[r], "head", r) for r in range(heads - 1, 0, -1)][::-1]

    flat = seq_count * heads
    previous = lax.ppermute(last, ("seq", "head"), [(i, i + 1) for i in range(flat - 1)])
    upcoming = lax.ppermute(first, ("seq", "head"), [(i + 1, i) for i in range(flat - 1)])

    sources, owner, slot = plan(
        random_table, seq_index, head_index, seq_count, heads, my_blocks, slots
    )
    sources = jnp.take(sources, chunk_of, axis=0).reshape(-1)
    shared = jnp.stack(
        [global_blocks % run_blocks, (global_blocks // run_blocks == seq_index).astype(jnp.int32)],
        axis=1,
    ).reshape(-1)
    picked = pick(order, sources, shared, arrived, seq_count, slots)
    outgoing, common = picked[:seq_count], picked[seq_count]
    chunks = [outgoing[0]] + [across(outgoing[k], "seq", k) for k in range(1, seq_count)]
    bit = seq_count // 2
    while bit:
        common = common + across(common, "seq", bit)
        bit //= 2
    half, last_part = seq_count // 2, (seq_count + seq_count // 2) // 2
    own = [
        chunks[0],
        join(chunks[1:half]),
        join([common] + chunks[half:last_part]),
        join(chunks[last_part:]),
    ]
    groups = {0: own}
    bit = heads // 2
    while bit:
        for r in sorted(groups):
            groups[r + bit] = [across(array, "head", bit) for array in groups[r]]
        bit //= 2

    local = jnp.arange(my_blocks, dtype=jnp.int32)
    chunk = owner ^ seq_index
    place = chunk * slots + slot + jnp.where(chunk >= half, GLOBALS, 0)
    place = jnp.take(place, order, axis=0).reshape(heads, my_blocks, RANDOM)
    commons = half * slots + jnp.arange(GLOBALS, dtype=jnp.int32)
    commons = jnp.broadcast_to(commons, (heads, my_blocks, GLOBALS))
    table = jnp.concatenate([commons, place], axis=2).reshape(heads, -1)
    number = (seq_index * heads + head_index) * my_blocks + local
    flags = (
        jnp.stack([number > 0, number < seq_count * run_blocks - 1], axis=1)
        .astype(jnp.int32)
        .reshape(-1)
    )
    half_heads = heads // 2
    shares = []
    for some in (slice(0, half_heads), slice(half_heads, heads)):
        shares.append(
            window_share(
                order[some],
                flags,
                query_rows,
                parts[some],
                (previous, upcoming),
            )
        )
    output = None
    for n, (begin, end) in enumerate(((0, half_heads), (half_heads, heads))):
        output = finish(
            order[begin:end],
            table[begin:end].reshape(-1),
            query_rows,
            shares[n],
            [groups[r] for r in range(begin, end)],
            output,
        )
    return output


def solution(mesh):
    placed = (
        P(("seq", "head"), None),
        P(("seq", "head"), None),
        P(("seq", "head"), None),
        P(),
        P(),
    )

    return jax.shard_map(
        on_device, mesh=mesh, in_specs=placed, out_specs=P(("seq", "head"), None), check_vma=False
    )
```

profile of v0, /device:TPU:0, one launch (start us, length us, event | category | flops | bytes accessed | tf_op | source)
XLA Modules:
  0.0 152.3 jit_solution(13384955460048504798)
XLA Ops:
  0.0 0.5 iota_xor_fusion.order
  0.5 3.6 %pack.1 = (bf16[2,512,128]{2,1,0:T(8,128)(2,1)}, bf16[2,512,128]{2,1,0:T(8,128)(2,1)}, bf16[2,512,128]{2,1,0:T(8,128)(2,1)}, bf16[2,512,128]{2,1,0:T(8,128)(2,1)...) custom-call(s32[4]{0:T(128)} %iota_xor_fusion.order, bf16[512,512]{1,0:T(8,128)(2,1)} %key_ref.1, ...), custom_call_target="tpu_custom_call" | custom-call | tf_op jit(solution)/shard_map/pack/pallas_call | solution.py:71
  4.1 0.6 collective-permute-start.2
  4.6 2.6 %collective-permute-start.3 = (bf16[2,512,128]{2,1,0:T(8,128)(2,1)}, bf16[2,512,128]{2,1,0:T(8,128)(2,1)S(1)}, u32[]{:S(2)}, u32[]{:S(2)}) collective-permute-start(bf16[2,512,128]{2,1,0:T(8,128)(2,1)} %get-tuple-element.24.rest_0_), channel_id=1, source_target_pairs={{0,2},{1,3},{2,0},{3,1},{4,6},{5,7},{6,4},{7,5},{8,10},{9,11},{10,... | collective-permute-start | bytes 786440 | tf_op jit(solution)/shard_map/ppermute | solution.py:416
  7.3 0.7 fusion.10
  7.9 0.7 fusion.9
  8.6 0.8 reshape.210
  9.6 0.2 fusion
  9.8 0.2 convert_reduce_fusion
  10.0 0.1 select_reduce_fusion
  10.3 0.6 gather_fusion.1
  11.0 0.1 copy.20
  11.2 0.1 copy.13
  11.3 0.1 reshape.211
  11.5 0.1 copy.14
  11.6 0.1 copy.15
  11.7 0.2 and_reduce_fusion
  11.9 0.3 convert_reduce_fusion.1
  12.3 0.1 copy.16
  12.4 0.1 fusion.4
  12.5 2.1 %collective-permute-done.3.rest_2_ = bf16[2,512,128]{2,1,0:T(8,128)(2,1)S(1)} collective-permute-done((bf16[2,512,128]{2,1,0:T(8,128)(2,1)}, bf16[2,512,128]{2,1,0:T(8,128)(2,1)S(1)}, u32[]{:S(2)}, u32[]{:S(2)}) %collective-permute-start.3) | collective-permute-done | bytes 262176 | tf_op jit(solution)/shard_map/ppermute | solution.py:416
  14.6 5.1 %collective-permute-done.4.rest_3_ = bf16[2,512,128]{2,1,0:T(8,128)(2,1)S(1)} collective-permute-done((bf16[2,512,128]{2,1,0:T(8,128)(2,1)}, bf16[2,512,128]{2,1,0:T(8,128)(2,1)S(1)}, u32[]{:S(2)}, u32[]{:S(2)}) %collective-permute-start.4) | collective-permute-done | bytes 262176 | tf_op jit(solution)/shard_map/ppermute | solution.py:416
  19.7 0.9 copy-done.3
  20.6 0.6 copy-done.5
  21.2 2.3 %pick.1 = (bf16[2,384,128]{2,1,0:T(8,128)(2,1)S(1)}, bf16[2,384,128]{2,1,0:T(8,128)(2,1)S(1)}, bf16[2,384,128]{2,1,0:T(8,128)(2,1)S(1)}, bf16[2,384,128]{2,1,0:T...) custom-call(s32[4]{0:T(128)S(1)} %copy-done.5, ...), custom_call_target="tpu_custom_call" | custom-call | tf_op jit(solution)/shard_map/pick/pallas_call | solution.py:124
  23.5 2.6 %collective-permute-start.10 = (bf16[2,256,128]{2,1,0:T(8,128)(2,1)S(1)}, bf16[2,256,128]{2,1,0:T(8,128)(2,1)S(1)}, u32[]{:S(2)}, u32[]{:S(2)}) collective-permute-start(bf16[2,256,128]{2,1,0:T(8,128)(2,1)S(1)} %get-tuple-element.36), channel_id=1, source_target_pairs={{0,16},{4,20},{8,24},{12,28},{16,0},{20,4},{24,8},{28,12},{1,17},{... | collective-permute-start | bytes 393224 | tf_op jit(solution)/shard_map/ppermute | solution.py:416
  26.1 1.5 collective-permute-start.6
  27.6 5.3 %collective-permute-done.10 = bf16[2,256,128]{2,1,0:T(8,128)(2,1)S(1)} collective-permute-done((bf16[2,256,128]{2,1,0:T(8,128)(2,1)S(1)}, bf16[2,256,128]{2,1,0:T(8,128)(2,1)S(1)}, u32[]{:S(2)}, u32[]{:S(2)}) %collective-permute-start.10) | collective-permute-done | bytes 131104 | tf_op jit(solution)/shard_map/ppermute | solution.py:416
  33.0 0.8 collective-permute-start.11
  33.8 0.6 gather_fusion
  34.4 2.9 %collective-permute-start.16 = (bf16[2,384,128]{2,1,0:T(8,128)(2,1)S(1)}, bf16[2,384,128]{2,1,0:T(8,128)(2,1)S(1)}, u32[]{:S(2)}, u32[]{:S(2)}) collective-permute-start(bf16[2,384,128]{2,1,0:T(8,128)(2,1)S(1)} %get-tuple-element.39), channel_id=1, source_target_pairs={{0,24},{4,28},{8,16},{12,20},{16,8},{20,12},{24,0},{28,4},{1,25},{... | collective-permute-start | bytes 589832 | tf_op jit(solution)/shard_map/ppermute | solution.py:416
  37.3 2.0 %collective-permute-start.17 = (bf16[2,384,128]{2,1,0:T(8,128)(2,1)S(1)}, bf16[2,384,128]{2,1,0:T(8,128)(2,1)S(1)}, u32[]{:S(2)}, u32[]{:S(2)}) collective-permute-start(bf16[2,384,128]{2,1,0:T(8,128)(2,1)S(1)} %get-tuple-element.40), channel_id=1, source_target_pairs={{0,28},{4,24},{8,20},{12,16},{16,12},{20,8},{24,4},{28,0},{1,29},{... | collective-permute-start | bytes 589832 | tf_op jit(solution)/shard_map/ppermute | solution.py:416
  39.3 0.2 collective-permute-start.7
  39.5 1.8 %collective-permute-start.8 = (bf16[2,384,128]{2,1,0:T(8,128)(2,1)S(1)}, bf16[2,384,128]{2,1,0:T(8,128)(2,1)S(1)}, u32[]{:S(2)}, u32[]{:S(2)}) collective-permute-start(bf16[2,384,128]{2,1,0:T(8,128)(2,1)S(1)} %get-tuple-element.35), channel_id=1, source_target_pairs={{0,12},{4,8},{8,4},{12,0},{16,28},{20,24},{24,20},{28,16},{1,13},{... | collective-permute-start | bytes 589832 | tf_op jit(solution)/shard_map/ppermute | solution.py:416
  41.3 1.6 %collective-permute-start.12 = (bf16[2,256,128]{2,1,0:T(8,128)(2,1)S(1)}, bf16[2,256,128]{2,1,0:T(8,128)(2,1)S(1)}, u32[]{:S(2)}, u32[]{:S(2)}) collective-permute-start(bf16[2,256,128]{2,1,0:T(8,128)(2,1)S(1)} %add.110), channel_id=1, source_target_pairs={{0,4},{4,0},{8,12},{12,8},{16,20},{20,16},{24,28},{28,24},{1,5},{5... | collective-permute-start | bytes 393224 | tf_op jit(solution)/shard_map/ppermute | solution.py:416
  43.0 10.2 %collective-permute-done.7.refs_1_ = bf16[2,384,128]{2,1,0:T(8,128)(2,1)S(1)} collective-permute-done((bf16[2,384,128]{2,1,0:T(8,128)(2,1)S(1)}, bf16[2,384,128]{2,1,0:T(8,128)(2,1)S(1)}, u32[]{:S(2)}, u32[]{:S(2)}) %collective-permute-start.7) | collective-permute-done | bytes 196640 | tf_op jit(solution)/shard_map/ppermute | solution.py:416
  53.1 1.8 %collective-permute-start = (bf16[2,128,512]{2,1,0:T(8,128)(2,1)}, bf16[2,128,512]{2,1,0:T(8,128)(2,1)S(1)}, u32[]{:S(2)}, u32[]{:S(2)}) collective-permute-start(bf16[2,128,512]{2,1,0:T(8,128)(2,1)} %get-tuple-element.26), channel_id=1, source_target_pairs={{0,1},{1,2},{2,3},{3,4},{4,5},{5,6},{6,7},{7,8},{8,9},{9,10},{10,1... | collective-permute-start | bytes 786440 | tf_op jit(solution)/shard_map/ppermute | solution.py:422
  55.0 2.7 %collective-permute-done.8.refs_2_ = bf16[2,384,128]{2,1,0:T(8,128)(2,1)S(1)} collective-permute-done((bf16[2,384,128]{2,1,0:T(8,128)(2,1)S(1)}, bf16[2,384,128]{2,1,0:T(8,128)(2,1)S(1)}, u32[]{:S(2)}, u32[]{:S(2)}) %collective-permute-start.8) | collective-permute-done | bytes 196640 | tf_op jit(solution)/shard_map/ppermute | solution.py:416
  57.7 1.5 collective-permute-start.1
  59.2 0.4 join.3.rest_1_
  59.6 5.4 %collective-permute-start.13 = (bf16[2,384,128]{2,1,0:T(8,128)(2,1)S(1)}, bf16[2,384,128]{2,1,0:T(8,128)(2,1)S(1)}, u32[]{:S(2)}, u32[]{:S(2)}) collective-permute-start(bf16[2,384,128]{2,1,0:T(8,128)(2,1)S(1)} %get-tuple-element.37), channel_id=1, source_target_pairs={{0,16},{4,20},{8,24},{12,28},{16,0},{20,4},{24,8},{28,12},{1,17},{... | collective-permute-start | bytes 589832 | tf_op jit(solution)/shard_map/ppermute | solution.py:416
  65.0 0.9 collective-permute-start.14
  65.9 0.3 collective-permute-start.9
  66.3 0.3 join.5.rest_3_
  66.6 17.0 %collective-permute-done.13.refs_1_ = bf16[2,384,128]{2,1,0:T(8,128)(2,1)S(1)} collective-permute-done((bf16[2,384,128]{2,1,0:T(8,128)(2,1)S(1)}, bf16[2,384,128]{2,1,0:T(8,128)(2,1)S(1)}, u32[]{:S(2)}, u32[]{:S(2)}) %collective-permute-start.13) | collective-permute-done | bytes 196640 | tf_op jit(solution)/shard_map/ppermute | solution.py:416
  83.6 0.7 collective-permute-start.5
  84.3 0.3 join.4.rest_2_
  84.8 1.5 collective-permute-start.15
  86.4 5.0 %collective-permute-done.5.rest_0_ = bf16[2,384,128]{2,1,0:T(8,128)(2,1)S(1)} collective-permute-done((bf16[2,384,128]{2,1,0:T(8,128)(2,1)S(1)}, bf16[2,384,128]{2,1,0:T(8,128)(2,1)S(1)}, u32[]{:S(2)}, u32[]{:S(2)}) %collective-permute-start.5) | collective-permute-done | bytes 196640 | tf_op jit(solution)/shard_map/ppermute | solution.py:416
  91.4 0.7 collective-permute-start.18
  92.1 0.7 fusion.13
  92.8 0.6 collective-permute-start.20
  93.4 0.6 reshape.214.table
  94.0 0.6 reshape.215.flags
  94.6 0.6 reshape.212.table
  95.2 7.5 %collective-permute-done.15.rest_2_ = bf16[2,1024,128]{2,1,0:T(8,128)(2,1)} collective-permute-done((bf16[2,1024,128]{2,1,0:T(8,128)(2,1)S(1)}, bf16[2,1024,128]{2,1,0:T(8,128)(2,1)}, u32[]{:S(2)}, u32[]{:S(2)}) %collective-permute-start.15) | collective-permute-done | bytes 524320 | tf_op jit(solution)/shard_map/ppermute | solution.py:416
  102.7 9.7 %window.3 = (f32[2,512,1024]{2,1,0:T(8,128)}, f32[2,512,1024]{2,1,0:T(8,128)}) custom-call(s32[2]{0:T(128)} %get-tuple-element.47.order, s32[8]{0:T(128)} %reshape.215.flags, bf16[512,4096]{1,0:T(8,128)(2,1)} %query_ref.7, bf16[2,512,128]{2,1,0:T(8,128)(2,1)} %get-tuple-element.30.rest_0_, bf16[2,512,128]{2,1,0:T(8,128)(2,1)} %get-tuple-element.31.rest_1_, ...), custom_call_target="tpu_custom_call" | custom-call | flops 1610612736 | bytes 8388608 | tf_op jit(solution)/shard_map/window/pallas_call | solution.py:269
  112.4 0.6 collective-permute-start.22
  113.0 9.8 %window.2 = (f32[2,512,1024]{2,1,0:T(8,128)}, f32[2,512,1024]{2,1,0:T(8,128)}) custom-call(s32[2]{0:T(128)} %get-tuple-element.48.order, s32[8]{0:T(128)} %reshape.215.flags, bf16[512,4096]{1,0:T(8,128)(2,1)} %query_ref.7, bf16[2,512,128]{2,1,0:T(8,128)(2,1)} %get-tuple-element.24.rest_0_, bf16[2,512,128]{2,1,0:T(8,128)(2,1)} %get-tuple-element.25.rest_1_, ...), custom_call_target="tpu_custom_call" | custom-call | flops 1610612736 | bytes 8388608 | tf_op jit(solution)/shard_map/window/pallas_call | solution.py:269
  122.9 0.7 copy-done.8
  123.6 13.9 %finish.2.rest_8_ = bf16[512,4096]{1,0:T(8,128)(2,1)} custom-call(s32[2]{0:T(128)} %get-tuple-element.47.order, s32[40]{0:T(128)} %reshape.214.table, bf16[512,4096]{1,0:T(8,128)(2,1)} %query_ref.7, f32[2,512,1024]{2,1,0:T(8,128)} %get-tuple-element.41.mixed_ref, f32[2,512,1024]{2,1,0:T(8,128)} %get-tuple-element.42.level_ref, ...), custom_call_target="tpu_custom_call" | custom-call | flops 2684354560 | bytes 8388608 | tf_op jit(solution)/shard_map/finish/pallas_call | solution.py:352
  137.6 0.6 copy-done.13
  138.2 0.2 copy-done.9
  138.4 13.9 %finish.3 = bf16[512,4096]{1,0:T(8,128)(2,1)} custom-call(s32[2]{0:T(128)} %get-tuple-element.48.order, s32[40]{0:T(128)} %reshape.212.table, bf16[512,4096]{1,0:T(8,128)(2,1)} %query_ref.7, f32[2,512,1024]{2,1,0:T(8,128)} %get-tuple-element.28.mixed_ref, f32[2,512,1024]{2,1,0:T(8,128)} %get-tuple-element.29.level_ref, ...), custom_call_target="tpu_custom_call", output_to_operand_aliasing={{}: (13, {})} | custom-call | flops 2684354560 | bytes 8388608 | tf_op jit(solution)/shard_map/finish/pallas_call | solution.py:352
  (85 shorter events, 1.5 us)
Async XLA Ops:
  0.5 91.6 %copy-start.6 = (s32[4]{0:T(128)S(1)}, s32[4]{0:T(128)}, u32[]{:S(2)}) copy-start(s32[4]{0:T(128)} %iota_xor_fusion.order) | copy-start | bytes 52
  4.1 8.4 %collective-permute-start.2 = (bf16[2,512,128]{2,1,0:T(8,128)(2,1)}, bf16[2,512,128]{2,1,0:T(8,128)(2,1)S(1)}, u32[]{:S(2)}, u32[]{:S(2)}) collective-permute-start(bf16[2,512,128]{2,1,0:T(8,128)(2,1)} %get-tuple-element.31.rest_1_), channel_id=1, source_target_pairs={{0,1},{1,0},{2,3},{3,2},{4,5},{5,4},{6,7},{7,6},{8,9},{9,8},{10,11... | collective-permute-start | bytes 786440 | tf_op jit(solution)/shard_map/ppermute | solution.py:416
  4.6 9.9 %collective-permute-start.3 = (bf16[2,512,128]{2,1,0:T(8,128)(2,1)}, bf16[2,512,128]{2,1,0:T(8,128)(2,1)S(1)}, u32[]{:S(2)}, u32[]{:S(2)}) collective-permute-start(bf16[2,512,128]{2,1,0:T(8,128)(2,1)} %get-tuple-element.24.rest_0_), channel_id=1, source_target_pairs={{0,2},{1,3},{2,0},{3,1},{4,6},{5,7},{6,4},{7,5},{8,10},{9,11},{10,... | collective-permute-start | bytes 786440 | tf_op jit(solution)/shard_map/ppermute | solution.py:416
  7.2 12.5 %collective-permute-start.4 = (bf16[2,512,128]{2,1,0:T(8,128)(2,1)}, bf16[2,512,128]{2,1,0:T(8,128)(2,1)S(1)}, u32[]{:S(2)}, u32[]{:S(2)}) collective-permute-start(bf16[2,512,128]{2,1,0:T(8,128)(2,1)} %get-tuple-element.25.rest_1_), channel_id=1, source_target_pairs={{0,3},{1,2},{2,1},{3,0},{4,7},{5,6},{6,5},{7,4},{8,11},{9,10},{10,... | collective-permute-start | bytes 786440 | tf_op jit(solution)/shard_map/ppermute | solution.py:416
  19.7 1.0 copy-start.3
  20.6 0.6 copy-start.5
  23.5 88.9 %copy-start.4 = (bf16[2,384,128]{2,1,0:T(8,128)(2,1)}, bf16[2,384,128]{2,1,0:T(8,128)(2,1)S(1)}, u32[]{:S(2)}) copy-start(bf16[2,384,128]{2,1,0:T(8,128)(2,1)S(1)} %get-tuple-element.32.rest_0_) | copy-start | bytes 589828
  23.5 9.5 %collective-permute-start.10 = (bf16[2,256,128]{2,1,0:T(8,128)(2,1)S(1)}, bf16[2,256,128]{2,1,0:T(8,128)(2,1)S(1)}, u32[]{:S(2)}, u32[]{:S(2)}) collective-permute-start(bf16[2,256,128]{2,1,0:T(8,128)(2,1)S(1)} %get-tuple-element.36), channel_id=1, source_target_pairs={{0,16},{4,20},{8,24},{12,28},{16,0},{20,4},{24,8},{28,12},{1,17},{... | collective-permute-start | bytes 393224 | tf_op jit(solution)/shard_map/ppermute | solution.py:416
  26.1 15.2 %collective-permute-start.6 = (bf16[2,384,128]{2,1,0:T(8,128)(2,1)S(1)}, bf16[2,384,128]{2,1,0:T(8,128)(2,1)S(1)}, u32[]{:S(2)}, u32[]{:S(2)}) collective-permute-start(bf16[2,384,128]{2,1,0:T(8,128)(2,1)S(1)} %get-tuple-element.33), channel_id=1, source_target_pairs={{0,4},{4,0},{8,12},{12,8},{16,20},{20,16},{24,28},{28,24},{1,5},{5... | collective-permute-start | bytes 589832 | tf_op jit(solution)/shard_map/ppermute | solution.py:416
  33.0 6.5 %collective-permute-start.11 = (bf16[2,256,128]{2,1,0:T(8,128)(2,1)S(1)}, bf16[2,256,128]{2,1,0:T(8,128)(2,1)S(1)}, u32[]{:S(2)}, u32[]{:S(2)}) collective-permute-start(bf16[2,256,128]{2,1,0:T(8,128)(2,1)S(1)} %add.109), channel_id=1, source_target_pairs={{0,8},{4,12},{8,0},{12,4},{16,24},{20,28},{24,16},{28,20},{1,9},{5... | collective-permute-start | bytes 393224 | tf_op jit(solution)/shard_map/ppermute | solution.py:416
  34.4 25.2 %collective-permute-start.16 = (bf16[2,384,128]{2,1,0:T(8,128)(2,1)S(1)}, bf16[2,384,128]{2,1,0:T(8,128)(2,1)S(1)}, u32[]{:S(2)}, u32[]{:S(2)}) collective-permute-start(bf16[2,384,128]{2,1,0:T(8,128)(2,1)S(1)} %get-tuple-element.39), channel_id=1, source_target_pairs={{0,24},{4,28},{8,16},{12,20},{16,8},{20,12},{24,0},{28,4},{1,25},{... | collective-permute-start | bytes 589832 | tf_op jit(solution)/shard_map/ppermute | solution.py:416
  37.3 27.7 %collective-permute-start.17 = (bf16[2,384,128]{2,1,0:T(8,128)(2,1)S(1)}, bf16[2,384,128]{2,1,0:T(8,128)(2,1)S(1)}, u32[]{:S(2)}, u32[]{:S(2)}) collective-permute-start(bf16[2,384,128]{2,1,0:T(8,128)(2,1)S(1)} %get-tuple-element.40), channel_id=1, source_target_pairs={{0,28},{4,24},{8,20},{12,16},{16,12},{20,8},{24,4},{28,0},{1,29},{... | collective-permute-start | bytes 589832 | tf_op jit(solution)/shard_map/ppermute | solution.py:416
  39.3 13.8 %collective-permute-start.7 = (bf16[2,384,128]{2,1,0:T(8,128)(2,1)S(1)}, bf16[2,384,128]{2,1,0:T(8,128)(2,1)S(1)}, u32[]{:S(2)}, u32[]{:S(2)}) collective-permute-start(bf16[2,384,128]{2,1,0:T(8,128)(2,1)S(1)} %get-tuple-element.34), channel_id=1, source_target_pairs={{0,8},{4,12},{8,0},{12,4},{16,24},{20,28},{24,16},{28,20},{1,9},{5... | collective-permute-start | bytes 589832 | tf_op jit(solution)/shard_map/ppermute | solution.py:416
  39.5 18.2 %collective-permute-start.8 = (bf16[2,384,128]{2,1,0:T(8,128)(2,1)S(1)}, bf16[2,384,128]{2,1,0:T(8,128)(2,1)S(1)}, u32[]{:S(2)}, u32[]{:S(2)}) collective-permute-start(bf16[2,384,128]{2,1,0:T(8,128)(2,1)S(1)} %get-tuple-element.35), channel_id=1, source_target_pairs={{0,12},{4,8},{8,4},{12,0},{16,28},{20,24},{24,20},{28,16},{1,13},{... | collective-permute-start | bytes 589832 | tf_op jit(solution)/shard_map/ppermute | solution.py:416
  41.3 24.6 %collective-permute-start.12 = (bf16[2,256,128]{2,1,0:T(8,128)(2,1)S(1)}, bf16[2,256,128]{2,1,0:T(8,128)(2,1)S(1)}, u32[]{:S(2)}, u32[]{:S(2)}) collective-permute-start(bf16[2,256,128]{2,1,0:T(8,128)(2,1)S(1)} %add.110), channel_id=1, source_target_pairs={{0,4},{4,0},{8,12},{12,8},{16,20},{20,16},{24,28},{28,24},{1,5},{5... | collective-permute-start | bytes 393224 | tf_op jit(solution)/shard_map/ppermute | solution.py:416
  53.1 31.6 %collective-permute-start = (bf16[2,128,512]{2,1,0:T(8,128)(2,1)}, bf16[2,128,512]{2,1,0:T(8,128)(2,1)S(1)}, u32[]{:S(2)}, u32[]{:S(2)}) collective-permute-start(bf16[2,128,512]{2,1,0:T(8,128)(2,1)} %get-tuple-element.26), channel_id=1, source_target_pairs={{0,1},{1,2},{2,3},{3,4},{4,5},{5,6},{6,7},{7,8},{8,9},{9,10},{10,1... | collective-permute-start | bytes 786440 | tf_op jit(solution)/shard_map/ppermute | solution.py:422
  57.7 27.1 %collective-permute-start.1 = (bf16[2,128,512]{2,1,0:T(8,128)(2,1)}, bf16[2,128,512]{2,1,0:T(8,128)(2,1)S(1)}, u32[]{:S(2)}, u32[]{:S(2)}) collective-permute-start(bf16[2,128,512]{2,1,0:T(8,128)(2,1)} %get-tuple-element.27), channel_id=1, source_target_pairs={{1,0},{2,1},{3,2},{4,3},{5,4},{6,5},{7,6},{8,7},{9,8},{10,9},{11,1... | collective-permute-start | bytes 786440 | tf_op jit(solution)/shard_map/ppermute | solution.py:423
  59.6 63.1 %copy-start = (bf16[2,1152,128]{2,1,0:T(8,128)(2,1)}, bf16[2,1152,128]{2,1,0:T(8,128)(2,1)S(1)}, u32[]{:S(2)}) copy-start(bf16[2,1152,128]{2,1,0:T(8,128)(2,1)S(1)} %join.3.rest_1_) | copy-start | bytes 1769476
  59.6 24.0 %collective-permute-start.13 = (bf16[2,384,128]{2,1,0:T(8,128)(2,1)S(1)}, bf16[2,384,128]{2,1,0:T(8,128)(2,1)S(1)}, u32[]{:S(2)}, u32[]{:S(2)}) collective-permute-start(bf16[2,384,128]{2,1,0:T(8,128)(2,1)S(1)} %get-tuple-element.37), channel_id=1, source_target_pairs={{0,16},{4,20},{8,24},{12,28},{16,0},{20,4},{24,8},{28,12},{1,17},{... | collective-permute-start | bytes 589832 | tf_op jit(solution)/shard_map/ppermute | solution.py:416
  65.0 18.6 %collective-permute-start.14 = (bf16[2,384,128]{2,1,0:T(8,128)(2,1)S(1)}, bf16[2,384,128]{2,1,0:T(8,128)(2,1)S(1)}, u32[]{:S(2)}, u32[]{:S(2)}) collective-permute-start(bf16[2,384,128]{2,1,0:T(8,128)(2,1)S(1)} %get-tuple-element.38), channel_id=1, source_target_pairs={{0,20},{4,16},{8,28},{12,24},{16,4},{20,0},{24,12},{28,8},{1,21},{... | collective-permute-start | bytes 589832 | tf_op jit(solution)/shard_map/ppermute | solution.py:416
  65.9 26.9 %collective-permute-start.9 = (bf16[2,1152,128]{2,1,0:T(8,128)(2,1)S(1)}, bf16[2,1152,128]{2,1,0:T(8,128)(2,1)S(1)}, u32[]{:S(2)}, u32[]{:S(2)}) collective-permute-start(bf16[2,1152,128]{2,1,0:T(8,128)(2,1)S(1)} %join.3.rest_1_), channel_id=1, source_target_pairs={{0,2},{1,3},{2,0},{3,1},{4,6},{5,7},{6,4},{7,5},{8,10},{9,11},{10,... | collective-permute-start | bytes 1769480 | tf_op jit(solution)/shard_map/ppermute | solution.py:416
  66.6 56.2 %copy-start.2 = (bf16[2,768,128]{2,1,0:T(8,128)(2,1)}, bf16[2,768,128]{2,1,0:T(8,128)(2,1)S(1)}, u32[]{:S(2)}) copy-start(bf16[2,768,128]{2,1,0:T(8,128)(2,1)S(1)} %join.5.rest_3_) | copy-start | bytes 1179652
  83.6 2.7 %collective-permute-start.23 = (bf16[2,384,128]{2,1,0:T(8,128)(2,1)S(1)}, bf16[2,384,128]{2,1,0:T(8,128)(2,1)S(1)}, u32[]{:S(2)}, u32[]{:S(2)}) collective-permute-start(bf16[2,384,128]{2,1,0:T(8,128)(2,1)S(1)} %get-tuple-element.32.rest_0_), channel_id=1, source_target_pairs={{0,1},{1,0},{2,3},{3,2},{4,5},{5,4},{6,7},{7,6},{8,9},{9,8},{10,11... | collective-permute-start | bytes 589832 | tf_op jit(solution)/shard_map/ppermute | solution.py:416
  83.6 7.8 %collective-permute-start.5 = (bf16[2,384,128]{2,1,0:T(8,128)(2,1)S(1)}, bf16[2,384,128]{2,1,0:T(8,128)(2,1)S(1)}, u32[]{:S(2)}, u32[]{:S(2)}) collective-permute-start(bf16[2,384,128]{2,1,0:T(8,128)(2,1)S(1)} %get-tuple-element.32.rest_0_), channel_id=1, source_target_pairs={{0,2},{1,3},{2,0},{3,1},{4,6},{5,7},{6,4},{7,5},{8,10},{9,11},{10,... | collective-permute-start | bytes 589832 | tf_op jit(solution)/shard_map/ppermute | solution.py:416
  84.7 38.0 %copy-start.1 = (bf16[2,1024,128]{2,1,0:T(8,128)(2,1)}, bf16[2,1024,128]{2,1,0:T(8,128)(2,1)S(1)}, u32[]{:S(2)}) copy-start(bf16[2,1024,128]{2,1,0:T(8,128)(2,1)S(1)} %join.4.rest_2_) | copy-start | bytes 1572868
  84.7 1.6 %copy-start.14 = (bf16[2,128,512]{2,1,0:T(8,128)(2,1)}, bf16[2,128,512]{2,1,0:T(8,128)(2,1)S(1)}, u32[]{:S(2)}) copy-start(bf16[2,128,512]{2,1,0:T(8,128)(2,1)S(1)} %collective-permute-done.rest_2_) | copy-start | bytes 786436
  84.7 8.0 %collective-permute-start.26 = (bf16[2,768,128]{2,1,0:T(8,128)(2,1)S(1)}, bf16[2,768,128]{2,1,0:T(8,128)(2,1)S(1)}, u32[]{:S(2)}, u32[]{:S(2)}) collective-permute-start(bf16[2,768,128]{2,1,0:T(8,128)(2,1)S(1)} %join.5.rest_3_), channel_id=1, source_target_pairs={{0,1},{1,0},{2,3},{3,2},{4,5},{5,4},{6,7},{7,6},{8,9},{9,8},{10,11... | collective-permute-start | bytes 1179656 | tf_op jit(solution)/shard_map/ppermute | solution.py:416
  84.8 1.5 %copy-start.15 = (bf16[2,128,512]{2,1,0:T(8,128)(2,1)}, bf16[2,128,512]{2,1,0:T(8,128)(2,1)S(1)}, u32[]{:S(2)}) copy-start(bf16[2,128,512]{2,1,0:T(8,128)(2,1)S(1)} %collective-permute-done.1.rest_3_) | copy-start | bytes 786436
  84.8 17.9 %collective-permute-start.15 = (bf16[2,1024,128]{2,1,0:T(8,128)(2,1)S(1)}, bf16[2,1024,128]{2,1,0:T(8,128)(2,1)}, u32[]{:S(2)}, u32[]{:S(2)}) collective-permute-start(bf16[2,1024,128]{2,1,0:T(8,128)(2,1)S(1)} %join.4.rest_2_), channel_id=1, source_target_pairs={{0,2},{1,3},{2,0},{3,1},{4,6},{5,7},{6,4},{7,5},{8,10},{9,11},{10,... | collective-permute-start | bytes 1572872 | tf_op jit(solution)/shard_map/ppermute | solution.py:416
  86.3 5.1 %copy-start.12 = (bf16[2,384,128]{2,1,0:T(8,128)(2,1)}, bf16[2,384,128]{2,1,0:T(8,128)(2,1)S(1)}, u32[]{:S(2)}) copy-start(bf16[2,384,128]{2,1,0:T(8,128)(2,1)S(1)} %collective-permute-done.23.rest_4_) | copy-start | bytes 589828
  86.3 36.4 %collective-permute-start.24 = (bf16[2,1152,128]{2,1,0:T(8,128)(2,1)S(1)}, bf16[2,1152,128]{2,1,0:T(8,128)(2,1)S(1)}, u32[]{:S(2)}, u32[]{:S(2)}) collective-permute-start(bf16[2,1152,128]{2,1,0:T(8,128)(2,1)S(1)} %join.3.rest_1_), channel_id=1, source_target_pairs={{0,1},{1,0},{2,3},{3,2},{4,5},{5,4},{6,7},{7,6},{8,9},{9,8},{10,11... | collective-permute-start | bytes 1769480 | tf_op jit(solution)/shard_map/ppermute | solution.py:416
  91.4 31.4 %copy-start.11 = (bf16[2,384,128]{2,1,0:T(8,128)(2,1)}, bf16[2,384,128]{2,1,0:T(8,128)(2,1)S(1)}, u32[]{:S(2)}) copy-start(bf16[2,384,128]{2,1,0:T(8,128)(2,1)S(1)} %collective-permute-done.5.rest_0_) | copy-start | bytes 589828
  91.4 21.0 %collective-permute-start.18 = (bf16[2,768,128]{2,1,0:T(8,128)(2,1)S(1)}, bf16[2,768,128]{2,1,0:T(8,128)(2,1)}, u32[]{:S(2)}, u32[]{:S(2)}) collective-permute-start(bf16[2,768,128]{2,1,0:T(8,128)(2,1)S(1)} %join.5.rest_3_), channel_id=1, source_target_pairs={{0,2},{1,3},{2,0},{3,1},{4,6},{5,7},{6,4},{7,5},{8,10},{9,11},{10,... | collective-permute-start | bytes 1179656 | tf_op jit(solution)/shard_map/ppermute | solution.py:416
  92.8 30.0 %copy-start.10 = (bf16[2,768,128]{2,1,0:T(8,128)(2,1)}, bf16[2,768,128]{2,1,0:T(8,128)(2,1)S(1)}, u32[]{:S(2)}) copy-start(bf16[2,768,128]{2,1,0:T(8,128)(2,1)S(1)} %collective-permute-done.26.rest_7_) | copy-start | bytes 1179652
  92.8 30.1 %collective-permute-start.25 = (bf16[2,1024,128]{2,1,0:T(8,128)(2,1)S(1)}, bf16[2,1024,128]{2,1,0:T(8,128)(2,1)}, u32[]{:S(2)}, u32[]{:S(2)}) collective-permute-start(bf16[2,1024,128]{2,1,0:T(8,128)(2,1)S(1)} %join.4.rest_2_), channel_id=1, source_target_pairs={{0,1},{1,0},{2,3},{3,2},{4,5},{5,4},{6,7},{7,6},{8,9},{9,8},{10,11... | collective-permute-start | bytes 1572872 | tf_op jit(solution)/shard_map/ppermute | solution.py:416
  92.8 30.0 %copy-start.7 = (bf16[2,1152,128]{2,1,0:T(8,128)(2,1)}, bf16[2,1152,128]{2,1,0:T(8,128)(2,1)S(1)}, u32[]{:S(2)}) copy-start(bf16[2,1152,128]{2,1,0:T(8,128)(2,1)S(1)} %collective-permute-done.9.rest_1_) | copy-start | bytes 1769476
  92.8 44.7 %collective-permute-start.20 = (bf16[2,1152,128]{2,1,0:T(8,128)(2,1)S(1)}, bf16[2,1152,128]{2,1,0:T(8,128)(2,1)}, u32[]{:S(2)}, u32[]{:S(2)}) collective-permute-start(bf16[2,1152,128]{2,1,0:T(8,128)(2,1)S(1)} %collective-permute-done.9.rest_1_), channel_id=1, source_target_pairs={{0,1},{1,0},{2,3},{3,2},{4,5},{5,4},{6,7},{7,6},{8,9},{9,8},{10,11... | collective-permute-start | bytes 1769480 | tf_op jit(solution)/shard_map/ppermute | solution.py:416
  102.7 34.8 %collective-permute-start.21 = (bf16[2,1024,128]{2,1,0:T(8,128)(2,1)}, bf16[2,1024,128]{2,1,0:T(8,128)(2,1)S(1)}, u32[]{:S(2)}, u32[]{:S(2)}) collective-permute-start(bf16[2,1024,128]{2,1,0:T(8,128)(2,1)} %collective-permute-done.15.rest_2_), channel_id=1, source_target_pairs={{0,1},{1,0},{2,3},{3,2},{4,5},{5,4},{6,7},{7,6},{8,9},{9,8},{10,11... | collective-permute-start | bytes 1572872 | tf_op jit(solution)/shard_map/ppermute | solution.py:416
  112.4 25.1 %collective-permute-start.22 = (bf16[2,768,128]{2,1,0:T(8,128)(2,1)}, bf16[2,768,128]{2,1,0:T(8,128)(2,1)}, u32[]{:S(2)}, u32[]{:S(2)}) collective-permute-start(bf16[2,768,128]{2,1,0:T(8,128)(2,1)} %collective-permute-done.18.rest_3_), channel_id=1, source_target_pairs={{0,1},{1,0},{2,3},{3,2},{4,5},{5,4},{6,7},{7,6},{8,9},{9,8},{10,11... | collective-permute-start | bytes 1179656 | tf_op jit(solution)/shard_map/ppermute | solution.py:416
  122.8 0.8 copy-start.8
  122.8 14.7 %collective-permute-start.19 = (bf16[2,384,128]{2,1,0:T(8,128)(2,1)S(1)}, bf16[2,384,128]{2,1,0:T(8,128)(2,1)S(1)}, u32[]{:S(2)}, u32[]{:S(2)}) collective-permute-start(bf16[2,384,128]{2,1,0:T(8,128)(2,1)S(1)} %collective-permute-done.5.rest_0_), channel_id=1, source_target_pairs={{0,1},{1,0},{2,3},{3,2},{4,5},{5,4},{6,7},{7,6},{8,9},{9,8},{10,11... | collective-permute-start | bytes 589832 | tf_op jit(solution)/shard_map/ppermute | solution.py:416
  137.5 0.7 copy-start.13
  137.6 0.8 copy-start.9
where the time goes:
time: 153 us; the launch traced here: 152 us
  waiting for transfers between devices  54.8 us (36%)
  Pallas kernels  54.1 us (35%)
  starting transfers between devices  30.7 us (20%)
  local copies, waits for them, and re-layouts  8.56 us (6%)
  other arithmetic  3.71 us (2%)
    ppermute x25, waiting for transfers between devices, across(): return lax.ppermute(array, axis, [(i, i ^ bit) for i in range(count)])  54.8 us
    pallas_call x2, Pallas kernels, finish(): pl.pallas_call(functools.partial(finish_kernel, [len(part) for part in pa...  27.8 us
    ppermute x25, starting transfers between devices, across(): return lax.ppermute(array, axis, [(i, i ^ bit) for i in range(count)])  27.4 us
    pallas_call x2, Pallas kernels, window_share(): pl.pallas_call(functools.partial(window_kernel, parts), grid_spec=pltpu.P...  19.4 us
    pallas_call x1, Pallas kernels, pack(): pl.pallas_call(functools.partial(pack_kernel, heads), in_specs=[SMEM, ANY...  3.56 us
    unnamed x33, local copies, waits for them, and re-layouts  3.22 us
  transfers between devices with their start and end apart: 27, of which 8 were waited for; matrix products, arithmetic and copies ran while one was open for 6% of the time, Pallas kernels for 23%

commit v1 on v0

--- a/solution.py
+++ b/solution.py
@@ -16,7 +16,7 @@
 WINDOW = 3
 MIB = 2**20
 SOME_VMEM = 20 * MIB
-MOST_VMEM = 60 * MIB
+MOST_VMEM = 50 * MIB
 
 
 ANY = pl.BlockSpec(memory_space=pl.ANY)
@@ -81,7 +81,7 @@
             pltpu.SemaphoreType.DMA((2, 2)),
             pltpu.SemaphoreType.DMA((2,)),
         ],
-        compiler_params=pltpu.CompilerParams(vmem_limit_bytes=MOST_VMEM),
+        compiler_params=pltpu.CompilerParams(vmem_limit_bytes=SOME_VMEM),
         name="pack",
     )(order, key_rows, value_rows)
 
@@ -257,7 +257,7 @@
     return pl.BlockSpec(array.shape, lambda *_: (0,) * array.ndim)
 
 
-def window_share(order, flags, queries, locals_, edges):
+def window_share(order, flags, queries, locals_, edges, begin):
     rows, columns = queries.shape
     heads = edges[0].shape[2] // HEAD_DIM
     width = columns // heads
@@ -265,13 +265,13 @@
     parts = len(locals_)
     pairs = parts * blocks * (width // HEAD_DIM) * BLOCK * WINDOW * BLOCK
     some = TOGETHER * BLOCK
-    edge = pl.BlockSpec((2, BLOCK, HEAD_DIM), lambda r, i, order, flags: (0, 0, order[r]))
+    edge = pl.BlockSpec((2, BLOCK, HEAD_DIM), lambda r, i, order, flags: (0, 0, order[begin + r]))
     return pl.pallas_call(
         functools.partial(window_kernel, parts),
         grid_spec=pltpu.PrefetchScalarGridSpec(
             num_scalar_prefetch=2,
             grid=(parts, blocks // TOGETHER),
-            in_specs=[pl.BlockSpec((some, width), lambda r, i, order, flags: (i, order[r]))]
+            in_specs=[pl.BlockSpec((some, width), lambda r, i, order, flags: (i, order[begin + r]))]
             + [whole_block(array) for array in locals_]
             + [edge, edge],
             out_specs=[pl.BlockSpec((1, some, width), lambda r, i, order, flags: (r, i, 0))] * 2,
@@ -289,7 +289,7 @@
 LISTED = GLOBALS + RANDOM
 
 
-def finish_kernel(counts, aliased, order, table, query_ref, mixed_ref, level_ref, *rest):
+def finish_kernel(begin, counts, aliased, order, table, query_ref, mixed_ref, level_ref, *rest):
     sources, (out_ref, held) = rest[: sum(counts)], rest[sum(counts) + aliased :]
     part, step = pl.program_id(0), pl.program_id(1)
     grouping = query_ref.shape[1] // HEAD_DIM
@@ -304,7 +304,7 @@
                 start += source.shape[1]
 
         number += count
-    base = (part * pl.num_programs(1) + step) * TOGETHER * LISTED
+    base = ((begin + part) * pl.num_programs(1) + step) * TOGETHER * LISTED
 
     def listed(which, unit):
         return jnp.concatenate(
@@ -339,18 +339,18 @@
     pipelined(tasks, scores_of, rest_of)
 
 
-def finish(order, table, queries, share, parts, output):
+def finish(order, table, queries, share, parts, begin, output):
     rows, columns = queries.shape
     width = share[0].shape[2]
     blocks = rows // BLOCK
     arrays = [array for part in parts for array in part]
     pairs = len(parts) * blocks * (width // HEAD_DIM) * BLOCK * LISTED * BLOCK
     some = TOGETHER * BLOCK
-    spec = pl.BlockSpec((some, width), lambda r, i, order, table: (i, order[r]))
+    spec = pl.BlockSpec((some, width), lambda r, i, order, table: (i, order[begin + r]))
     aliased = [] if output is None else [output]
     operands = (order, table, queries, *share, *arrays, *aliased)
     return pl.pallas_call(
-        functools.partial(finish_kernel, [len(part) for part in parts], len(aliased)),
+        functools.partial(finish_kernel, begin, [len(part) for part in parts], len(aliased)),
         grid_spec=pltpu.PrefetchScalarGridSpec(
             num_scalar_prefetch=2,
             grid=(len(parts), blocks // TOGETHER),
@@ -457,7 +457,7 @@
     place = jnp.take(place, order, axis=0).reshape(heads, my_blocks, RANDOM)
     commons = half * slots + jnp.arange(GLOBALS, dtype=jnp.int32)
     commons = jnp.broadcast_to(commons, (heads, my_blocks, GLOBALS))
-    table = jnp.concatenate([commons, place], axis=2).reshape(heads, -1)
+    table = jnp.concatenate([commons, place], axis=2).reshape(-1)
     number = (seq_index * heads + head_index) * my_blocks + local
     flags = (
         jnp.stack([number > 0, number < seq_count * run_blocks - 1], axis=1)
@@ -468,22 +468,17 @@
     shares = []
     for some in (slice(0, half_heads), slice(half_heads, heads)):
         shares.append(
-            window_share(
-                order[some],
-                flags,
-                query_rows,
-                parts[some],
-                (previous, upcoming),
-            )
+            window_share(order, flags, query_rows, parts[some], (previous, upcoming), some.start)
         )
     output = None
     for n, (begin, end) in enumerate(((0, half_heads), (half_heads, heads))):
         output = finish(
-            order[begin:end],
-            table[begin:end].reshape(-1),
+            order,
+            table,
             query_rows,
             shares[n],
             [groups[r] for r in range(begin, end)],
+            begin,
             output,
         )
     return output

time: 153 us -> 150 us (0.980)
  waiting for transfers between devices: 54.8 us -> 50.5 us
  Pallas kernels: 54.1 us -> 50.3 us
  local copies, waits for them, and re-layouts: 8.56 us -> 12 us
    unnamed x33 -> x37, local copies, waits for them, and re-layouts: 3.22 us -> 8.32 us
    ppermute x25, waiting for transfers between devices: 54.8 us -> 50.5 us  [across(): return lax.ppermute(array, axis, [(i, i ^ bit) for i in range(count)])]
    pallas_call x2, Pallas kernels: 27.8 us -> 25.9 us  [finish(): pl.pallas_call(functools.partial(finish_kernel, begin, [len(part) for par...]
  transfers between devices with their start and end apart: 27 -> 27, of which waited for: 8 -> 9; matrix products, arithmetic and copies ran while one was open for 6% -> 6% of each run, Pallas kernels for 23% -> 23%
where the time goes in v1:
time: 150 us
  waiting for transfers between devices  50.5 us (34%)
  Pallas kernels  50.3 us (34%)
  starting transfers between devices  32 us (21%)
  local copies, waits for them, and re-layouts  12 us (8%)
  other arithmetic  4.68 us (3%)
    ppermute x25, waiting for transfers between devices, across(): return lax.ppermute(array, axis, [(i, i ^ bit) for i in range(count)])  50.5 us
    ppermute x25, starting transfers between devices, across(): return lax.ppermute(array, axis, [(i, i ^ bit) for i in range(count)])  28.6 us
    pallas_call x2, Pallas kernels, finish(): pl.pallas_call(functools.partial(finish_kernel, begin, [len(part) for par...  25.9 us
    pallas_call x2, Pallas kernels, window_share(): pl.pallas_call(functools.partial(window_kernel, parts), grid_spec=pltpu.P...  18.7 us
    unnamed x37, local copies, waits for them, and re-layouts  8.32 us
  transfers between devices with their start and end apart: 27, of which 9 were waited for; matrix products, arithmetic and copies ran while one was open for 6% of the time, Pallas kernels for 23%

profile of v1, /device:TPU:0, one launch (start us, length us, event | category | flops | bytes accessed | tf_op | source)
XLA Modules:
  0.0 149.9 jit_solution(6239157927252067124)
XLA Ops:
  0.0 1.0 copy-done
  1.0 1.0 copy-done.1
  2.1 2.4 %pack.1 = (bf16[2,512,128]{2,1,0:T(8,128)(2,1)S(1)}, bf16[2,512,128]{2,1,0:T(8,128)(2,1)S(1)}, bf16[2,512,128]{2,1,0:T(8,128)(2,1)S(1)}, bf16[2,512,128]{2,1,0:T...) custom-call(s32[4]{0:T(128)S(1)} %iota_xor_fusion.order, bf16[512,512]{1,0:T(8,128)(2,1)S(1)} %copy-done, ...), custom_call_target="tpu_custom_call" | custom-call | tf_op jit(solution)/shard_map/pack/pallas_call | solution.py:71
  4.5 0.6 collective-permute-start.2
  5.0 0.7 copy-done.14
  5.8 2.5 %collective-permute-start.3 = (bf16[2,512,128]{2,1,0:T(8,128)(2,1)S(1)}, bf16[2,512,128]{2,1,0:T(8,128)(2,1)S(1)}, u32[]{:S(2)}, u32[]{:S(2)}) collective-permute-start(bf16[2,512,128]{2,1,0:T(8,128)(2,1)S(1)} %get-tuple-element.24.rest_0_), channel_id=1, source_target_pairs={{0,2},{1,3},{2,0},{3,1},{4,6},{5,7},{6,4},{7,5},{8,10},{9,11},{10,... | collective-permute-start | bytes 786440 | tf_op jit(solution)/shard_map/ppermute | solution.py:416
  8.2 0.1 collective-permute-start.4
  8.3 0.7 copy-done.12
  9.0 2.0 %collective-permute-start = (bf16[2,128,512]{2,1,0:T(8,128)(2,1)S(1)}, bf16[2,128,512]{2,1,0:T(8,128)(2,1)S(1)}, u32[]{:S(2)}, u32[]{:S(2)}) collective-permute-start(bf16[2,128,512]{2,1,0:T(8,128)(2,1)S(1)} %get-tuple-element.26), channel_id=1, source_target_pairs={{0,1},{1,2},{2,3},{3,4},{4,5},{5,6},{6,7},{7,8},{8,9},{9,10},{10,1... | collective-permute-start | bytes 786440 | tf_op jit(solution)/shard_map/ppermute | solution.py:422
  11.1 0.7 fusion.10
  11.8 0.7 fusion.9
  12.5 0.8 reshape.202
  13.4 0.2 fusion
  13.6 0.2 convert_reduce_fusion
  13.9 0.1 select_reduce_fusion
  14.1 0.6 gather_fusion.1
  15.0 0.1 copy.13
  15.3 0.1 collective-permute-done.3.rest_2_
  15.4 5.2 %collective-permute-done.4.rest_3_ = bf16[2,512,128]{2,1,0:T(8,128)(2,1)S(1)} collective-permute-done((bf16[2,512,128]{2,1,0:T(8,128)(2,1)S(1)}, bf16[2,512,128]{2,1,0:T(8,128)(2,1)S(1)}, u32[]{:S(2)}, u32[]{:S(2)}) %collective-permute-start.4) | collective-permute-done | bytes 262176 | tf_op jit(solution)/shard_map/ppermute | solution.py:416
  20.6 2.3 %pick.1 = (bf16[2,384,128]{2,1,0:T(8,128)(2,1)S(1)}, bf16[2,384,128]{2,1,0:T(8,128)(2,1)S(1)}, bf16[2,384,128]{2,1,0:T(8,128)(2,1)S(1)}, bf16[2,384,128]{2,1,0:T...) custom-call(s32[4]{0:T(128)S(1)} %iota_xor_fusion.order, ...), custom_call_target="tpu_custom_call" | custom-call | tf_op jit(solution)/shard_map/pick/pallas_call | solution.py:124
  22.9 2.6 %collective-permute-start.10 = (bf16[2,256,128]{2,1,0:T(8,128)(2,1)S(1)}, bf16[2,256,128]{2,1,0:T(8,128)(2,1)S(1)}, u32[]{:S(2)}, u32[]{:S(2)}) collective-permute-start(bf16[2,256,128]{2,1,0:T(8,128)(2,1)S(1)} %get-tuple-element.36), channel_id=1, source_target_pairs={{0,16},{4,20},{8,24},{12,28},{16,0},{20,4},{24,8},{28,12},{1,17},{... | collective-permute-start | bytes 393224 | tf_op jit(solution)/shard_map/ppermute | solution.py:416
  25.6 0.2 and_reduce_fusion
  25.8 1.4 collective-permute-start.16
  27.2 10.1 %collective-permute-done.10 = bf16[2,256,128]{2,1,0:T(8,128)(2,1)S(1)} collective-permute-done((bf16[2,256,128]{2,1,0:T(8,128)(2,1)S(1)}, bf16[2,256,128]{2,1,0:T(8,128)(2,1)S(1)}, u32[]{:S(2)}, u32[]{:S(2)}) %collective-permute-start.10) | collective-permute-done | bytes 131104 | tf_op jit(solution)/shard_map/ppermute | solution.py:416
  37.3 0.5 collective-permute-start.11
  38.2 0.3 convert_reduce_fusion.1
  38.6 6.4 %collective-permute-start.17 = (bf16[2,384,128]{2,1,0:T(8,128)(2,1)S(1)}, bf16[2,384,128]{2,1,0:T(8,128)(2,1)S(1)}, u32[]{:S(2)}, u32[]{:S(2)}) collective-permute-start(bf16[2,384,128]{2,1,0:T(8,128)(2,1)S(1)} %get-tuple-element.40), channel_id=1, source_target_pairs={{0,28},{4,24},{8,20},{12,16},{16,12},{20,8},{24,4},{28,0},{1,29},{... | collective-permute-start | bytes 589832 | tf_op jit(solution)/shard_map/ppermute | solution.py:416
  45.0 1.1 collective-permute-start.7
  46.1 2.4 %collective-permute-start.8 = (bf16[2,384,128]{2,1,0:T(8,128)(2,1)S(1)}, bf16[2,384,128]{2,1,0:T(8,128)(2,1)S(1)}, u32[]{:S(2)}, u32[]{:S(2)}) collective-permute-start(bf16[2,384,128]{2,1,0:T(8,128)(2,1)S(1)} %get-tuple-element.35), channel_id=1, source_target_pairs={{0,12},{4,8},{8,4},{12,0},{16,28},{20,24},{24,20},{28,16},{1,13},{... | collective-permute-start | bytes 589832 | tf_op jit(solution)/shard_map/ppermute | solution.py:416
  48.5 0.1 fusion.4
  48.7 4.2 %collective-permute-done.17.refs_1_ = bf16[2,384,128]{2,1,0:T(8,128)(2,1)S(1)} collective-permute-done((bf16[2,384,128]{2,1,0:T(8,128)(2,1)S(1)}, bf16[2,384,128]{2,1,0:T(8,128)(2,1)S(1)}, u32[]{:S(2)}, u32[]{:S(2)}) %collective-permute-start.17) | collective-permute-done | bytes 196640 | tf_op jit(solution)/shard_map/ppermute | solution.py:416
  52.9 3.0 %collective-permute-start.13 = (bf16[2,384,128]{2,1,0:T(8,128)(2,1)}, bf16[2,384,128]{2,1,0:T(8,128)(2,1)S(1)}, u32[]{:S(2)}, u32[]{:S(2)}) collective-permute-start(bf16[2,384,128]{2,1,0:T(8,128)(2,1)} %get-tuple-element.37), channel_id=1, source_target_pairs={{0,16},{4,20},{8,24},{12,28},{16,0},{20,4},{24,8},{28,12},{1,17},{... | collective-permute-start | bytes 589832 | tf_op jit(solution)/shard_map/ppermute | solution.py:416
  55.8 2.9 %collective-permute-start.14 = (bf16[2,384,128]{2,1,0:T(8,128)(2,1)}, bf16[2,384,128]{2,1,0:T(8,128)(2,1)S(1)}, u32[]{:S(2)}, u32[]{:S(2)}) collective-permute-start(bf16[2,384,128]{2,1,0:T(8,128)(2,1)} %get-tuple-element.38), channel_id=1, source_target_pairs={{0,20},{4,16},{8,28},{12,24},{16,4},{20,0},{24,12},{28,8},{1,21},{... | collective-permute-start | bytes 589832 | tf_op jit(solution)/shard_map/ppermute | solution.py:416
  58.8 0.6 collective-permute-start.12
  59.4 3.7 %collective-permute-done.8.refs_2_ = bf16[2,384,128]{2,1,0:T(8,128)(2,1)S(1)} collective-permute-done((bf16[2,384,128]{2,1,0:T(8,128)(2,1)S(1)}, bf16[2,384,128]{2,1,0:T(8,128)(2,1)S(1)}, u32[]{:S(2)}, u32[]{:S(2)}) %collective-permute-start.8) | collective-permute-done | bytes 196640 | tf_op jit(solution)/shard_map/ppermute | solution.py:416
  63.1 1.5 collective-permute-start.1
  64.6 0.6 gather_fusion
  65.2 0.3 join.5.rest_3_
  65.5 0.4 join.3.rest_1_
  65.9 0.7 copy-done.16
  66.7 1.1 collective-permute-start.23
  67.8 2.6 %collective-permute-done.13.refs_1_ = bf16[2,384,128]{2,1,0:T(8,128)(2,1)S(1)} collective-permute-done((bf16[2,384,128]{2,1,0:T(8,128)(2,1)}, bf16[2,384,128]{2,1,0:T(8,128)(2,1)S(1)}, u32[]{:S(2)}, u32[]{:S(2)}) %collective-permute-start.13) | collective-permute-done | bytes 196640 | tf_op jit(solution)/shard_map/ppermute | solution.py:416
  70.4 4.7 %collective-permute-done.14.refs_2_ = bf16[2,384,128]{2,1,0:T(8,128)(2,1)S(1)} collective-permute-done((bf16[2,384,128]{2,1,0:T(8,128)(2,1)}, bf16[2,384,128]{2,1,0:T(8,128)(2,1)S(1)}, u32[]{:S(2)}, u32[]{:S(2)}) %collective-permute-start.14) | collective-permute-done | bytes 196640 | tf_op jit(solution)/shard_map/ppermute | solution.py:416
  75.1 0.2 collective-permute-start.9
  75.3 0.9 add.111.refs_0_
  76.3 0.4 join.4.rest_2_
  76.7 1.9 %collective-permute-start.15 = (bf16[2,1024,128]{2,1,0:T(8,128)(2,1)S(1)}, bf16[2,1024,128]{2,1,0:T(8,128)(2,1)}, u32[]{:S(2)}, u32[]{:S(2)}) collective-permute-start(bf16[2,1024,128]{2,1,0:T(8,128)(2,1)S(1)} %join.4.rest_2_), channel_id=1, source_target_pairs={{0,2},{1,3},{2,0},{3,1},{4,6},{5,7},{6,4},{7,5},{8,10},{9,11},{10,... | collective-permute-start | bytes 1572872 | tf_op jit(solution)/shard_map/ppermute | solution.py:416
  78.6 0.7 copy-done.8
  79.3 0.7 copy-done.6
  79.9 0.3 collective-permute-start.18
  80.3 0.7 copy-done.2
  81.0 0.3 collective-permute-start.25
  81.3 10.0 %collective-permute-done.9.rest_1_ = bf16[2,1152,128]{2,1,0:T(8,128)(2,1)S(1)} collective-permute-done((bf16[2,1152,128]{2,1,0:T(8,128)(2,1)S(1)}, bf16[2,1152,128]{2,1,0:T(8,128)(2,1)S(1)}, u32[]{:S(2)}, u32[]{:S(2)}) %collective-permute-start.9) | collective-permute-done | bytes 589856 | tf_op jit(solution)/shard_map/ppermute | solution.py:416
  91.3 0.6 add_convert_fusion
  92.0 0.7 reshape.206.flags
  92.7 9.9 %collective-permute-done.15.rest_2_ = bf16[2,1024,128]{2,1,0:T(8,128)(2,1)} collective-permute-done((bf16[2,1024,128]{2,1,0:T(8,128)(2,1)S(1)}, bf16[2,1024,128]{2,1,0:T(8,128)(2,1)}, u32[]{:S(2)}, u32[]{:S(2)}) %collective-permute-start.15) | collective-permute-done | bytes 524320 | tf_op jit(solution)/shard_map/ppermute | solution.py:416
  102.6 0.9 copy-done.15
  103.6 0.9 copy-done.17
  104.5 9.3 %window.3 = (f32[2,512,1024]{2,1,0:T(8,128)}, f32[2,512,1024]{2,1,0:T(8,128)}) custom-call(s32[4]{0:T(128)S(1)} %iota_xor_fusion.order, s32[8]{0:T(128)S(1)} %reshape.206.flags, bf16[512,4096]{1,0:T(8,128)(2,1)} %query_ref.7, bf16[2,512,128]{2,1,0:T(8,128)(2,1)S(1)} %get-tuple-element.30.rest_0_, bf16[2,512,128]{2,1,0:T(8,128)(2,1)S(1)} %copy-done.15, ...), custom_call_target="tpu_custom_call" | custom-call | flops 1610612736 | bytes 8388608 | tf_op jit(solution)/shard_map/window/pallas_call | solution.py:269
  113.9 0.6 collective-permute-start.22
  114.4 9.4 %window.2 = (f32[2,512,1024]{2,1,0:T(8,128)}, f32[2,512,1024]{2,1,0:T(8,128)}) custom-call(s32[4]{0:T(128)S(1)} %iota_xor_fusion.order, s32[8]{0:T(128)S(1)} %reshape.206.flags, bf16[512,4096]{1,0:T(8,128)(2,1)} %query_ref.7, bf16[2,512,128]{2,1,0:T(8,128)(2,1)S(1)} %copy-done.11, bf16[2,512,128]{2,1,0:T(8,128)(2,1)S(1)} %copy-done.13, ...), custom_call_target="tpu_custom_call" | custom-call | flops 1610612736 | bytes 8388608 | tf_op jit(solution)/shard_map/window/pallas_call | solution.py:269
  123.8 0.1 collective-permute-start.19
  124.0 12.9 %finish.2.rest_8_ = bf16[512,4096]{1,0:T(8,128)(2,1)} custom-call(s32[4]{0:T(128)S(1)} %iota_xor_fusion.order, s32[80]{0:T(128)S(1)} %reshape.204.table, bf16[512,4096]{1,0:T(8,128)(2,1)} %query_ref.7, f32[2,512,1024]{2,1,0:T(8,128)} %get-tuple-element.41.mixed_ref, f32[2,512,1024]{2,1,0:T(8,128)} %get-tuple-element.42.level_ref, ...), custom_call_target="tpu_custom_call" | custom-call | flops 2684354560 | bytes 8388608 | tf_op jit(solution)/shard_map/finish/pallas_call | solution.py:352
  136.9 13.0 %finish.3 = bf16[512,4096]{1,0:T(8,128)(2,1)} custom-call(s32[4]{0:T(128)S(1)} %iota_xor_fusion.order, s32[80]{0:T(128)S(1)} %reshape.204.table, bf16[512,4096]{1,0:T(8,128)(2,1)} %query_ref.7, f32[2,512,1024]{2,1,0:T(8,128)} %get-tuple-element.28.mixed_ref, f32[2,512,1024]{2,1,0:T(8,128)} %get-tuple-element.29.level_ref, ...), custom_call_target="tpu_custom_call", output_to_operand_aliasing={{}: (13, {})} | custom-call | flops 2684354560 | bytes 8388608 | tf_op jit(solution)/shard_map/finish/pallas_call | solution.py:352
  (86 shorter events, 1.7 us)
Async XLA Ops:
  0.0 1.0 copy-start
  1.0 1.0 copy-start.1
  4.5 16.2 %copy-start.10 = (bf16[2,512,128]{2,1,0:T(8,128)(2,1)}, bf16[2,512,128]{2,1,0:T(8,128)(2,1)S(1)}, u32[]{:S(2)}) copy-start(bf16[2,512,128]{2,1,0:T(8,128)(2,1)S(1)} %get-tuple-element.24.rest_0_) | copy-start | bytes 786436
  4.5 10.8 %collective-permute-start.2 = (bf16[2,512,128]{2,1,0:T(8,128)(2,1)S(1)}, bf16[2,512,128]{2,1,0:T(8,128)(2,1)S(1)}, u32[]{:S(2)}, u32[]{:S(2)}) collective-permute-start(bf16[2,512,128]{2,1,0:T(8,128)(2,1)S(1)} %get-tuple-element.31.rest_1_), channel_id=1, source_target_pairs={{0,1},{1,0},{2,3},{3,2},{4,5},{5,4},{6,7},{7,6},{8,9},{9,8},{10,11... | collective-permute-start | bytes 786440 | tf_op jit(solution)/shard_map/ppermute | solution.py:416
  5.0 0.7 copy-start.14
  5.8 9.6 %collective-permute-start.3 = (bf16[2,512,128]{2,1,0:T(8,128)(2,1)S(1)}, bf16[2,512,128]{2,1,0:T(8,128)(2,1)S(1)}, u32[]{:S(2)}, u32[]{:S(2)}) collective-permute-start(bf16[2,512,128]{2,1,0:T(8,128)(2,1)S(1)} %get-tuple-element.24.rest_0_), channel_id=1, source_target_pairs={{0,2},{1,3},{2,0},{3,1},{4,6},{5,7},{6,4},{7,5},{8,10},{9,11},{10,... | collective-permute-start | bytes 786440 | tf_op jit(solution)/shard_map/ppermute | solution.py:416
  8.2 12.4 %collective-permute-start.4 = (bf16[2,512,128]{2,1,0:T(8,128)(2,1)S(1)}, bf16[2,512,128]{2,1,0:T(8,128)(2,1)S(1)}, u32[]{:S(2)}, u32[]{:S(2)}) collective-permute-start(bf16[2,512,128]{2,1,0:T(8,128)(2,1)S(1)} %get-tuple-element.25.rest_1_), channel_id=1, source_target_pairs={{0,3},{1,2},{2,1},{3,0},{4,7},{5,6},{6,5},{7,4},{8,11},{9,10},{10,... | collective-permute-start | bytes 786440 | tf_op jit(solution)/shard_map/ppermute | solution.py:416
  8.3 0.7 copy-start.12
  9.0 56.9 %collective-permute-start = (bf16[2,128,512]{2,1,0:T(8,128)(2,1)S(1)}, bf16[2,128,512]{2,1,0:T(8,128)(2,1)S(1)}, u32[]{:S(2)}, u32[]{:S(2)}) collective-permute-start(bf16[2,128,512]{2,1,0:T(8,128)(2,1)S(1)} %get-tuple-element.26), channel_id=1, source_target_pairs={{0,1},{1,2},{2,3},{3,4},{4,5},{5,6},{6,7},{7,8},{8,9},{9,10},{10,1... | collective-permute-start | bytes 786440 | tf_op jit(solution)/shard_map/ppermute | solution.py:422
  22.9 58.3 %copy-start.4 = (bf16[2,384,128]{2,1,0:T(8,128)(2,1)}, bf16[2,384,128]{2,1,0:T(8,128)(2,1)S(1)}, u32[]{:S(2)}) copy-start(bf16[2,384,128]{2,1,0:T(8,128)(2,1)S(1)} %get-tuple-element.32.rest_0_) | copy-start | bytes 589828
  22.9 14.4 %collective-permute-start.10 = (bf16[2,256,128]{2,1,0:T(8,128)(2,1)S(1)}, bf16[2,256,128]{2,1,0:T(8,128)(2,1)S(1)}, u32[]{:S(2)}, u32[]{:S(2)}) collective-permute-start(bf16[2,256,128]{2,1,0:T(8,128)(2,1)S(1)} %get-tuple-element.36), channel_id=1, source_target_pairs={{0,16},{4,20},{8,24},{12,28},{16,0},{20,4},{24,8},{28,12},{1,17},{... | collective-permute-start | bytes 393224 | tf_op jit(solution)/shard_map/ppermute | solution.py:416
  25.8 19.2 %collective-permute-start.16 = (bf16[2,384,128]{2,1,0:T(8,128)(2,1)S(1)}, bf16[2,384,128]{2,1,0:T(8,128)(2,1)S(1)}, u32[]{:S(2)}, u32[]{:S(2)}) collective-permute-start(bf16[2,384,128]{2,1,0:T(8,128)(2,1)S(1)} %get-tuple-element.39), channel_id=1, source_target_pairs={{0,24},{4,28},{8,16},{12,20},{16,8},{20,12},{24,0},{28,4},{1,25},{... | collective-permute-start | bytes 589832 | tf_op jit(solution)/shard_map/ppermute | solution.py:416
  37.3 8.8 %collective-permute-start.11 = (bf16[2,256,128]{2,1,0:T(8,128)(2,1)S(1)}, bf16[2,256,128]{2,1,0:T(8,128)(2,1)S(1)}, u32[]{:S(2)}, u32[]{:S(2)}) collective-permute-start(bf16[2,256,128]{2,1,0:T(8,128)(2,1)S(1)} %add.109), channel_id=1, source_target_pairs={{0,8},{4,12},{8,0},{12,4},{16,24},{20,28},{24,16},{28,20},{1,9},{5... | collective-permute-start | bytes 393224 | tf_op jit(solution)/shard_map/ppermute | solution.py:416
  38.6 14.3 %collective-permute-start.17 = (bf16[2,384,128]{2,1,0:T(8,128)(2,1)S(1)}, bf16[2,384,128]{2,1,0:T(8,128)(2,1)S(1)}, u32[]{:S(2)}, u32[]{:S(2)}) collective-permute-start(bf16[2,384,128]{2,1,0:T(8,128)(2,1)S(1)} %get-tuple-element.40), channel_id=1, source_target_pairs={{0,28},{4,24},{8,20},{12,16},{16,12},{20,8},{24,4},{28,0},{1,29},{... | collective-permute-start | bytes 589832 | tf_op jit(solution)/shard_map/ppermute | solution.py:416
  45.0 10.9 %collective-permute-start.6 = (bf16[2,384,128]{2,1,0:T(8,128)(2,1)S(1)}, bf16[2,384,128]{2,1,0:T(8,128)(2,1)S(1)}, u32[]{:S(2)}, u32[]{:S(2)}) collective-permute-start(bf16[2,384,128]{2,1,0:T(8,128)(2,1)S(1)} %get-tuple-element.33), channel_id=1, source_target_pairs={{0,4},{4,0},{8,12},{12,8},{16,20},{20,16},{24,28},{28,24},{1,5},{5... | collective-permute-start | bytes 589832 | tf_op jit(solution)/shard_map/ppermute | solution.py:416
  45.0 13.8 %collective-permute-start.7 = (bf16[2,384,128]{2,1,0:T(8,128)(2,1)S(1)}, bf16[2,384,128]{2,1,0:T(8,128)(2,1)S(1)}, u32[]{:S(2)}, u32[]{:S(2)}) collective-permute-start(bf16[2,384,128]{2,1,0:T(8,128)(2,1)S(1)} %get-tuple-element.34), channel_id=1, source_target_pairs={{0,8},{4,12},{8,0},{12,4},{16,24},{20,28},{24,16},{28,20},{1,9},{5... | collective-permute-start | bytes 589832 | tf_op jit(solution)/shard_map/ppermute | solution.py:416
  46.1 17.0 %collective-permute-start.8 = (bf16[2,384,128]{2,1,0:T(8,128)(2,1)S(1)}, bf16[2,384,128]{2,1,0:T(8,128)(2,1)S(1)}, u32[]{:S(2)}, u32[]{:S(2)}) collective-permute-start(bf16[2,384,128]{2,1,0:T(8,128)(2,1)S(1)} %get-tuple-element.35), channel_id=1, source_target_pairs={{0,12},{4,8},{8,4},{12,0},{16,28},{20,24},{24,20},{28,16},{1,13},{... | collective-permute-start | bytes 589832 | tf_op jit(solution)/shard_map/ppermute | solution.py:416
  52.9 17.5 %collective-permute-start.13 = (bf16[2,384,128]{2,1,0:T(8,128)(2,1)}, bf16[2,384,128]{2,1,0:T(8,128)(2,1)S(1)}, u32[]{:S(2)}, u32[]{:S(2)}) collective-permute-start(bf16[2,384,128]{2,1,0:T(8,128)(2,1)} %get-tuple-element.37), channel_id=1, source_target_pairs={{0,16},{4,20},{8,24},{12,28},{16,0},{20,4},{24,8},{28,12},{1,17},{... | collective-permute-start | bytes 589832 | tf_op jit(solution)/shard_map/ppermute | solution.py:416
  55.8 19.2 %collective-permute-start.14 = (bf16[2,384,128]{2,1,0:T(8,128)(2,1)}, bf16[2,384,128]{2,1,0:T(8,128)(2,1)S(1)}, u32[]{:S(2)}, u32[]{:S(2)}) collective-permute-start(bf16[2,384,128]{2,1,0:T(8,128)(2,1)} %get-tuple-element.38), channel_id=1, source_target_pairs={{0,20},{4,16},{8,28},{12,24},{16,4},{20,0},{24,12},{28,8},{1,21},{... | collective-permute-start | bytes 589832 | tf_op jit(solution)/shard_map/ppermute | solution.py:416
  58.8 16.3 %collective-permute-start.12 = (bf16[2,256,128]{2,1,0:T(8,128)(2,1)S(1)}, bf16[2,256,128]{2,1,0:T(8,128)(2,1)}, u32[]{:S(2)}, u32[]{:S(2)}) collective-permute-start(bf16[2,256,128]{2,1,0:T(8,128)(2,1)S(1)} %add.110), channel_id=1, source_target_pairs={{0,4},{4,0},{8,12},{12,8},{16,20},{20,16},{24,28},{28,24},{1,5},{5... | collective-permute-start | bytes 393224 | tf_op jit(solution)/shard_map/ppermute | solution.py:416
  63.1 13.6 %collective-permute-start.1 = (bf16[2,128,512]{2,1,0:T(8,128)(2,1)}, bf16[2,128,512]{2,1,0:T(8,128)(2,1)}, u32[]{:S(2)}, u32[]{:S(2)}) collective-permute-start(bf16[2,128,512]{2,1,0:T(8,128)(2,1)} %get-tuple-element.27), channel_id=1, source_target_pairs={{1,0},{2,1},{3,2},{4,3},{5,4},{6,5},{7,6},{8,7},{9,8},{10,9},{11,1... | collective-permute-start | bytes 786440 | tf_op jit(solution)/shard_map/ppermute | solution.py:423
  65.9 0.7 copy-start.16
  66.7 11.9 %collective-permute-start.23 = (bf16[2,384,128]{2,1,0:T(8,128)(2,1)S(1)}, bf16[2,384,128]{2,1,0:T(8,128)(2,1)S(1)}, u32[]{:S(2)}, u32[]{:S(2)}) collective-permute-start(bf16[2,384,128]{2,1,0:T(8,128)(2,1)S(1)} %get-tuple-element.32.rest_0_), channel_id=1, source_target_pairs={{0,1},{1,0},{2,3},{3,2},{4,5},{5,4},{6,7},{7,6},{8,9},{9,8},{10,11... | collective-permute-start | bytes 589832 | tf_op jit(solution)/shard_map/ppermute | solution.py:416
  70.4 8.9 %collective-permute-start.5 = (bf16[2,384,128]{2,1,0:T(8,128)(2,1)S(1)}, bf16[2,384,128]{2,1,0:T(8,128)(2,1)S(1)}, u32[]{:S(2)}, u32[]{:S(2)}) collective-permute-start(bf16[2,384,128]{2,1,0:T(8,128)(2,1)S(1)} %get-tuple-element.32.rest_0_), channel_id=1, source_target_pairs={{0,2},{1,3},{2,0},{3,1},{4,6},{5,7},{6,4},{7,5},{8,10},{9,11},{10,... | collective-permute-start | bytes 589832 | tf_op jit(solution)/shard_map/ppermute | solution.py:416
  75.0 5.2 %collective-permute-start.26 = (bf16[2,768,128]{2,1,0:T(8,128)(2,1)S(1)}, bf16[2,768,128]{2,1,0:T(8,128)(2,1)S(1)}, u32[]{:S(2)}, u32[]{:S(2)}) collective-permute-start(bf16[2,768,128]{2,1,0:T(8,128)(2,1)S(1)} %join.5.rest_3_), channel_id=1, source_target_pairs={{0,1},{1,0},{2,3},{3,2},{4,5},{5,4},{6,7},{7,6},{8,9},{9,8},{10,11... | collective-permute-start | bytes 1179656 | tf_op jit(solution)/shard_map/ppermute | solution.py:416
  75.1 16.2 %collective-permute-start.9 = (bf16[2,1152,128]{2,1,0:T(8,128)(2,1)S(1)}, bf16[2,1152,128]{2,1,0:T(8,128)(2,1)S(1)}, u32[]{:S(2)}, u32[]{:S(2)}) collective-permute-start(bf16[2,1152,128]{2,1,0:T(8,128)(2,1)S(1)} %join.3.rest_1_), channel_id=1, source_target_pairs={{0,2},{1,3},{2,0},{3,1},{4,6},{5,7},{6,4},{7,5},{8,10},{9,11},{10,... | collective-permute-start | bytes 1769480 | tf_op jit(solution)/shard_map/ppermute | solution.py:416
  76.7 25.9 %collective-permute-start.15 = (bf16[2,1024,128]{2,1,0:T(8,128)(2,1)S(1)}, bf16[2,1024,128]{2,1,0:T(8,128)(2,1)}, u32[]{:S(2)}, u32[]{:S(2)}) collective-permute-start(bf16[2,1024,128]{2,1,0:T(8,128)(2,1)S(1)} %join.4.rest_2_), channel_id=1, source_target_pairs={{0,2},{1,3},{2,0},{3,1},{4,6},{5,7},{6,4},{7,5},{8,10},{9,11},{10,... | collective-permute-start | bytes 1572872 | tf_op jit(solution)/shard_map/ppermute | solution.py:416
  78.6 0.7 copy-start.8
  79.2 44.6 %collective-permute-start.24 = (bf16[2,1152,128]{2,1,0:T(8,128)(2,1)S(1)}, bf16[2,1152,128]{2,1,0:T(8,128)(2,1)S(1)}, u32[]{:S(2)}, u32[]{:S(2)}) collective-permute-start(bf16[2,1152,128]{2,1,0:T(8,128)(2,1)S(1)} %join.3.rest_1_), channel_id=1, source_target_pairs={{0,1},{1,0},{2,3},{3,2},{4,5},{5,4},{6,7},{7,6},{8,9},{9,8},{10,11... | collective-permute-start | bytes 1769480 | tf_op jit(solution)/shard_map/ppermute | solution.py:416
  79.3 0.7 copy-start.6
  79.9 33.9 %collective-permute-start.18 = (bf16[2,768,128]{2,1,0:T(8,128)(2,1)S(1)}, bf16[2,768,128]{2,1,0:T(8,128)(2,1)}, u32[]{:S(2)}, u32[]{:S(2)}) collective-permute-start(bf16[2,768,128]{2,1,0:T(8,128)(2,1)S(1)} %join.5.rest_3_), channel_id=1, source_target_pairs={{0,2},{1,3},{2,0},{3,1},{4,6},{5,7},{6,4},{7,5},{8,10},{9,11},{10,... | collective-permute-start | bytes 1179656 | tf_op jit(solution)/shard_map/ppermute | solution.py:416
  80.3 0.7 copy-start.2
  81.0 42.9 %collective-permute-start.25 = (bf16[2,1024,128]{2,1,0:T(8,128)(2,1)S(1)}, bf16[2,1024,128]{2,1,0:T(8,128)(2,1)}, u32[]{:S(2)}, u32[]{:S(2)}) collective-permute-start(bf16[2,1024,128]{2,1,0:T(8,128)(2,1)S(1)} %join.4.rest_2_), channel_id=1, source_target_pairs={{0,1},{1,0},{2,3},{3,2},{4,5},{5,4},{6,7},{7,6},{8,9},{9,8},{10,11... | collective-permute-start | bytes 1572872 | tf_op jit(solution)/shard_map/ppermute | solution.py:416
  91.3 45.6 %collective-permute-start.20 = (bf16[2,1152,128]{2,1,0:T(8,128)(2,1)S(1)}, bf16[2,1152,128]{2,1,0:T(8,128)(2,1)S(1)}, u32[]{:S(2)}, u32[]{:S(2)}) collective-permute-start(bf16[2,1152,128]{2,1,0:T(8,128)(2,1)S(1)} %collective-permute-done.9.rest_1_), channel_id=1, source_target_pairs={{0,1},{1,0},{2,3},{3,2},{4,5},{5,4},{6,7},{7,6},{8,9},{9,8},{10,11... | collective-permute-start | bytes 1769480 | tf_op jit(solution)/shard_map/ppermute | solution.py:416
  92.7 21.7 %copy-start.11 = (bf16[2,512,128]{2,1,0:T(8,128)(2,1)S(1)}, bf16[2,512,128]{2,1,0:T(8,128)(2,1)}, u32[]{:S(2)}) copy-start(bf16[2,512,128]{2,1,0:T(8,128)(2,1)} %copy-done.10) | copy-start | bytes 786436
  92.7 21.7 %copy-start.13 = (bf16[2,512,128]{2,1,0:T(8,128)(2,1)S(1)}, bf16[2,512,128]{2,1,0:T(8,128)(2,1)}, u32[]{:S(2)}) copy-start(bf16[2,512,128]{2,1,0:T(8,128)(2,1)} %copy-done.12) | copy-start | bytes 786436
  102.6 34.3 %collective-permute-start.21 = (bf16[2,1024,128]{2,1,0:T(8,128)(2,1)}, bf16[2,1024,128]{2,1,0:T(8,128)(2,1)S(1)}, u32[]{:S(2)}, u32[]{:S(2)}) collective-permute-start(bf16[2,1024,128]{2,1,0:T(8,128)(2,1)} %collective-permute-done.15.rest_2_), channel_id=1, source_target_pairs={{0,1},{1,0},{2,3},{3,2},{4,5},{5,4},{6,7},{7,6},{8,9},{9,8},{10,11... | collective-permute-start | bytes 1572872 | tf_op jit(solution)/shard_map/ppermute | solution.py:416
  102.6 1.0 copy-start.15
  103.5 0.9 copy-start.17
  113.8 10.0 %copy-start.7 = (bf16[2,384,128]{2,1,0:T(8,128)(2,1)S(1)}, bf16[2,384,128]{2,1,0:T(8,128)(2,1)}, u32[]{:S(2)}) copy-start(bf16[2,384,128]{2,1,0:T(8,128)(2,1)} %copy-done.6) | copy-start | bytes 589828
  113.8 10.1 %copy-start.3 = (bf16[2,768,128]{2,1,0:T(8,128)(2,1)S(1)}, bf16[2,768,128]{2,1,0:T(8,128)(2,1)}, u32[]{:S(2)}) copy-start(bf16[2,768,128]{2,1,0:T(8,128)(2,1)} %copy-done.2) | copy-start | bytes 1179652
  113.8 10.1 %copy-start.5 = (bf16[2,384,128]{2,1,0:T(8,128)(2,1)S(1)}, bf16[2,384,128]{2,1,0:T(8,128)(2,1)}, u32[]{:S(2)}) copy-start(bf16[2,384,128]{2,1,0:T(8,128)(2,1)} %copy-done.4) | copy-start | bytes 589828
  113.8 10.1 %copy-start.9 = (bf16[2,384,128]{2,1,0:T(8,128)(2,1)S(1)}, bf16[2,384,128]{2,1,0:T(8,128)(2,1)}, u32[]{:S(2)}) copy-start(bf16[2,384,128]{2,1,0:T(8,128)(2,1)} %copy-done.8) | copy-start | bytes 589828
  113.9 23.0 %collective-permute-start.22 = (bf16[2,768,128]{2,1,0:T(8,128)(2,1)}, bf16[2,768,128]{2,1,0:T(8,128)(2,1)S(1)}, u32[]{:S(2)}, u32[]{:S(2)}) collective-permute-start(bf16[2,768,128]{2,1,0:T(8,128)(2,1)} %collective-permute-done.18.rest_3_), channel_id=1, source_target_pairs={{0,1},{1,0},{2,3},{3,2},{4,5},{5,4},{6,7},{7,6},{8,9},{9,8},{10,11... | collective-permute-start | bytes 1179656 | tf_op jit(solution)/shard_map/ppermute | solution.py:416
  123.8 13.0 %collective-permute-start.19 = (bf16[2,384,128]{2,1,0:T(8,128)(2,1)S(1)}, bf16[2,384,128]{2,1,0:T(8,128)(2,1)S(1)}, u32[]{:S(2)}, u32[]{:S(2)}) collective-permute-start(bf16[2,384,128]{2,1,0:T(8,128)(2,1)S(1)} %copy-done.7), channel_id=1, source_target_pairs={{0,1},{1,0},{2,3},{3,2},{4,5},{5,4},{6,7},{7,6},{8,9},{9,8},{10,11... | collective-permute-start | bytes 589832 | tf_op jit(solution)/shard_map/ppermute | solution.py:416

commit v2 on v1

--- a/solution.py
+++ b/solution.py
@@ -16,7 +16,8 @@
 WINDOW = 3
 MIB = 2**20
 SOME_VMEM = 20 * MIB
-MOST_VMEM = 50 * MIB
+MOST_VMEM = 60 * MIB
+LESS_VMEM = 50 * MIB
 
 
 ANY = pl.BlockSpec(memory_space=pl.ANY)
@@ -278,7 +279,7 @@
             scratch_shapes=[pltpu.VMEM((2, rows + 2 * BLOCK, HEAD_DIM), queries.dtype)],
         ),
         out_shape=[jax.ShapeDtypeStruct((parts, rows, width), jnp.float32)] * 2,
-        compiler_params=pltpu.CompilerParams(vmem_limit_bytes=MOST_VMEM),
+        compiler_params=pltpu.CompilerParams(vmem_limit_bytes=LESS_VMEM if begin == 0 else MOST_VMEM),
         cost_estimate=pl.CostEstimate(
             flops=4 * pairs * HEAD_DIM, bytes_accessed=8 * MIB, transcendentals=pairs
         ),
@@ -369,7 +370,7 @@
         ),
         out_shape=jax.ShapeDtypeStruct((rows, columns), queries.dtype),
         input_output_aliases={len(operands) - 1: 0} if aliased else {},
-        compiler_params=pltpu.CompilerParams(vmem_limit_bytes=MOST_VMEM),
+        compiler_params=pltpu.CompilerParams(vmem_limit_bytes=LESS_VMEM),
         cost_estimate=pl.CostEstimate(
             flops=4 * pairs * HEAD_DIM, bytes_accessed=8 * MIB, transcendentals=pairs
         ),
@@ -438,12 +439,7 @@
         common = common + across(common, "seq", bit)
         bit //= 2
     half, last_part = seq_count // 2, (seq_count + seq_count // 2) // 2
-    own = [
-        chunks[0],
-        join(chunks[1:half]),
-        join([common] + chunks[half:last_part]),
-        join(chunks[last_part:]),
-    ]
+    own = [join(chunks[:half]), join(chunks[half:last_part]), join(chunks[last_part:] + [common])]
     groups = {0: own}
     bit = heads // 2
     while bit:
@@ -453,9 +449,9 @@
 
     local = jnp.arange(my_blocks, dtype=jnp.int32)
     chunk = owner ^ seq_index
-    place = chunk * slots + slot + jnp.where(chunk >= half, GLOBALS, 0)
+    place = chunk * slots + slot
     place = jnp.take(place, order, axis=0).reshape(heads, my_blocks, RANDOM)
-    commons = half * slots + jnp.arange(GLOBALS, dtype=jnp.int32)
+    commons = seq_count * slots + jnp.arange(GLOBALS, dtype=jnp.int32)
     commons = jnp.broadcast_to(commons, (heads, my_blocks, GLOBALS))
     table = jnp.concatenate([commons, place], axis=2).reshape(-1)
     number = (seq_index * heads + head_index) * my_blocks + local

time: 150 us -> 140 us (0.933)
  starting transfers between devices: 32 us -> 27.6 us
  local copies, waits for them, and re-layouts: 12 us -> 8.8 us
  waiting for transfers between devices: 50.5 us -> 48.9 us
    ppermute x25 -> x22, starting transfers between devices: 28.6 us -> 24.2 us  [across(): return lax.ppermute(array, axis, [(i, i ^ bit) for i in range(count)])]
    unnamed x37, local copies, waits for them, and re-layouts: 8.32 us -> 5.73 us
    ppermute x25 -> x22, waiting for transfers between devices: 50.5 us -> 48.9 us  [across(): return lax.ppermute(array, axis, [(i, i ^ bit) for i in range(count)])]
  transfers between devices with their start and end apart: 27 -> 24, of which waited for: 9 -> 8; matrix products, arithmetic and copies ran while one was open for 6% -> 5% of each run, Pallas kernels for 23% -> 24%
where the time goes in v2:
time: 140 us; the launch traced here: 139 us
  Pallas kernels  50.6 us (36%)
  waiting for transfers between devices  48.9 us (35%)
  starting transfers between devices  27.6 us (20%)
  local copies, waits for them, and re-layouts  8.8 us (6%)
  other arithmetic  3.21 us (2%)
    ppermute x22, waiting for transfers between devices, across(): return lax.ppermute(array, axis, [(i, i ^ bit) for i in range(count)])  48.9 us
    pallas_call x2, Pallas kernels, finish(): pl.pallas_call(functools.partial(finish_kernel, begin, [len(part) for par...  26.4 us
    ppermute x22, starting transfers between devices, across(): return lax.ppermute(array, axis, [(i, i ^ bit) for i in range(count)])  24.2 us
    pallas_call x2, Pallas kernels, window_share(): pl.pallas_call(functools.partial(window_kernel, parts), grid_spec=pltpu.P...  19.1 us
    unnamed x37, local copies, waits for them, and re-layouts  5.73 us
  transfers between devices with their start and end apart: 24, of which 8 were waited for; matrix products, arithmetic and copies ran while one was open for 5% of the time, Pallas kernels for 24%

profile of v2, /device:TPU:0, one launch (start us, length us, event | category | flops | bytes accessed | tf_op | source)
XLA Modules:
  0.0 139.5 jit_solution(2709621585149331470)
XLA Ops:
  0.0 1.0 copy-done
  1.0 1.0 copy-done.1
  2.1 1.7 %pack.1 = (bf16[2,512,128]{2,1,0:T(8,128)(2,1)S(1)}, bf16[2,512,128]{2,1,0:T(8,128)(2,1)S(1)}, bf16[2,512,128]{2,1,0:T(8,128)(2,1)S(1)}, bf16[2,512,128]{2,1,0:T...) custom-call(s32[4]{0:T(128)S(1)} %iota_xor_fusion.order, ...), custom_call_target="tpu_custom_call" | custom-call | tf_op jit(solution)/shard_map/pack/pallas_call | solution.py:72
  3.9 0.6 collective-permute-start.2
  4.4 2.6 %collective-permute-start.3 = (bf16[2,512,128]{2,1,0:T(8,128)(2,1)S(1)}, bf16[2,512,128]{2,1,0:T(8,128)(2,1)S(1)}, u32[]{:S(2)}, u32[]{:S(2)}) collective-permute-start(bf16[2,512,128]{2,1,0:T(8,128)(2,1)S(1)} %get-tuple-element.24.rest_0_), channel_id=1, source_target_pairs={{0,2},{1,3},{2,0},{3,1},{4,6},{5,7},{6,4},{7,5},{8,10},{9,11},{10,... | collective-permute-start | bytes 786440 | tf_op jit(solution)/shard_map/ppermute | solution.py:417
  7.0 0.7 fusion.10
  7.7 0.7 fusion.9
  8.4 0.8 reshape.202
  9.4 0.2 fusion
  9.6 0.2 convert_reduce_fusion
  9.8 0.1 select_reduce_fusion
  10.0 0.1 copy.19
  10.1 0.1 copy.13
  10.2 0.1 reshape.203
  10.3 0.6 gather_fusion.1
  10.9 0.2 and_reduce_fusion
  11.2 0.1 copy.20
  11.3 0.1 reshape.205.shared
  11.4 2.7 %collective-permute-done.3.rest_2_ = bf16[2,512,128]{2,1,0:T(8,128)(2,1)S(1)} collective-permute-done((bf16[2,512,128]{2,1,0:T(8,128)(2,1)S(1)}, bf16[2,512,128]{2,1,0:T(8,128)(2,1)S(1)}, u32[]{:S(2)}, u32[]{:S(2)}) %collective-permute-start.3) | collective-permute-done | bytes 262176 | tf_op jit(solution)/shard_map/ppermute | solution.py:417
  14.1 5.1 %collective-permute-done.4.rest_3_ = bf16[2,512,128]{2,1,0:T(8,128)(2,1)S(1)} collective-permute-done((bf16[2,512,128]{2,1,0:T(8,128)(2,1)S(1)}, bf16[2,512,128]{2,1,0:T(8,128)(2,1)S(1)}, u32[]{:S(2)}, u32[]{:S(2)}) %collective-permute-start.4) | collective-permute-done | bytes 262176 | tf_op jit(solution)/shard_map/ppermute | solution.py:417
  19.2 2.3 %pick.1 = (bf16[2,384,128]{2,1,0:T(8,128)(2,1)S(1)}, bf16[2,384,128]{2,1,0:T(8,128)(2,1)}, bf16[2,384,128]{2,1,0:T(8,128)(2,1)S(1)}, bf16[2,384,128]{2,1,0:T(8,1...) custom-call(s32[4]{0:T(128)S(1)} %iota_xor_fusion.order, ...), custom_call_target="tpu_custom_call" | custom-call | tf_op jit(solution)/shard_map/pick/pallas_call | solution.py:125
  21.5 2.6 %collective-permute-start.14 = (bf16[2,256,128]{2,1,0:T(8,128)(2,1)S(1)}, bf16[2,256,128]{2,1,0:T(8,128)(2,1)S(1)}, u32[]{:S(2)}, u32[]{:S(2)}) collective-permute-start(bf16[2,256,128]{2,1,0:T(8,128)(2,1)S(1)} %get-tuple-element.40), channel_id=1, source_target_pairs={{0,16},{4,20},{8,24},{12,28},{16,0},{20,4},{24,8},{28,12},{1,17},{... | collective-permute-start | bytes 393224 | tf_op jit(solution)/shard_map/ppermute | solution.py:417
  24.2 1.5 %collective-permute-start.5 = (bf16[2,384,128]{2,1,0:T(8,128)(2,1)}, bf16[2,384,128]{2,1,0:T(8,128)(2,1)S(1)}, u32[]{:S(2)}, u32[]{:S(2)}) collective-permute-start(bf16[2,384,128]{2,1,0:T(8,128)(2,1)} %get-tuple-element.33), channel_id=1, source_target_pairs={{0,4},{4,0},{8,12},{12,8},{16,20},{20,16},{24,28},{28,24},{1,5},{5... | collective-permute-start | bytes 589832 | tf_op jit(solution)/shard_map/ppermute | solution.py:417
  25.7 1.6 %collective-permute-start.6 = (bf16[2,384,128]{2,1,0:T(8,128)(2,1)S(1)}, bf16[2,384,128]{2,1,0:T(8,128)(2,1)S(1)}, u32[]{:S(2)}, u32[]{:S(2)}) collective-permute-start(bf16[2,384,128]{2,1,0:T(8,128)(2,1)S(1)} %get-tuple-element.34), channel_id=1, source_target_pairs={{0,8},{4,12},{8,0},{12,4},{16,24},{20,28},{24,16},{28,20},{1,9},{5... | collective-permute-start | bytes 589832 | tf_op jit(solution)/shard_map/ppermute | solution.py:417
  27.3 0.4 collective-permute-start.7
  27.7 0.1 copy.14
  27.8 0.1 copy.15
  27.9 0.3 convert_reduce_fusion.1
  28.3 0.1 copy.16
  28.4 1.3 collective-permute-start.10
  29.7 1.4 %collective-permute-done.14 = bf16[2,256,128]{2,1,0:T(8,128)(2,1)S(1)} collective-permute-done((bf16[2,256,128]{2,1,0:T(8,128)(2,1)S(1)}, bf16[2,256,128]{2,1,0:T(8,128)(2,1)S(1)}, u32[]{:S(2)}, u32[]{:S(2)}) %collective-permute-start.14) | collective-permute-done | bytes 131104 | tf_op jit(solution)/shard_map/ppermute | solution.py:417
  31.1 0.8 collective-permute-start.15
  31.9 7.2 %collective-permute-done.6.refs_2_ = bf16[2,384,128]{2,1,0:T(8,128)(2,1)S(1)} collective-permute-done((bf16[2,384,128]{2,1,0:T(8,128)(2,1)S(1)}, bf16[2,384,128]{2,1,0:T(8,128)(2,1)S(1)}, u32[]{:S(2)}, u32[]{:S(2)}) %collective-permute-start.6) | collective-permute-done | bytes 196640 | tf_op jit(solution)/shard_map/ppermute | solution.py:417
  39.1 4.4 %collective-permute-done.7.refs_3_ = bf16[2,384,128]{2,1,0:T(8,128)(2,1)S(1)} collective-permute-done((bf16[2,384,128]{2,1,0:T(8,128)(2,1)S(1)}, bf16[2,384,128]{2,1,0:T(8,128)(2,1)S(1)}, u32[]{:S(2)}, u32[]{:S(2)}) %collective-permute-start.7) | collective-permute-done | bytes 196640 | tf_op jit(solution)/shard_map/ppermute | solution.py:417
  43.5 0.5 join.3.rest_0_
  44.1 1.6 %collective-permute-start.8 = (bf16[2,1536,128]{2,1,0:T(8,128)(2,1)S(1)}, bf16[2,1536,128]{2,1,0:T(8,128)(2,1)S(1)}, u32[]{:S(2)}, u32[]{:S(2)}) collective-permute-start(bf16[2,1536,128]{2,1,0:T(8,128)(2,1)S(1)} %join.3.rest_0_), channel_id=1, source_target_pairs={{0,2},{1,3},{2,0},{3,1},{4,6},{5,7},{6,4},{7,5},{8,10},{9,11},{10,... | collective-permute-start | bytes 2359304 | tf_op jit(solution)/shard_map/ppermute | solution.py:417
  45.6 0.1 fusion.4
  45.7 2.5 %collective-permute-start.12 = (bf16[2,384,128]{2,1,0:T(8,128)(2,1)}, bf16[2,384,128]{2,1,0:T(8,128)(2,1)S(1)}, u32[]{:S(2)}, u32[]{:S(2)}) collective-permute-start(bf16[2,384,128]{2,1,0:T(8,128)(2,1)} %copy-done.16), channel_id=1, source_target_pairs={{0,24},{4,28},{8,16},{12,20},{16,8},{20,12},{24,0},{28,4},{1,25},{... | collective-permute-start | bytes 589832 | tf_op jit(solution)/shard_map/ppermute | solution.py:417
  48.3 1.5 %collective-permute-start.16 = (bf16[2,256,128]{2,1,0:T(8,128)(2,1)S(1)}, bf16[2,256,128]{2,1,0:T(8,128)(2,1)S(1)}, u32[]{:S(2)}, u32[]{:S(2)}) collective-permute-start(bf16[2,256,128]{2,1,0:T(8,128)(2,1)S(1)} %add.106), channel_id=1, source_target_pairs={{0,4},{4,0},{8,12},{12,8},{16,20},{20,16},{24,28},{28,24},{1,5},{5... | collective-permute-start | bytes 393224 | tf_op jit(solution)/shard_map/ppermute | solution.py:417
  49.8 2.0 %collective-permute-start = (bf16[2,128,512]{2,1,0:T(8,128)(2,1)}, bf16[2,128,512]{2,1,0:T(8,128)(2,1)}, u32[]{:S(2)}, u32[]{:S(2)}) collective-permute-start(bf16[2,128,512]{2,1,0:T(8,128)(2,1)} %copy-done.12), channel_id=1, source_target_pairs={{0,1},{1,2},{2,3},{3,4},{4,5},{5,6},{6,7},{7,8},{8,9},{9,10},{10,1... | collective-permute-start | bytes 786440 | tf_op jit(solution)/shard_map/ppermute | solution.py:423
  51.8 0.6 gather_fusion
  52.4 0.1 gather.11
  52.5 10.2 %collective-permute-done.9.refs_0_ = bf16[2,384,128]{2,1,0:T(8,128)(2,1)S(1)} collective-permute-done((bf16[2,384,128]{2,1,0:T(8,128)(2,1)}, bf16[2,384,128]{2,1,0:T(8,128)(2,1)S(1)}, u32[]{:S(2)}, u32[]{:S(2)}) %collective-permute-start.9) | collective-permute-done | bytes 196640 | tf_op jit(solution)/shard_map/ppermute | solution.py:417
  62.7 1.5 %collective-permute-start.1 = (bf16[2,128,512]{2,1,0:T(8,128)(2,1)}, bf16[2,128,512]{2,1,0:T(8,128)(2,1)S(1)}, u32[]{:S(2)}, u32[]{:S(2)}) collective-permute-start(bf16[2,128,512]{2,1,0:T(8,128)(2,1)} %copy-done.11), channel_id=1, source_target_pairs={{1,0},{2,1},{3,2},{4,3},{5,4},{6,5},{7,6},{8,7},{9,8},{10,9},{11,1... | collective-permute-start | bytes 786440 | tf_op jit(solution)/shard_map/ppermute | solution.py:424
  64.1 0.3 join.4.rest_1_
  64.4 3.8 %collective-permute-start.13 = (bf16[2,384,128]{2,1,0:T(8,128)(2,1)}, bf16[2,384,128]{2,1,0:T(8,128)(2,1)S(1)}, u32[]{:S(2)}, u32[]{:S(2)}) collective-permute-start(bf16[2,384,128]{2,1,0:T(8,128)(2,1)} %copy-done.15), channel_id=1, source_target_pairs={{0,28},{4,24},{8,20},{12,16},{16,12},{20,8},{24,4},{28,0},{1,29},{... | collective-permute-start | bytes 589832 | tf_op jit(solution)/shard_map/ppermute | solution.py:417
  68.2 0.2 collective-permute-start.22
  68.5 6.6 %collective-permute-done.13.refs_1_ = bf16[2,384,128]{2,1,0:T(8,128)(2,1)S(1)} collective-permute-done((bf16[2,384,128]{2,1,0:T(8,128)(2,1)}, bf16[2,384,128]{2,1,0:T(8,128)(2,1)S(1)}, u32[]{:S(2)}, u32[]{:S(2)}) %collective-permute-start.13) | collective-permute-done | bytes 196640 | tf_op jit(solution)/shard_map/ppermute | solution.py:417
  75.2 0.9 copy-done.3
  76.1 0.3 join.5.rest_2_
  76.5 1.1 collective-permute-start.17
  77.6 0.7 copy-done.13
  78.2 1.0 collective-permute-start.11
  79.4 0.1 reshape.204.table
  79.5 0.6 collective-permute-start.23
  80.1 0.1 reshape.206.flags
  80.2 11.2 %collective-permute-done.17.rest_2_ = bf16[2,1024,128]{2,1,0:T(8,128)(2,1)} collective-permute-done((bf16[2,1024,128]{2,1,0:T(8,128)(2,1)S(1)}, bf16[2,1024,128]{2,1,0:T(8,128)(2,1)}, u32[]{:S(2)}, u32[]{:S(2)}) %collective-permute-start.17) | collective-permute-done | bytes 524320 | tf_op jit(solution)/shard_map/ppermute | solution.py:417
  91.5 0.9 copy-done.10
  92.4 0.9 copy-done.14
  93.4 9.3 %window.3 = (f32[2,512,1024]{2,1,0:T(8,128)}, f32[2,512,1024]{2,1,0:T(8,128)}) custom-call(s32[4]{0:T(128)S(1)} %iota_xor_fusion.order, s32[8]{0:T(128)S(1)} %reshape.206.flags, bf16[512,4096]{1,0:T(8,128)(2,1)} %query_ref.7, bf16[2,512,128]{2,1,0:T(8,128)(2,1)S(1)} %get-tuple-element.30.rest_0_, bf16[2,512,128]{2,1,0:T(8,128)(2,1)S(1)} %copy-done.10, ...), custom_call_target="tpu_custom_call" | custom-call | flops 1610612736 | bytes 8388608 | tf_op jit(solution)/shard_map/window/pallas_call | solution.py:270
  102.7 0.6 collective-permute-start.19
  103.3 9.7 %window.2 = (f32[2,512,1024]{2,1,0:T(8,128)}, f32[2,512,1024]{2,1,0:T(8,128)}) custom-call(s32[4]{0:T(128)} %copy-done.4, s32[8]{0:T(128)} %copy-done.6, bf16[512,4096]{1,0:T(8,128)(2,1)} %query_ref.7, bf16[2,512,128]{2,1,0:T(8,128)(2,1)} %copy-done.7, bf16[2,512,128]{2,1,0:T(8,128)(2,1)} %copy-done.8, bf16[2,128,512]{2,1,0:T(8,128)(2,1)} %collective-permute-done.rest_2_, ...), custom_call_target="tpu_custom_call" | custom-call | flops 1610612736 | bytes 8388608 | tf_op jit(solution)/shard_map/window/pallas_call | solution.py:270
  113.0 13.0 %finish.2.rest_6_ = bf16[512,4096]{1,0:T(8,128)(2,1)} custom-call(s32[4]{0:T(128)S(1)} %copy-done.5, s32[80]{0:T(128)S(1)} %reshape.204.table, bf16[512,4096]{1,0:T(8,128)(2,1)} %query_ref.7, f32[2,512,1024]{2,1,0:T(8,128)} %get-tuple-element.41.mixed_ref, f32[2,512,1024]{2,1,0:T(8,128)} %get-tuple-element.42.level_ref, ...), custom_call_target="tpu_custom_call" | custom-call | flops 2684354560 | bytes 8388608 | tf_op jit(solution)/shard_map/finish/pallas_call | solution.py:353
  126.1 13.4 %finish.3 = bf16[512,4096]{1,0:T(8,128)(2,1)} custom-call(s32[4]{0:T(128)S(1)} %copy-done.5, s32[80]{0:T(128)S(1)} %reshape.204.table, bf16[512,4096]{1,0:T(8,128)(2,1)} %query_ref.7, f32[2,512,1024]{2,1,0:T(8,128)} %get-tuple-element.28.mixed_ref, f32[2,512,1024]{2,1,0:T(8,128)} %get-tuple-element.29.level_ref, ...), custom_call_target="tpu_custom_call", output_to_operand_aliasing={{}: (11, {})} | custom-call | flops 2684354560 | bytes 8388608 | tf_op jit(solution)/shard_map/finish/pallas_call | solution.py:353
  (80 shorter events, 1.1 us)
Async XLA Ops:
  0.0 1.0 copy-start
  1.0 1.0 copy-start.1
  2.1 100.6 %copy-start.4 = (s32[4]{0:T(128)}, s32[4]{0:T(128)S(1)}, u32[]{:S(2)}) copy-start(s32[4]{0:T(128)S(1)} %iota_xor_fusion.order) | copy-start | bytes 52
  3.8 3.2 %copy-start.11 = (bf16[2,128,512]{2,1,0:T(8,128)(2,1)}, bf16[2,128,512]{2,1,0:T(8,128)(2,1)S(1)}, u32[]{:S(2)}) copy-start(bf16[2,128,512]{2,1,0:T(8,128)(2,1)S(1)} %get-tuple-element.27) | copy-start | bytes 786436
  3.8 15.4 %copy-start.8 = (bf16[2,512,128]{2,1,0:T(8,128)(2,1)}, bf16[2,512,128]{2,1,0:T(8,128)(2,1)S(1)}, u32[]{:S(2)}) copy-start(bf16[2,512,128]{2,1,0:T(8,128)(2,1)S(1)} %get-tuple-element.25.rest_1_) | copy-start | bytes 786436
  3.8 20.3 %copy-start.9 = (bf16[2,512,128]{2,1,0:T(8,128)(2,1)}, bf16[2,512,128]{2,1,0:T(8,128)(2,1)S(1)}, u32[]{:S(2)}) copy-start(bf16[2,512,128]{2,1,0:T(8,128)(2,1)S(1)} %get-tuple-element.31.rest_1_) | copy-start | bytes 786436
  3.8 21.8 %copy-start.12 = (bf16[2,128,512]{2,1,0:T(8,128)(2,1)}, bf16[2,128,512]{2,1,0:T(8,128)(2,1)S(1)}, u32[]{:S(2)}) copy-start(bf16[2,128,512]{2,1,0:T(8,128)(2,1)S(1)} %get-tuple-element.26) | copy-start | bytes 786436
  3.8 64.7 %copy-start.7 = (bf16[2,512,128]{2,1,0:T(8,128)(2,1)}, bf16[2,512,128]{2,1,0:T(8,128)(2,1)S(1)}, u32[]{:S(2)}) copy-start(bf16[2,512,128]{2,1,0:T(8,128)(2,1)S(1)} %get-tuple-element.24.rest_0_) | copy-start | bytes 786436
  3.9 7.5 %collective-permute-start.2 = (bf16[2,512,128]{2,1,0:T(8,128)(2,1)S(1)}, bf16[2,512,128]{2,1,0:T(8,128)(2,1)S(1)}, u32[]{:S(2)}, u32[]{:S(2)}) collective-permute-start(bf16[2,512,128]{2,1,0:T(8,128)(2,1)S(1)} %get-tuple-element.31.rest_1_), channel_id=1, source_target_pairs={{0,1},{1,0},{2,3},{3,2},{4,5},{5,4},{6,7},{7,6},{8,9},{9,8},{10,11... | collective-permute-start | bytes 786440 | tf_op jit(solution)/shard_map/ppermute | solution.py:417
  4.4 9.7 %collective-permute-start.3 = (bf16[2,512,128]{2,1,0:T(8,128)(2,1)S(1)}, bf16[2,512,128]{2,1,0:T(8,128)(2,1)S(1)}, u32[]{:S(2)}, u32[]{:S(2)}) collective-permute-start(bf16[2,512,128]{2,1,0:T(8,128)(2,1)S(1)} %get-tuple-element.24.rest_0_), channel_id=1, source_target_pairs={{0,2},{1,3},{2,0},{3,1},{4,6},{5,7},{6,4},{7,5},{8,10},{9,11},{10,... | collective-permute-start | bytes 786440 | tf_op jit(solution)/shard_map/ppermute | solution.py:417
  7.0 12.3 %collective-permute-start.4 = (bf16[2,512,128]{2,1,0:T(8,128)(2,1)S(1)}, bf16[2,512,128]{2,1,0:T(8,128)(2,1)S(1)}, u32[]{:S(2)}, u32[]{:S(2)}) collective-permute-start(bf16[2,512,128]{2,1,0:T(8,128)(2,1)S(1)} %get-tuple-element.25.rest_1_), channel_id=1, source_target_pairs={{0,3},{1,2},{2,1},{3,0},{4,7},{5,6},{6,5},{7,4},{8,11},{9,10},{10,... | collective-permute-start | bytes 786440 | tf_op jit(solution)/shard_map/ppermute | solution.py:417
  21.5 5.8 %copy-start.17 = (bf16[2,384,128]{2,1,0:T(8,128)(2,1)}, bf16[2,384,128]{2,1,0:T(8,128)(2,1)S(1)}, u32[]{:S(2)}) copy-start(bf16[2,384,128]{2,1,0:T(8,128)(2,1)S(1)} %get-tuple-element.36) | copy-start | bytes 589828
  21.5 22.0 %copy-start.15 = (bf16[2,384,128]{2,1,0:T(8,128)(2,1)}, bf16[2,384,128]{2,1,0:T(8,128)(2,1)S(1)}, u32[]{:S(2)}) copy-start(bf16[2,384,128]{2,1,0:T(8,128)(2,1)S(1)} %get-tuple-element.39) | copy-start | bytes 589828
  21.5 22.0 %copy-start.16 = (bf16[2,384,128]{2,1,0:T(8,128)(2,1)}, bf16[2,384,128]{2,1,0:T(8,128)(2,1)S(1)}, u32[]{:S(2)}) copy-start(bf16[2,384,128]{2,1,0:T(8,128)(2,1)S(1)} %get-tuple-element.38) | copy-start | bytes 589828
  21.5 9.6 %collective-permute-start.14 = (bf16[2,256,128]{2,1,0:T(8,128)(2,1)S(1)}, bf16[2,256,128]{2,1,0:T(8,128)(2,1)S(1)}, u32[]{:S(2)}, u32[]{:S(2)}) collective-permute-start(bf16[2,256,128]{2,1,0:T(8,128)(2,1)S(1)} %get-tuple-element.40), channel_id=1, source_target_pairs={{0,16},{4,20},{8,24},{12,28},{16,0},{20,4},{24,8},{28,12},{1,17},{... | collective-permute-start | bytes 393224 | tf_op jit(solution)/shard_map/ppermute | solution.py:417
  24.2 7.8 %collective-permute-start.5 = (bf16[2,384,128]{2,1,0:T(8,128)(2,1)}, bf16[2,384,128]{2,1,0:T(8,128)(2,1)S(1)}, u32[]{:S(2)}, u32[]{:S(2)}) collective-permute-start(bf16[2,384,128]{2,1,0:T(8,128)(2,1)} %get-tuple-element.33), channel_id=1, source_target_pairs={{0,4},{4,0},{8,12},{12,8},{16,20},{20,16},{24,28},{28,24},{1,5},{5... | collective-permute-start | bytes 589832 | tf_op jit(solution)/shard_map/ppermute | solution.py:417
  25.7 13.4 %collective-permute-start.6 = (bf16[2,384,128]{2,1,0:T(8,128)(2,1)S(1)}, bf16[2,384,128]{2,1,0:T(8,128)(2,1)S(1)}, u32[]{:S(2)}, u32[]{:S(2)}) collective-permute-start(bf16[2,384,128]{2,1,0:T(8,128)(2,1)S(1)} %get-tuple-element.34), channel_id=1, source_target_pairs={{0,8},{4,12},{8,0},{12,4},{16,24},{20,28},{24,16},{28,20},{1,9},{5... | collective-permute-start | bytes 589832 | tf_op jit(solution)/shard_map/ppermute | solution.py:417
  27.3 16.3 %collective-permute-start.7 = (bf16[2,384,128]{2,1,0:T(8,128)(2,1)S(1)}, bf16[2,384,128]{2,1,0:T(8,128)(2,1)S(1)}, u32[]{:S(2)}, u32[]{:S(2)}) collective-permute-start(bf16[2,384,128]{2,1,0:T(8,128)(2,1)S(1)} %get-tuple-element.35), channel_id=1, source_target_pairs={{0,12},{4,8},{8,4},{12,0},{16,28},{20,24},{24,20},{28,16},{1,13},{... | collective-permute-start | bytes 589832 | tf_op jit(solution)/shard_map/ppermute | solution.py:417
  28.4 21.4 %collective-permute-start.10 = (bf16[2,384,128]{2,1,0:T(8,128)(2,1)}, bf16[2,384,128]{2,1,0:T(8,128)(2,1)S(1)}, u32[]{:S(2)}, u32[]{:S(2)}) collective-permute-start(bf16[2,384,128]{2,1,0:T(8,128)(2,1)} %get-tuple-element.37), channel_id=1, source_target_pairs={{0,20},{4,16},{8,28},{12,24},{16,4},{20,0},{24,12},{28,8},{1,21},{... | collective-permute-start | bytes 589832 | tf_op jit(solution)/shard_map/ppermute | solution.py:417
  31.1 17.1 %collective-permute-start.15 = (bf16[2,256,128]{2,1,0:T(8,128)(2,1)S(1)}, bf16[2,256,128]{2,1,0:T(8,128)(2,1)S(1)}, u32[]{:S(2)}, u32[]{:S(2)}) collective-permute-start(bf16[2,256,128]{2,1,0:T(8,128)(2,1)S(1)} %add.105), channel_id=1, source_target_pairs={{0,8},{4,12},{8,0},{12,4},{16,24},{20,28},{24,16},{28,20},{1,9},{5... | collective-permute-start | bytes 393224 | tf_op jit(solution)/shard_map/ppermute | solution.py:417
  44.1 35.2 %collective-permute-start.8 = (bf16[2,1536,128]{2,1,0:T(8,128)(2,1)S(1)}, bf16[2,1536,128]{2,1,0:T(8,128)(2,1)S(1)}, u32[]{:S(2)}, u32[]{:S(2)}) collective-permute-start(bf16[2,1536,128]{2,1,0:T(8,128)(2,1)S(1)} %join.3.rest_0_), channel_id=1, source_target_pairs={{0,2},{1,3},{2,0},{3,1},{4,6},{5,7},{6,4},{7,5},{8,10},{9,11},{10,... | collective-permute-start | bytes 2359304 | tf_op jit(solution)/shard_map/ppermute | solution.py:417
  45.7 18.7 %collective-permute-start.12 = (bf16[2,384,128]{2,1,0:T(8,128)(2,1)}, bf16[2,384,128]{2,1,0:T(8,128)(2,1)S(1)}, u32[]{:S(2)}, u32[]{:S(2)}) collective-permute-start(bf16[2,384,128]{2,1,0:T(8,128)(2,1)} %copy-done.16), channel_id=1, source_target_pairs={{0,24},{4,28},{8,16},{12,20},{16,8},{20,12},{24,0},{28,4},{1,25},{... | collective-permute-start | bytes 589832 | tf_op jit(solution)/shard_map/ppermute | solution.py:417
  48.2 14.4 %collective-permute-start.9 = (bf16[2,384,128]{2,1,0:T(8,128)(2,1)}, bf16[2,384,128]{2,1,0:T(8,128)(2,1)S(1)}, u32[]{:S(2)}, u32[]{:S(2)}) collective-permute-start(bf16[2,384,128]{2,1,0:T(8,128)(2,1)} %copy-done.17), channel_id=1, source_target_pairs={{0,16},{4,20},{8,24},{12,28},{16,0},{20,4},{24,8},{28,12},{1,17},{... | collective-permute-start | bytes 589832 | tf_op jit(solution)/shard_map/ppermute | solution.py:417
  48.3 19.9 %collective-permute-start.16 = (bf16[2,256,128]{2,1,0:T(8,128)(2,1)S(1)}, bf16[2,256,128]{2,1,0:T(8,128)(2,1)S(1)}, u32[]{:S(2)}, u32[]{:S(2)}) collective-permute-start(bf16[2,256,128]{2,1,0:T(8,128)(2,1)S(1)} %add.106), channel_id=1, source_target_pairs={{0,4},{4,0},{8,12},{12,8},{16,20},{20,16},{24,28},{28,24},{1,5},{5... | collective-permute-start | bytes 393224 | tf_op jit(solution)/shard_map/ppermute | solution.py:417
  49.8 26.7 %collective-permute-start = (bf16[2,128,512]{2,1,0:T(8,128)(2,1)}, bf16[2,128,512]{2,1,0:T(8,128)(2,1)}, u32[]{:S(2)}, u32[]{:S(2)}) collective-permute-start(bf16[2,128,512]{2,1,0:T(8,128)(2,1)} %copy-done.12), channel_id=1, source_target_pairs={{0,1},{1,2},{2,3},{3,4},{4,5},{5,6},{6,7},{7,8},{8,9},{9,10},{10,1... | collective-permute-start | bytes 786440 | tf_op jit(solution)/shard_map/ppermute | solution.py:423
  62.7 14.9 %collective-permute-start.1 = (bf16[2,128,512]{2,1,0:T(8,128)(2,1)}, bf16[2,128,512]{2,1,0:T(8,128)(2,1)S(1)}, u32[]{:S(2)}, u32[]{:S(2)}) collective-permute-start(bf16[2,128,512]{2,1,0:T(8,128)(2,1)} %copy-done.11), channel_id=1, source_target_pairs={{1,0},{2,1},{3,2},{4,3},{5,4},{6,5},{7,6},{8,7},{9,8},{10,9},{11,1... | collective-permute-start | bytes 786440 | tf_op jit(solution)/shard_map/ppermute | solution.py:424
  64.4 10.7 %copy-start.2 = (bf16[2,384,128]{2,1,0:T(8,128)(2,1)}, bf16[2,384,128]{2,1,0:T(8,128)(2,1)S(1)}, u32[]{:S(2)}) copy-start(bf16[2,384,128]{2,1,0:T(8,128)(2,1)S(1)} %collective-permute-done.12.refs_0_) | copy-start | bytes 589828
  64.4 10.7 %collective-permute-start.13 = (bf16[2,384,128]{2,1,0:T(8,128)(2,1)}, bf16[2,384,128]{2,1,0:T(8,128)(2,1)S(1)}, u32[]{:S(2)}, u32[]{:S(2)}) collective-permute-start(bf16[2,384,128]{2,1,0:T(8,128)(2,1)} %copy-done.15), channel_id=1, source_target_pairs={{0,28},{4,24},{8,20},{12,16},{16,12},{20,8},{24,4},{28,0},{1,29},{... | collective-permute-start | bytes 589832 | tf_op jit(solution)/shard_map/ppermute | solution.py:417
  68.2 11.3 %collective-permute-start.22 = (bf16[2,768,128]{2,1,0:T(8,128)(2,1)S(1)}, bf16[2,768,128]{2,1,0:T(8,128)(2,1)}, u32[]{:S(2)}, u32[]{:S(2)}) collective-permute-start(bf16[2,768,128]{2,1,0:T(8,128)(2,1)S(1)} %join.4.rest_1_), channel_id=1, source_target_pairs={{0,1},{1,0},{2,3},{3,2},{4,5},{5,4},{6,7},{7,6},{8,9},{9,8},{10,11... | collective-permute-start | bytes 1179656 | tf_op jit(solution)/shard_map/ppermute | solution.py:417
  75.1 37.9 %collective-permute-start.21 = (bf16[2,1536,128]{2,1,0:T(8,128)(2,1)S(1)}, bf16[2,1536,128]{2,1,0:T(8,128)(2,1)S(1)}, u32[]{:S(2)}, u32[]{:S(2)}) collective-permute-start(bf16[2,1536,128]{2,1,0:T(8,128)(2,1)S(1)} %join.3.rest_0_), channel_id=1, source_target_pairs={{0,1},{1,0},{2,3},{3,2},{4,5},{5,4},{6,7},{7,6},{8,9},{9,8},{10,11... | collective-permute-start | bytes 2359304 | tf_op jit(solution)/shard_map/ppermute | solution.py:417
  75.2 0.9 copy-start.3
  76.5 15.0 %collective-permute-start.17 = (bf16[2,1024,128]{2,1,0:T(8,128)(2,1)S(1)}, bf16[2,1024,128]{2,1,0:T(8,128)(2,1)}, u32[]{:S(2)}, u32[]{:S(2)}) collective-permute-start(bf16[2,1024,128]{2,1,0:T(8,128)(2,1)S(1)} %join.5.rest_2_), channel_id=1, source_target_pairs={{0,2},{1,3},{2,0},{3,1},{4,6},{5,7},{6,4},{7,5},{8,10},{9,11},{10,... | collective-permute-start | bytes 1572872 | tf_op jit(solution)/shard_map/ppermute | solution.py:417
  77.6 0.7 copy-start.13
  78.2 24.5 %collective-permute-start.11 = (bf16[2,768,128]{2,1,0:T(8,128)(2,1)S(1)}, bf16[2,768,128]{2,1,0:T(8,128)(2,1)}, u32[]{:S(2)}, u32[]{:S(2)}) collective-permute-start(bf16[2,768,128]{2,1,0:T(8,128)(2,1)S(1)} %join.4.rest_1_), channel_id=1, source_target_pairs={{0,2},{1,3},{2,0},{3,1},{4,6},{5,7},{6,4},{7,5},{8,10},{9,11},{10,... | collective-permute-start | bytes 1179656 | tf_op jit(solution)/shard_map/ppermute | solution.py:417
  79.3 46.8 %collective-permute-start.18 = (bf16[2,1536,128]{2,1,0:T(8,128)(2,1)S(1)}, bf16[2,1536,128]{2,1,0:T(8,128)(2,1)}, u32[]{:S(2)}, u32[]{:S(2)}) collective-permute-start(bf16[2,1536,128]{2,1,0:T(8,128)(2,1)S(1)} %collective-permute-done.8.rest_0_), channel_id=1, source_target_pairs={{0,1},{1,0},{2,3},{3,2},{4,5},{5,4},{6,7},{7,6},{8,9},{9,8},{10,11... | collective-permute-start | bytes 2359304 | tf_op jit(solution)/shard_map/ppermute | solution.py:417
  79.5 33.5 %collective-permute-start.23 = (bf16[2,1024,128]{2,1,0:T(8,128)(2,1)S(1)}, bf16[2,1024,128]{2,1,0:T(8,128)(2,1)}, u32[]{:S(2)}, u32[]{:S(2)}) collective-permute-start(bf16[2,1024,128]{2,1,0:T(8,128)(2,1)S(1)} %join.5.rest_2_), channel_id=1, source_target_pairs={{0,1},{1,0},{2,3},{3,2},{4,5},{5,4},{6,7},{7,6},{8,9},{9,8},{10,11... | collective-permute-start | bytes 1572872 | tf_op jit(solution)/shard_map/ppermute | solution.py:417
  80.2 23.1 %copy-start.6 = (s32[8]{0:T(128)}, s32[8]{0:T(128)S(1)}, u32[]{:S(2)}) copy-start(s32[8]{0:T(128)S(1)} %reshape.206.flags) | copy-start | bytes 100
  91.5 34.6 %collective-permute-start.20 = (bf16[2,1024,128]{2,1,0:T(8,128)(2,1)}, bf16[2,1024,128]{2,1,0:T(8,128)(2,1)S(1)}, u32[]{:S(2)}, u32[]{:S(2)}) collective-permute-start(bf16[2,1024,128]{2,1,0:T(8,128)(2,1)} %collective-permute-done.17.rest_2_), channel_id=1, source_target_pairs={{0,1},{1,0},{2,3},{3,2},{4,5},{5,4},{6,7},{7,6},{8,9},{9,8},{10,11... | collective-permute-start | bytes 1572872 | tf_op jit(solution)/shard_map/ppermute | solution.py:417
  91.5 1.0 copy-start.10
  92.4 0.9 copy-start.14
  102.7 10.3 %copy-start.5 = (s32[4]{0:T(128)S(1)}, s32[4]{0:T(128)}, u32[]{:S(2)}) copy-start(s32[4]{0:T(128)} %copy-done.4) | copy-start | bytes 52
  102.7 23.3 %collective-permute-start.19 = (bf16[2,768,128]{2,1,0:T(8,128)(2,1)}, bf16[2,768,128]{2,1,0:T(8,128)(2,1)}, u32[]{:S(2)}, u32[]{:S(2)}) collective-permute-start(bf16[2,768,128]{2,1,0:T(8,128)(2,1)} %collective-permute-done.11.rest_1_), channel_id=1, source_target_pairs={{0,1},{1,0},{2,3},{3,2},{4,5},{5,4},{6,7},{7,6},{8,9},{9,8},{10,11... | collective-permute-start | bytes 1179656 | tf_op jit(solution)/shard_map/ppermute | solution.py:417

commit v3 on v2

--- a/solution.py
+++ b/solution.py
@@ -291,26 +291,47 @@
 
 
 def finish_kernel(begin, counts, aliased, order, table, query_ref, mixed_ref, level_ref, *rest):
-    sources, (out_ref, held) = rest[: sum(counts)], rest[sum(counts) + aliased :]
+    sources, (out_ref, held, sems) = rest[: sum(counts)], rest[sum(counts) + aliased :]
     part, step = pl.program_id(0), pl.program_id(1)
     grouping = query_ref.shape[1] // HEAD_DIM
-    number = 0
-    for r, count in enumerate(counts):
-
-        @pl.when((part == r) & (step == 0))
-        def _(mine=sources[number : number + count]):
-            start = 0
-            for source in mine:
-                held[:, start : start + source.shape[1]] = source[...]
-                start += source.shape[1]
-
-        number += count
+    later, number = [], counts[0]
+    for r in range(1, len(counts)):
+        start, group = 0, []
+        for place, source in enumerate(sources[number : number + counts[r]]):
+            rows = source.shape[1]
+            group.append(
+                pltpu.make_async_copy(
+                    source, held.at[r, :, start : start + rows], sems.at[r, place]
+                )
+            )
+            start += rows
+        later.append(group)
+        number += counts[r]
+
+    @pl.when((part == 0) & (step == 0))
+    def _():
+        for group in later:
+            for copy in group:
+                copy.start()
+        start = 0
+        for source in sources[: counts[0]]:
+            held[0, :, start : start + source.shape[1]] = source[...]
+            start += source.shape[1]
+
+    for r, group in enumerate(later):
+
+        @pl.when((part == r + 1) & (step == 0))
+        def _(group=group):
+            for copy in group:
+                copy.wait()
+
     base = ((begin + part) * pl.num_programs(1) + step) * TOGETHER * LISTED
 
     def listed(which, unit):
         return jnp.concatenate(
             [
                 held[
+                    part,
                     which,
                     pl.ds(pl.multiple_of(table[base + unit * LISTED + n] * BLOCK, BLOCK), BLOCK),
                 ]
@@ -359,13 +380,15 @@
                 spec,
             ]
             + [pl.BlockSpec((1, some, width), lambda r, i, order, table: (r, i, 0))] * 2
-            + [whole_block(array) for array in arrays]
-            + [ANY] * len(aliased),
+            + [whole_block(array) for array in parts[0]]
+            + [ANY] * (len(arrays) - len(parts[0]) + len(aliased)),
             out_specs=spec,
             scratch_shapes=[
                 pltpu.VMEM(
-                    (2, sum(array.shape[1] for array in parts[0]), HEAD_DIM), queries.dtype
+                    (len(parts), 2, sum(array.shape[1] for array in parts[0]), HEAD_DIM),
+                    queries.dtype,
                 ),
+                pltpu.SemaphoreType.DMA((len(parts), len(parts[0]))),
             ],
         ),
         out_shape=jax.ShapeDtypeStruct((rows, columns), queries.dtype),

time: 140 us -> 139 us (level)
  no operation moved by 1% of the time
where the time goes in v3:
time: 139 us
  Pallas kernels  49.7 us (36%)
  waiting for transfers between devices  48.9 us (35%)
  starting transfers between devices  27.6 us (20%)
  local copies, waits for them, and re-layouts  8.8 us (6%)
  other arithmetic  3.21 us (2%)
    ppermute x22, waiting for transfers between devices, across(): return lax.ppermute(array, axis, [(i, i ^ bit) for i in range(count)])  48.9 us
    pallas_call x2, Pallas kernels, finish(): pl.pallas_call(functools.partial(finish_kernel, begin, [len(part) for par...  25.5 us
    ppermute x22, starting transfers between devices, across(): return lax.ppermute(array, axis, [(i, i ^ bit) for i in range(count)])  24.2 us
    pallas_call x2, Pallas kernels, window_share(): pl.pallas_call(functools.partial(window_kernel, parts), grid_spec=pltpu.P...  19.1 us
    unnamed x37, local copies, waits for them, and re-layouts  5.73 us
  transfers between devices with their start and end apart: 24, of which 8 were waited for; matrix products, arithmetic and copies ran while one was open for 5% of the time, Pallas kernels for 24%

profile of v3, /device:TPU:0, one launch (start us, length us, event | category | flops | bytes accessed | tf_op | source)
XLA Modules:
  0.0 138.7 jit_solution(12987282803599947941)
XLA Ops:
  0.0 1.0 copy-done
  1.0 1.0 copy-done.1
  2.1 1.7 %pack.1 = (bf16[2,512,128]{2,1,0:T(8,128)(2,1)S(1)}, bf16[2,512,128]{2,1,0:T(8,128)(2,1)S(1)}, bf16[2,512,128]{2,1,0:T(8,128)(2,1)S(1)}, bf16[2,512,128]{2,1,0:T...) custom-call(s32[4]{0:T(128)S(1)} %iota_xor_fusion.order, ...), custom_call_target="tpu_custom_call" | custom-call | tf_op jit(solution)/shard_map/pack/pallas_call | solution.py:72
  3.9 0.6 collective-permute-start.2
  4.4 2.6 %collective-permute-start.3 = (bf16[2,512,128]{2,1,0:T(8,128)(2,1)S(1)}, bf16[2,512,128]{2,1,0:T(8,128)(2,1)S(1)}, u32[]{:S(2)}, u32[]{:S(2)}) collective-permute-start(bf16[2,512,128]{2,1,0:T(8,128)(2,1)S(1)} %get-tuple-element.24.rest_0_), channel_id=1, source_target_pairs={{0,2},{1,3},{2,0},{3,1},{4,6},{5,7},{6,4},{7,5},{8,10},{9,11},{10,... | collective-permute-start | bytes 786440 | tf_op jit(solution)/shard_map/ppermute | solution.py:440
  7.0 0.7 fusion.10
  7.7 0.7 fusion.9
  8.4 0.8 reshape.202
  9.4 0.2 fusion
  9.6 0.2 convert_reduce_fusion
  9.8 0.1 select_reduce_fusion
  10.0 0.1 copy.19
  10.1 0.1 copy.13
  10.2 0.1 reshape.203
  10.3 0.6 gather_fusion.1
  10.9 0.2 and_reduce_fusion
  11.2 0.1 copy.20
  11.3 0.1 reshape.205.shared
  11.4 2.7 %collective-permute-done.3.rest_2_ = bf16[2,512,128]{2,1,0:T(8,128)(2,1)S(1)} collective-permute-done((bf16[2,512,128]{2,1,0:T(8,128)(2,1)S(1)}, bf16[2,512,128]{2,1,0:T(8,128)(2,1)S(1)}, u32[]{:S(2)}, u32[]{:S(2)}) %collective-permute-start.3) | collective-permute-done | bytes 262176 | tf_op jit(solution)/shard_map/ppermute | solution.py:440
  14.1 5.1 %collective-permute-done.4.rest_3_ = bf16[2,512,128]{2,1,0:T(8,128)(2,1)S(1)} collective-permute-done((bf16[2,512,128]{2,1,0:T(8,128)(2,1)S(1)}, bf16[2,512,128]{2,1,0:T(8,128)(2,1)S(1)}, u32[]{:S(2)}, u32[]{:S(2)}) %collective-permute-start.4) | collective-permute-done | bytes 262176 | tf_op jit(solution)/shard_map/ppermute | solution.py:440
  19.2 2.3 %pick.1 = (bf16[2,384,128]{2,1,0:T(8,128)(2,1)S(1)}, bf16[2,384,128]{2,1,0:T(8,128)(2,1)}, bf16[2,384,128]{2,1,0:T(8,128)(2,1)S(1)}, bf16[2,384,128]{2,1,0:T(8,1...) custom-call(s32[4]{0:T(128)S(1)} %iota_xor_fusion.order, ...), custom_call_target="tpu_custom_call" | custom-call | tf_op jit(solution)/shard_map/pick/pallas_call | solution.py:125
  21.5 2.6 %collective-permute-start.14 = (bf16[2,256,128]{2,1,0:T(8,128)(2,1)S(1)}, bf16[2,256,128]{2,1,0:T(8,128)(2,1)S(1)}, u32[]{:S(2)}, u32[]{:S(2)}) collective-permute-start(bf16[2,256,128]{2,1,0:T(8,128)(2,1)S(1)} %get-tuple-element.40), channel_id=1, source_target_pairs={{0,16},{4,20},{8,24},{12,28},{16,0},{20,4},{24,8},{28,12},{1,17},{... | collective-permute-start | bytes 393224 | tf_op jit(solution)/shard_map/ppermute | solution.py:440
  24.2 1.5 %collective-permute-start.5 = (bf16[2,384,128]{2,1,0:T(8,128)(2,1)}, bf16[2,384,128]{2,1,0:T(8,128)(2,1)S(1)}, u32[]{:S(2)}, u32[]{:S(2)}) collective-permute-start(bf16[2,384,128]{2,1,0:T(8,128)(2,1)} %get-tuple-element.33), channel_id=1, source_target_pairs={{0,4},{4,0},{8,12},{12,8},{16,20},{20,16},{24,28},{28,24},{1,5},{5... | collective-permute-start | bytes 589832 | tf_op jit(solution)/shard_map/ppermute | solution.py:440
  25.7 1.6 %collective-permute-start.6 = (bf16[2,384,128]{2,1,0:T(8,128)(2,1)S(1)}, bf16[2,384,128]{2,1,0:T(8,128)(2,1)S(1)}, u32[]{:S(2)}, u32[]{:S(2)}) collective-permute-start(bf16[2,384,128]{2,1,0:T(8,128)(2,1)S(1)} %get-tuple-element.34), channel_id=1, source_target_pairs={{0,8},{4,12},{8,0},{12,4},{16,24},{20,28},{24,16},{28,20},{1,9},{5... | collective-permute-start | bytes 589832 | tf_op jit(solution)/shard_map/ppermute | solution.py:440
  27.3 0.4 collective-permute-start.7
  27.7 0.1 copy.14
  27.8 0.1 copy.15
  27.9 0.3 convert_reduce_fusion.1
  28.3 0.1 copy.16
  28.4 1.3 collective-permute-start.10
  29.7 1.4 %collective-permute-done.14 = bf16[2,256,128]{2,1,0:T(8,128)(2,1)S(1)} collective-permute-done((bf16[2,256,128]{2,1,0:T(8,128)(2,1)S(1)}, bf16[2,256,128]{2,1,0:T(8,128)(2,1)S(1)}, u32[]{:S(2)}, u32[]{:S(2)}) %collective-permute-start.14) | collective-permute-done | bytes 131104 | tf_op jit(solution)/shard_map/ppermute | solution.py:440
  31.1 0.8 collective-permute-start.15
  31.9 7.2 %collective-permute-done.6.refs_2_ = bf16[2,384,128]{2,1,0:T(8,128)(2,1)S(1)} collective-permute-done((bf16[2,384,128]{2,1,0:T(8,128)(2,1)S(1)}, bf16[2,384,128]{2,1,0:T(8,128)(2,1)S(1)}, u32[]{:S(2)}, u32[]{:S(2)}) %collective-permute-start.6) | collective-permute-done | bytes 196640 | tf_op jit(solution)/shard_map/ppermute | solution.py:440
  39.1 4.4 %collective-permute-done.7.refs_3_ = bf16[2,384,128]{2,1,0:T(8,128)(2,1)S(1)} collective-permute-done((bf16[2,384,128]{2,1,0:T(8,128)(2,1)S(1)}, bf16[2,384,128]{2,1,0:T(8,128)(2,1)S(1)}, u32[]{:S(2)}, u32[]{:S(2)}) %collective-permute-start.7) | collective-permute-done | bytes 196640 | tf_op jit(solution)/shard_map/ppermute | solution.py:440
  43.5 0.5 join.3.rest_0_
  44.1 1.6 %collective-permute-start.8 = (bf16[2,1536,128]{2,1,0:T(8,128)(2,1)S(1)}, bf16[2,1536,128]{2,1,0:T(8,128)(2,1)S(1)}, u32[]{:S(2)}, u32[]{:S(2)}) collective-permute-start(bf16[2,1536,128]{2,1,0:T(8,128)(2,1)S(1)} %join.3.rest_0_), channel_id=1, source_target_pairs={{0,2},{1,3},{2,0},{3,1},{4,6},{5,7},{6,4},{7,5},{8,10},{9,11},{10,... | collective-permute-start | bytes 2359304 | tf_op jit(solution)/shard_map/ppermute | solution.py:440
  45.6 0.1 fusion.4
  45.7 2.5 %collective-permute-start.12 = (bf16[2,384,128]{2,1,0:T(8,128)(2,1)}, bf16[2,384,128]{2,1,0:T(8,128)(2,1)S(1)}, u32[]{:S(2)}, u32[]{:S(2)}) collective-permute-start(bf16[2,384,128]{2,1,0:T(8,128)(2,1)} %copy-done.16), channel_id=1, source_target_pairs={{0,24},{4,28},{8,16},{12,20},{16,8},{20,12},{24,0},{28,4},{1,25},{... | collective-permute-start | bytes 589832 | tf_op jit(solution)/shard_map/ppermute | solution.py:440
  48.3 1.5 %collective-permute-start.16 = (bf16[2,256,128]{2,1,0:T(8,128)(2,1)S(1)}, bf16[2,256,128]{2,1,0:T(8,128)(2,1)S(1)}, u32[]{:S(2)}, u32[]{:S(2)}) collective-permute-start(bf16[2,256,128]{2,1,0:T(8,128)(2,1)S(1)} %add.106), channel_id=1, source_target_pairs={{0,4},{4,0},{8,12},{12,8},{16,20},{20,16},{24,28},{28,24},{1,5},{5... | collective-permute-start | bytes 393224 | tf_op jit(solution)/shard_map/ppermute | solution.py:440
  49.8 2.0 %collective-permute-start = (bf16[2,128,512]{2,1,0:T(8,128)(2,1)}, bf16[2,128,512]{2,1,0:T(8,128)(2,1)}, u32[]{:S(2)}, u32[]{:S(2)}) collective-permute-start(bf16[2,128,512]{2,1,0:T(8,128)(2,1)} %copy-done.12), channel_id=1, source_target_pairs={{0,1},{1,2},{2,3},{3,4},{4,5},{5,6},{6,7},{7,8},{8,9},{9,10},{10,1... | collective-permute-start | bytes 786440 | tf_op jit(solution)/shard_map/ppermute | solution.py:446
  51.8 0.6 gather_fusion
  52.4 0.1 gather.11
  52.5 10.2 %collective-permute-done.9.refs_0_ = bf16[2,384,128]{2,1,0:T(8,128)(2,1)S(1)} collective-permute-done((bf16[2,384,128]{2,1,0:T(8,128)(2,1)}, bf16[2,384,128]{2,1,0:T(8,128)(2,1)S(1)}, u32[]{:S(2)}, u32[]{:S(2)}) %collective-permute-start.9) | collective-permute-done | bytes 196640 | tf_op jit(solution)/shard_map/ppermute | solution.py:440
  62.7 1.5 %collective-permute-start.1 = (bf16[2,128,512]{2,1,0:T(8,128)(2,1)}, bf16[2,128,512]{2,1,0:T(8,128)(2,1)S(1)}, u32[]{:S(2)}, u32[]{:S(2)}) collective-permute-start(bf16[2,128,512]{2,1,0:T(8,128)(2,1)} %copy-done.11), channel_id=1, source_target_pairs={{1,0},{2,1},{3,2},{4,3},{5,4},{6,5},{7,6},{8,7},{9,8},{10,9},{11,1... | collective-permute-start | bytes 786440 | tf_op jit(solution)/shard_map/ppermute | solution.py:447
  64.1 0.3 join.4.rest_1_
  64.4 3.8 %collective-permute-start.13 = (bf16[2,384,128]{2,1,0:T(8,128)(2,1)}, bf16[2,384,128]{2,1,0:T(8,128)(2,1)S(1)}, u32[]{:S(2)}, u32[]{:S(2)}) collective-permute-start(bf16[2,384,128]{2,1,0:T(8,128)(2,1)} %copy-done.15), channel_id=1, source_target_pairs={{0,28},{4,24},{8,20},{12,16},{16,12},{20,8},{24,4},{28,0},{1,29},{... | collective-permute-start | bytes 589832 | tf_op jit(solution)/shard_map/ppermute | solution.py:440
  68.2 0.2 collective-permute-start.22
  68.5 6.6 %collective-permute-done.13.refs_1_ = bf16[2,384,128]{2,1,0:T(8,128)(2,1)S(1)} collective-permute-done((bf16[2,384,128]{2,1,0:T(8,128)(2,1)}, bf16[2,384,128]{2,1,0:T(8,128)(2,1)S(1)}, u32[]{:S(2)}, u32[]{:S(2)}) %collective-permute-start.13) | collective-permute-done | bytes 196640 | tf_op jit(solution)/shard_map/ppermute | solution.py:440
  75.2 0.9 copy-done.3
  76.1 0.3 join.5.rest_2_
  76.5 1.1 collective-permute-start.17
  77.6 0.7 copy-done.13
  78.2 1.0 collective-permute-start.11
  79.4 0.1 reshape.204.table
  79.5 0.6 collective-permute-start.23
  80.1 0.1 reshape.206.flags
  80.2 11.2 %collective-permute-done.17.rest_2_ = bf16[2,1024,128]{2,1,0:T(8,128)(2,1)} collective-permute-done((bf16[2,1024,128]{2,1,0:T(8,128)(2,1)S(1)}, bf16[2,1024,128]{2,1,0:T(8,128)(2,1)}, u32[]{:S(2)}, u32[]{:S(2)}) %collective-permute-start.17) | collective-permute-done | bytes 524320 | tf_op jit(solution)/shard_map/ppermute | solution.py:440
  91.5 0.9 copy-done.10
  92.4 0.9 copy-done.14
  93.4 9.3 %window.3 = (f32[2,512,1024]{2,1,0:T(8,128)}, f32[2,512,1024]{2,1,0:T(8,128)}) custom-call(s32[4]{0:T(128)S(1)} %iota_xor_fusion.order, s32[8]{0:T(128)S(1)} %reshape.206.flags, bf16[512,4096]{1,0:T(8,128)(2,1)} %query_ref.7, bf16[2,512,128]{2,1,0:T(8,128)(2,1)S(1)} %get-tuple-element.30.rest_0_, bf16[2,512,128]{2,1,0:T(8,128)(2,1)S(1)} %copy-done.10, ...), custom_call_target="tpu_custom_call" | custom-call | flops 1610612736 | bytes 8388608 | tf_op jit(solution)/shard_map/window/pallas_call | solution.py:270
  102.7 0.6 collective-permute-start.19
  103.3 9.7 %window.2 = (f32[2,512,1024]{2,1,0:T(8,128)}, f32[2,512,1024]{2,1,0:T(8,128)}) custom-call(s32[4]{0:T(128)} %copy-done.4, s32[8]{0:T(128)} %copy-done.6, bf16[512,4096]{1,0:T(8,128)(2,1)} %query_ref.7, bf16[2,512,128]{2,1,0:T(8,128)(2,1)} %copy-done.7, bf16[2,512,128]{2,1,0:T(8,128)(2,1)} %copy-done.8, bf16[2,128,512]{2,1,0:T(8,128)(2,1)} %collective-permute-done.rest_2_, ...), custom_call_target="tpu_custom_call" | custom-call | flops 1610612736 | bytes 8388608 | tf_op jit(solution)/shard_map/window/pallas_call | solution.py:270
  113.0 12.4 %finish.2.rest_6_ = bf16[512,4096]{1,0:T(8,128)(2,1)} custom-call(s32[4]{0:T(128)S(1)} %copy-done.5, s32[80]{0:T(128)S(1)} %reshape.204.table, bf16[512,4096]{1,0:T(8,128)(2,1)} %query_ref.7, f32[2,512,1024]{2,1,0:T(8,128)} %get-tuple-element.41.mixed_ref, f32[2,512,1024]{2,1,0:T(8,128)} %get-tuple-element.42.level_ref, ...), custom_call_target="tpu_custom_call" | custom-call | flops 2684354560 | bytes 8388608 | tf_op jit(solution)/shard_map/finish/pallas_call | solution.py:374
  125.5 13.0 %finish.3 = bf16[512,4096]{1,0:T(8,128)(2,1)} custom-call(s32[4]{0:T(128)S(1)} %copy-done.5, s32[80]{0:T(128)S(1)} %reshape.204.table, bf16[512,4096]{1,0:T(8,128)(2,1)} %query_ref.7, f32[2,512,1024]{2,1,0:T(8,128)} %get-tuple-element.28.mixed_ref, f32[2,512,1024]{2,1,0:T(8,128)} %get-tuple-element.29.level_ref, ...), custom_call_target="tpu_custom_call", output_to_operand_aliasing={{}: (11, {})} | custom-call | flops 2684354560 | bytes 8388608 | tf_op jit(solution)/shard_map/finish/pallas_call | solution.py:374
  (80 shorter events, 1.1 us)
Async XLA Ops:
  0.0 1.0 copy-start
  1.0 1.0 copy-start.1
  2.1 100.6 %copy-start.4 = (s32[4]{0:T(128)}, s32[4]{0:T(128)S(1)}, u32[]{:S(2)}) copy-start(s32[4]{0:T(128)S(1)} %iota_xor_fusion.order) | copy-start | bytes 52
  3.8 3.2 %copy-start.11 = (bf16[2,128,512]{2,1,0:T(8,128)(2,1)}, bf16[2,128,512]{2,1,0:T(8,128)(2,1)S(1)}, u32[]{:S(2)}) copy-start(bf16[2,128,512]{2,1,0:T(8,128)(2,1)S(1)} %get-tuple-element.27) | copy-start | bytes 786436
  3.8 15.4 %copy-start.8 = (bf16[2,512,128]{2,1,0:T(8,128)(2,1)}, bf16[2,512,128]{2,1,0:T(8,128)(2,1)S(1)}, u32[]{:S(2)}) copy-start(bf16[2,512,128]{2,1,0:T(8,128)(2,1)S(1)} %get-tuple-element.25.rest_1_) | copy-start | bytes 786436
  3.8 20.3 %copy-start.9 = (bf16[2,512,128]{2,1,0:T(8,128)(2,1)}, bf16[2,512,128]{2,1,0:T(8,128)(2,1)S(1)}, u32[]{:S(2)}) copy-start(bf16[2,512,128]{2,1,0:T(8,128)(2,1)S(1)} %get-tuple-element.31.rest_1_) | copy-start | bytes 786436
  3.8 21.8 %copy-start.12 = (bf16[2,128,512]{2,1,0:T(8,128)(2,1)}, bf16[2,128,512]{2,1,0:T(8,128)(2,1)S(1)}, u32[]{:S(2)}) copy-start(bf16[2,128,512]{2,1,0:T(8,128)(2,1)S(1)} %get-tuple-element.26) | copy-start | bytes 786436
  3.8 64.7 %copy-start.7 = (bf16[2,512,128]{2,1,0:T(8,128)(2,1)}, bf16[2,512,128]{2,1,0:T(8,128)(2,1)S(1)}, u32[]{:S(2)}) copy-start(bf16[2,512,128]{2,1,0:T(8,128)(2,1)S(1)} %get-tuple-element.24.rest_0_) | copy-start | bytes 786436
  3.9 7.5 %collective-permute-start.2 = (bf16[2,512,128]{2,1,0:T(8,128)(2,1)S(1)}, bf16[2,512,128]{2,1,0:T(8,128)(2,1)S(1)}, u32[]{:S(2)}, u32[]{:S(2)}) collective-permute-start(bf16[2,512,128]{2,1,0:T(8,128)(2,1)S(1)} %get-tuple-element.31.rest_1_), channel_id=1, source_target_pairs={{0,1},{1,0},{2,3},{3,2},{4,5},{5,4},{6,7},{7,6},{8,9},{9,8},{10,11... | collective-permute-start | bytes 786440 | tf_op jit(solution)/shard_map/ppermute | solution.py:440
  4.4 9.7 %collective-permute-start.3 = (bf16[2,512,128]{2,1,0:T(8,128)(2,1)S(1)}, bf16[2,512,128]{2,1,0:T(8,128)(2,1)S(1)}, u32[]{:S(2)}, u32[]{:S(2)}) collective-permute-start(bf16[2,512,128]{2,1,0:T(8,128)(2,1)S(1)} %get-tuple-element.24.rest_0_), channel_id=1, source_target_pairs={{0,2},{1,3},{2,0},{3,1},{4,6},{5,7},{6,4},{7,5},{8,10},{9,11},{10,... | collective-permute-start | bytes 786440 | tf_op jit(solution)/shard_map/ppermute | solution.py:440
  7.0 12.3 %collective-permute-start.4 = (bf16[2,512,128]{2,1,0:T(8,128)(2,1)S(1)}, bf16[2,512,128]{2,1,0:T(8,128)(2,1)S(1)}, u32[]{:S(2)}, u32[]{:S(2)}) collective-permute-start(bf16[2,512,128]{2,1,0:T(8,128)(2,1)S(1)} %get-tuple-element.25.rest_1_), channel_id=1, source_target_pairs={{0,3},{1,2},{2,1},{3,0},{4,7},{5,6},{6,5},{7,4},{8,11},{9,10},{10,... | collective-permute-start | bytes 786440 | tf_op jit(solution)/shard_map/ppermute | solution.py:440
  21.5 5.8 %copy-start.17 = (bf16[2,384,128]{2,1,0:T(8,128)(2,1)}, bf16[2,384,128]{2,1,0:T(8,128)(2,1)S(1)}, u32[]{:S(2)}) copy-start(bf16[2,384,128]{2,1,0:T(8,128)(2,1)S(1)} %get-tuple-element.36) | copy-start | bytes 589828
  21.5 22.0 %copy-start.15 = (bf16[2,384,128]{2,1,0:T(8,128)(2,1)}, bf16[2,384,128]{2,1,0:T(8,128)(2,1)S(1)}, u32[]{:S(2)}) copy-start(bf16[2,384,128]{2,1,0:T(8,128)(2,1)S(1)} %get-tuple-element.39) | copy-start | bytes 589828
  21.5 22.0 %copy-start.16 = (bf16[2,384,128]{2,1,0:T(8,128)(2,1)}, bf16[2,384,128]{2,1,0:T(8,128)(2,1)S(1)}, u32[]{:S(2)}) copy-start(bf16[2,384,128]{2,1,0:T(8,128)(2,1)S(1)} %get-tuple-element.38) | copy-start | bytes 589828
  21.5 9.6 %collective-permute-start.14 = (bf16[2,256,128]{2,1,0:T(8,128)(2,1)S(1)}, bf16[2,256,128]{2,1,0:T(8,128)(2,1)S(1)}, u32[]{:S(2)}, u32[]{:S(2)}) collective-permute-start(bf16[2,256,128]{2,1,0:T(8,128)(2,1)S(1)} %get-tuple-element.40), channel_id=1, source_target_pairs={{0,16},{4,20},{8,24},{12,28},{16,0},{20,4},{24,8},{28,12},{1,17},{... | collective-permute-start | bytes 393224 | tf_op jit(solution)/shard_map/ppermute | solution.py:440
  24.2 7.8 %collective-permute-start.5 = (bf16[2,384,128]{2,1,0:T(8,128)(2,1)}, bf16[2,384,128]{2,1,0:T(8,128)(2,1)S(1)}, u32[]{:S(2)}, u32[]{:S(2)}) collective-permute-start(bf16[2,384,128]{2,1,0:T(8,128)(2,1)} %get-tuple-element.33), channel_id=1, source_target_pairs={{0,4},{4,0},{8,12},{12,8},{16,20},{20,16},{24,28},{28,24},{1,5},{5... | collective-permute-start | bytes 589832 | tf_op jit(solution)/shard_map/ppermute | solution.py:440
  25.7 13.4 %collective-permute-start.6 = (bf16[2,384,128]{2,1,0:T(8,128)(2,1)S(1)}, bf16[2,384,128]{2,1,0:T(8,128)(2,1)S(1)}, u32[]{:S(2)}, u32[]{:S(2)}) collective-permute-start(bf16[2,384,128]{2,1,0:T(8,128)(2,1)S(1)} %get-tuple-element.34), channel_id=1, source_target_pairs={{0,8},{4,12},{8,0},{12,4},{16,24},{20,28},{24,16},{28,20},{1,9},{5... | collective-permute-start | bytes 589832 | tf_op jit(solution)/shard_map/ppermute | solution.py:440
  27.3 16.3 %collective-permute-start.7 = (bf16[2,384,128]{2,1,0:T(8,128)(2,1)S(1)}, bf16[2,384,128]{2,1,0:T(8,128)(2,1)S(1)}, u32[]{:S(2)}, u32[]{:S(2)}) collective-permute-start(bf16[2,384,128]{2,1,0:T(8,128)(2,1)S(1)} %get-tuple-element.35), channel_id=1, source_target_pairs={{0,12},{4,8},{8,4},{12,0},{16,28},{20,24},{24,20},{28,16},{1,13},{... | collective-permute-start | bytes 589832 | tf_op jit(solution)/shard_map/ppermute | solution.py:440
  28.4 21.4 %collective-permute-start.10 = (bf16[2,384,128]{2,1,0:T(8,128)(2,1)}, bf16[2,384,128]{2,1,0:T(8,128)(2,1)S(1)}, u32[]{:S(2)}, u32[]{:S(2)}) collective-permute-start(bf16[2,384,128]{2,1,0:T(8,128)(2,1)} %get-tuple-element.37), channel_id=1, source_target_pairs={{0,20},{4,16},{8,28},{12,24},{16,4},{20,0},{24,12},{28,8},{1,21},{... | collective-permute-start | bytes 589832 | tf_op jit(solution)/shard_map/ppermute | solution.py:440
  31.1 17.1 %collective-permute-start.15 = (bf16[2,256,128]{2,1,0:T(8,128)(2,1)S(1)}, bf16[2,256,128]{2,1,0:T(8,128)(2,1)S(1)}, u32[]{:S(2)}, u32[]{:S(2)}) collective-permute-start(bf16[2,256,128]{2,1,0:T(8,128)(2,1)S(1)} %add.105), channel_id=1, source_target_pairs={{0,8},{4,12},{8,0},{12,4},{16,24},{20,28},{24,16},{28,20},{1,9},{5... | collective-permute-start | bytes 393224 | tf_op jit(solution)/shard_map/ppermute | solution.py:440
  44.1 35.2 %collective-permute-start.8 = (bf16[2,1536,128]{2,1,0:T(8,128)(2,1)S(1)}, bf16[2,1536,128]{2,1,0:T(8,128)(2,1)S(1)}, u32[]{:S(2)}, u32[]{:S(2)}) collective-permute-start(bf16[2,1536,128]{2,1,0:T(8,128)(2,1)S(1)} %join.3.rest_0_), channel_id=1, source_target_pairs={{0,2},{1,3},{2,0},{3,1},{4,6},{5,7},{6,4},{7,5},{8,10},{9,11},{10,... | collective-permute-start | bytes 2359304 | tf_op jit(solution)/shard_map/ppermute | solution.py:440
  45.7 18.7 %collective-permute-start.12 = (bf16[2,384,128]{2,1,0:T(8,128)(2,1)}, bf16[2,384,128]{2,1,0:T(8,128)(2,1)S(1)}, u32[]{:S(2)}, u32[]{:S(2)}) collective-permute-start(bf16[2,384,128]{2,1,0:T(8,128)(2,1)} %copy-done.16), channel_id=1, source_target_pairs={{0,24},{4,28},{8,16},{12,20},{16,8},{20,12},{24,0},{28,4},{1,25},{... | collective-permute-start | bytes 589832 | tf_op jit(solution)/shard_map/ppermute | solution.py:440
  48.2 14.4 %collective-permute-start.9 = (bf16[2,384,128]{2,1,0:T(8,128)(2,1)}, bf16[2,384,128]{2,1,0:T(8,128)(2,1)S(1)}, u32[]{:S(2)}, u32[]{:S(2)}) collective-permute-start(bf16[2,384,128]{2,1,0:T(8,128)(2,1)} %copy-done.17), channel_id=1, source_target_pairs={{0,16},{4,20},{8,24},{12,28},{16,0},{20,4},{24,8},{28,12},{1,17},{... | collective-permute-start | bytes 589832 | tf_op jit(solution)/shard_map/ppermute | solution.py:440
  48.3 19.9 %collective-permute-start.16 = (bf16[2,256,128]{2,1,0:T(8,128)(2,1)S(1)}, bf16[2,256,128]{2,1,0:T(8,128)(2,1)S(1)}, u32[]{:S(2)}, u32[]{:S(2)}) collective-permute-start(bf16[2,256,128]{2,1,0:T(8,128)(2,1)S(1)} %add.106), channel_id=1, source_target_pairs={{0,4},{4,0},{8,12},{12,8},{16,20},{20,16},{24,28},{28,24},{1,5},{5... | collective-permute-start | bytes 393224 | tf_op jit(solution)/shard_map/ppermute | solution.py:440
  49.8 26.7 %collective-permute-start = (bf16[2,128,512]{2,1,0:T(8,128)(2,1)}, bf16[2,128,512]{2,1,0:T(8,128)(2,1)}, u32[]{:S(2)}, u32[]{:S(2)}) collective-permute-start(bf16[2,128,512]{2,1,0:T(8,128)(2,1)} %copy-done.12), channel_id=1, source_target_pairs={{0,1},{1,2},{2,3},{3,4},{4,5},{5,6},{6,7},{7,8},{8,9},{9,10},{10,1... | collective-permute-start | bytes 786440 | tf_op jit(solution)/shard_map/ppermute | solution.py:446
  62.7 14.9 %collective-permute-start.1 = (bf16[2,128,512]{2,1,0:T(8,128)(2,1)}, bf16[2,128,512]{2,1,0:T(8,128)(2,1)S(1)}, u32[]{:S(2)}, u32[]{:S(2)}) collective-permute-start(bf16[2,128,512]{2,1,0:T(8,128)(2,1)} %copy-done.11), channel_id=1, source_target_pairs={{1,0},{2,1},{3,2},{4,3},{5,4},{6,5},{7,6},{8,7},{9,8},{10,9},{11,1... | collective-permute-start | bytes 786440 | tf_op jit(solution)/shard_map/ppermute | solution.py:447
  64.4 10.7 %copy-start.2 = (bf16[2,384,128]{2,1,0:T(8,128)(2,1)}, bf16[2,384,128]{2,1,0:T(8,128)(2,1)S(1)}, u32[]{:S(2)}) copy-start(bf16[2,384,128]{2,1,0:T(8,128)(2,1)S(1)} %collective-permute-done.12.refs_0_) | copy-start | bytes 589828
  64.4 10.7 %collective-permute-start.13 = (bf16[2,384,128]{2,1,0:T(8,128)(2,1)}, bf16[2,384,128]{2,1,0:T(8,128)(2,1)S(1)}, u32[]{:S(2)}, u32[]{:S(2)}) collective-permute-start(bf16[2,384,128]{2,1,0:T(8,128)(2,1)} %copy-done.15), channel_id=1, source_target_pairs={{0,28},{4,24},{8,20},{12,16},{16,12},{20,8},{24,4},{28,0},{1,29},{... | collective-permute-start | bytes 589832 | tf_op jit(solution)/shard_map/ppermute | solution.py:440
  68.2 11.3 %collective-permute-start.22 = (bf16[2,768,128]{2,1,0:T(8,128)(2,1)S(1)}, bf16[2,768,128]{2,1,0:T(8,128)(2,1)}, u32[]{:S(2)}, u32[]{:S(2)}) collective-permute-start(bf16[2,768,128]{2,1,0:T(8,128)(2,1)S(1)} %join.4.rest_1_), channel_id=1, source_target_pairs={{0,1},{1,0},{2,3},{3,2},{4,5},{5,4},{6,7},{7,6},{8,9},{9,8},{10,11... | collective-permute-start | bytes 1179656 | tf_op jit(solution)/shard_map/ppermute | solution.py:440
  75.1 37.9 %collective-permute-start.21 = (bf16[2,1536,128]{2,1,0:T(8,128)(2,1)S(1)}, bf16[2,1536,128]{2,1,0:T(8,128)(2,1)S(1)}, u32[]{:S(2)}, u32[]{:S(2)}) collective-permute-start(bf16[2,1536,128]{2,1,0:T(8,128)(2,1)S(1)} %join.3.rest_0_), channel_id=1, source_target_pairs={{0,1},{1,0},{2,3},{3,2},{4,5},{5,4},{6,7},{7,6},{8,9},{9,8},{10,11... | collective-permute-start | bytes 2359304 | tf_op jit(solution)/shard_map/ppermute | solution.py:440
  75.2 0.9 copy-start.3
  76.5 15.0 %collective-permute-start.17 = (bf16[2,1024,128]{2,1,0:T(8,128)(2,1)S(1)}, bf16[2,1024,128]{2,1,0:T(8,128)(2,1)}, u32[]{:S(2)}, u32[]{:S(2)}) collective-permute-start(bf16[2,1024,128]{2,1,0:T(8,128)(2,1)S(1)} %join.5.rest_2_), channel_id=1, source_target_pairs={{0,2},{1,3},{2,0},{3,1},{4,6},{5,7},{6,4},{7,5},{8,10},{9,11},{10,... | collective-permute-start | bytes 1572872 | tf_op jit(solution)/shard_map/ppermute | solution.py:440
  77.6 0.7 copy-start.13
  78.2 24.5 %collective-permute-start.11 = (bf16[2,768,128]{2,1,0:T(8,128)(2,1)S(1)}, bf16[2,768,128]{2,1,0:T(8,128)(2,1)}, u32[]{:S(2)}, u32[]{:S(2)}) collective-permute-start(bf16[2,768,128]{2,1,0:T(8,128)(2,1)S(1)} %join.4.rest_1_), channel_id=1, source_target_pairs={{0,2},{1,3},{2,0},{3,1},{4,6},{5,7},{6,4},{7,5},{8,10},{9,11},{10,... | collective-permute-start | bytes 1179656 | tf_op jit(solution)/shard_map/ppermute | solution.py:440
  79.3 46.2 %collective-permute-start.18 = (bf16[2,1536,128]{2,1,0:T(8,128)(2,1)S(1)}, bf16[2,1536,128]{2,1,0:T(8,128)(2,1)}, u32[]{:S(2)}, u32[]{:S(2)}) collective-permute-start(bf16[2,1536,128]{2,1,0:T(8,128)(2,1)S(1)} %collective-permute-done.8.rest_0_), channel_id=1, source_target_pairs={{0,1},{1,0},{2,3},{3,2},{4,5},{5,4},{6,7},{7,6},{8,9},{9,8},{10,11... | collective-permute-start | bytes 2359304 | tf_op jit(solution)/shard_map/ppermute | solution.py:440
  79.5 33.5 %collective-permute-start.23 = (bf16[2,1024,128]{2,1,0:T(8,128)(2,1)S(1)}, bf16[2,1024,128]{2,1,0:T(8,128)(2,1)}, u32[]{:S(2)}, u32[]{:S(2)}) collective-permute-start(bf16[2,1024,128]{2,1,0:T(8,128)(2,1)S(1)} %join.5.rest_2_), channel_id=1, source_target_pairs={{0,1},{1,0},{2,3},{3,2},{4,5},{5,4},{6,7},{7,6},{8,9},{9,8},{10,11... | collective-permute-start | bytes 1572872 | tf_op jit(solution)/shard_map/ppermute | solution.py:440
  80.2 23.1 %copy-start.6 = (s32[8]{0:T(128)}, s32[8]{0:T(128)S(1)}, u32[]{:S(2)}) copy-start(s32[8]{0:T(128)S(1)} %reshape.206.flags) | copy-start | bytes 100
  91.5 34.0 %collective-permute-start.20 = (bf16[2,1024,128]{2,1,0:T(8,128)(2,1)}, bf16[2,1024,128]{2,1,0:T(8,128)(2,1)S(1)}, u32[]{:S(2)}, u32[]{:S(2)}) collective-permute-start(bf16[2,1024,128]{2,1,0:T(8,128)(2,1)} %collective-permute-done.17.rest_2_), channel_id=1, source_target_pairs={{0,1},{1,0},{2,3},{3,2},{4,5},{5,4},{6,7},{7,6},{8,9},{9,8},{10,11... | collective-permute-start | bytes 1572872 | tf_op jit(solution)/shard_map/ppermute | solution.py:440
  91.5 1.0 copy-start.10
  92.4 0.9 copy-start.14
  102.7 10.3 %copy-start.5 = (s32[4]{0:T(128)S(1)}, s32[4]{0:T(128)}, u32[]{:S(2)}) copy-start(s32[4]{0:T(128)} %copy-done.4) | copy-start | bytes 52
  102.7 22.8 %collective-permute-start.19 = (bf16[2,768,128]{2,1,0:T(8,128)(2,1)}, bf16[2,768,128]{2,1,0:T(8,128)(2,1)}, u32[]{:S(2)}, u32[]{:S(2)}) collective-permute-start(bf16[2,768,128]{2,1,0:T(8,128)(2,1)} %collective-permute-done.11.rest_1_), channel_id=1, source_target_pairs={{0,1},{1,0},{2,3},{3,2},{4,5},{5,4},{6,7},{7,6},{8,9},{9,8},{10,11... | collective-permute-start | bytes 1179656 | tf_op jit(solution)/shard_map/ppermute | solution.py:440

commit v4 on v3

--- a/solution.py
+++ b/solution.py
@@ -165,7 +165,7 @@
 
 
 SCALE = math.log2(math.e) / math.sqrt(HEAD_DIM)
-JOINED = 2
+JOINED = 4
 TOGETHER = 2
 
 
@@ -462,7 +462,12 @@
         common = common + across(common, "seq", bit)
         bit //= 2
     half, last_part = seq_count // 2, (seq_count + seq_count // 2) // 2
-    own = [join(chunks[:half]), join(chunks[half:last_part]), join(chunks[last_part:] + [common])]
+    own = [
+        chunks[0],
+        join(chunks[1:half]),
+        join(chunks[half:last_part]),
+        join(chunks[last_part:] + [common]),
+    ]
     groups = {0: own}
     bit = heads // 2
     while bit:

time: 139 us -> 153 us (1.10)
  the two profiles are of different devices: /device:TPU:0 before, /device:TPU:25 now
where the time goes in v4:
time: 153 us; the launch traced here: 152 us
  waiting for transfers between devices  50.9 us (33%)
  Pallas kernels  49.4 us (32%)
  starting transfers between devices  34.8 us (23%)
  local copies, waits for them, and re-layouts  11.9 us (8%)
  other arithmetic  4.69 us (3%)
    ppermute x25, waiting for transfers between devices, across(): return lax.ppermute(array, axis, [(i, i ^ bit) for i in range(count)])  50.9 us
    ppermute x25, starting transfers between devices, across(): return lax.ppermute(array, axis, [(i, i ^ bit) for i in range(count)])  28.4 us
    pallas_call x2, Pallas kernels, finish(): pl.pallas_call(functools.partial(finish_kernel, begin, [len(part) for par...  25.8 us
    pallas_call x2, Pallas kernels, window_share(): pl.pallas_call(functools.partial(window_kernel, parts), grid_spec=pltpu.P...  17.7 us
    unnamed x35, local copies, waits for them, and re-layouts  8.14 us
    ppermute x1, starting transfers between devices, on_device(): lax.ppermute(first, ('seq', 'head'), [(i + 1, i) for i in range(flat - 1)])  3.23 us
    ppermute x1, starting transfers between devices, on_device(): lax.ppermute(last, ('seq', 'head'), [(i, i + 1) for i in range(flat - 1)])  3.14 us
  transfers between devices with their start and end apart: 27, of which 8 were waited for; matrix products, arithmetic and copies ran while one was open for 6% of the time, Pallas kernels for 22%

profile of v4, /device:TPU:25, one launch (start us, length us, event | category | flops | bytes accessed | tf_op | source)
XLA Modules:
  0.0 152.2 jit_solution(15088419825121046334)
XLA Ops:
  0.0 1.0 copy-done
  1.0 1.0 copy-done.1
  2.1 2.4 %pack.1 = (bf16[2,512,128]{2,1,0:T(8,128)(2,1)S(1)}, bf16[2,512,128]{2,1,0:T(8,128)(2,1)S(1)}, bf16[2,512,128]{2,1,0:T(8,128)(2,1)S(1)}, bf16[2,512,128]{2,1,0:T...) custom-call(s32[4]{0:T(128)S(1)} %iota_xor_fusion.order, bf16[512,512]{1,0:T(8,128)(2,1)S(1)} %copy-done, ...), custom_call_target="tpu_custom_call" | custom-call | tf_op jit(solution)/shard_map/pack/pallas_call | solution.py:72
  4.5 0.7 collective-permute-start.2
  5.2 1.2 collective-permute-start.3
  6.4 0.5 collective-permute-start.4
  6.9 3.1 %collective-permute-start = (bf16[2,128,512]{2,1,0:T(8,128)(2,1)S(1)}, bf16[2,128,512]{2,1,0:T(8,128)(2,1)S(1)}, u32[]{:S(2)}, u32[]{:S(2)}) collective-permute-start(bf16[2,128,512]{2,1,0:T(8,128)(2,1)S(1)} %get-tuple-element.26), channel_id=1, source_target_pairs={{0,1},{1,2},{2,3},{3,4},{4,5},{5,6},{6,7},{7,8},{8,9},{9,10},{10,1... | collective-permute-start | bytes 786440 | tf_op jit(solution)/shard_map/ppermute | solution.py:446
  10.1 0.7 fusion.10
  10.8 0.7 fusion.9
  11.5 0.8 reshape.202
  12.4 0.2 fusion
  12.7 0.2 convert_reduce_fusion
  12.9 0.1 select_reduce_fusion
  13.2 0.6 gather_fusion.1
  14.3 5.1 %collective-permute-done.4.rest_3_ = bf16[2,512,128]{2,1,0:T(8,128)(2,1)S(1)} collective-permute-done((bf16[2,512,128]{2,1,0:T(8,128)(2,1)S(1)}, bf16[2,512,128]{2,1,0:T(8,128)(2,1)S(1)}, u32[]{:S(2)}, u32[]{:S(2)}) %collective-permute-start.4) | collective-permute-done | bytes 262176 | tf_op jit(solution)/shard_map/ppermute | solution.py:440
  19.4 2.5 %pick.1 = (bf16[2,384,128]{2,1,0:T(8,128)(2,1)S(1)}, bf16[2,384,128]{2,1,0:T(8,128)(2,1)S(1)}, bf16[2,384,128]{2,1,0:T(8,128)(2,1)}, bf16[2,384,128]{2,1,0:T(8,1...) custom-call(s32[4]{0:T(128)S(1)} %iota_xor_fusion.order, ...), custom_call_target="tpu_custom_call" | custom-call | tf_op jit(solution)/shard_map/pick/pallas_call | solution.py:125
  21.9 0.1 collective-permute-start.15
  22.1 0.2 and_reduce_fusion
  22.3 2.4 %collective-permute-start.10 = (bf16[2,384,128]{2,1,0:T(8,128)(2,1)S(1)}, bf16[2,384,128]{2,1,0:T(8,128)(2,1)S(1)}, u32[]{:S(2)}, u32[]{:S(2)}) collective-permute-start(bf16[2,384,128]{2,1,0:T(8,128)(2,1)S(1)} %get-tuple-element.36), channel_id=1, source_target_pairs={{0,16},{4,20},{8,24},{12,28},{16,0},{20,4},{24,8},{28,12},{1,17},{... | collective-permute-start | bytes 589832 | tf_op jit(solution)/shard_map/ppermute | solution.py:440
  24.7 10.6 %collective-permute-done.15 = bf16[2,256,128]{2,1,0:T(8,128)(2,1)S(1)} collective-permute-done((bf16[2,256,128]{2,1,0:T(8,128)(2,1)S(1)}, bf16[2,256,128]{2,1,0:T(8,128)(2,1)S(1)}, u32[]{:S(2)}, u32[]{:S(2)}) %collective-permute-start.15) | collective-permute-done | bytes 131104 | tf_op jit(solution)/shard_map/ppermute | solution.py:440
  35.7 0.3 convert_reduce_fusion.1
  36.2 3.7 %collective-permute-start.11 = (bf16[2,384,128]{2,1,0:T(8,128)(2,1)S(1)}, bf16[2,384,128]{2,1,0:T(8,128)(2,1)S(1)}, u32[]{:S(2)}, u32[]{:S(2)}) collective-permute-start(bf16[2,384,128]{2,1,0:T(8,128)(2,1)S(1)} %get-tuple-element.37), channel_id=1, source_target_pairs={{0,20},{4,16},{8,28},{12,24},{16,4},{20,0},{24,12},{28,8},{1,21},{... | collective-permute-start | bytes 589832 | tf_op jit(solution)/shard_map/ppermute | solution.py:440
  39.8 0.1 collective-permute-start.6
  40.0 1.4 collective-permute-start.7
  41.4 0.9 collective-permute-done.16
  42.3 3.2 %collective-permute-start.8 = (bf16[2,384,128]{2,1,0:T(8,128)(2,1)S(1)}, bf16[2,384,128]{2,1,0:T(8,128)(2,1)S(1)}, u32[]{:S(2)}, u32[]{:S(2)}) collective-permute-start(bf16[2,384,128]{2,1,0:T(8,128)(2,1)S(1)} %get-tuple-element.35), channel_id=1, source_target_pairs={{0,12},{4,8},{8,4},{12,0},{16,28},{20,24},{24,20},{28,16},{1,13},{... | collective-permute-start | bytes 589832 | tf_op jit(solution)/shard_map/ppermute | solution.py:440
  45.5 0.1 fusion.4
  45.6 5.8 %collective-permute-done.11.refs_1_ = bf16[2,384,128]{2,1,0:T(8,128)(2,1)S(1)} collective-permute-done((bf16[2,384,128]{2,1,0:T(8,128)(2,1)S(1)}, bf16[2,384,128]{2,1,0:T(8,128)(2,1)S(1)}, u32[]{:S(2)}, u32[]{:S(2)}) %collective-permute-start.11) | collective-permute-done | bytes 196640 | tf_op jit(solution)/shard_map/ppermute | solution.py:440
  51.4 0.5 collective-permute-start.13
  52.0 3.0 %collective-permute-start.14 = (bf16[2,384,128]{2,1,0:T(8,128)(2,1)}, bf16[2,384,128]{2,1,0:T(8,128)(2,1)S(1)}, u32[]{:S(2)}, u32[]{:S(2)}) collective-permute-start(bf16[2,384,128]{2,1,0:T(8,128)(2,1)} %get-tuple-element.39), channel_id=1, source_target_pairs={{0,28},{4,24},{8,20},{12,16},{16,12},{20,8},{24,4},{28,0},{1,29},{... | collective-permute-start | bytes 589832 | tf_op jit(solution)/shard_map/ppermute | solution.py:440
  55.0 0.9 collective-permute-start.17
  55.9 10.5 %collective-permute-done.8.refs_2_ = bf16[2,384,128]{2,1,0:T(8,128)(2,1)S(1)} collective-permute-done((bf16[2,384,128]{2,1,0:T(8,128)(2,1)S(1)}, bf16[2,384,128]{2,1,0:T(8,128)(2,1)S(1)}, u32[]{:S(2)}, u32[]{:S(2)}) %collective-permute-start.8) | collective-permute-done | bytes 196640 | tf_op jit(solution)/shard_map/ppermute | solution.py:440
  66.4 3.2 %collective-permute-start.1 = (bf16[2,128,512]{2,1,0:T(8,128)(2,1)}, bf16[2,128,512]{2,1,0:T(8,128)(2,1)}, u32[]{:S(2)}, u32[]{:S(2)}) collective-permute-start(bf16[2,128,512]{2,1,0:T(8,128)(2,1)} %get-tuple-element.27), channel_id=1, source_target_pairs={{1,0},{2,1},{3,2},{4,3},{5,4},{6,5},{7,6},{8,7},{9,8},{10,9},{11,1... | collective-permute-start | bytes 786440 | tf_op jit(solution)/shard_map/ppermute | solution.py:447
  69.6 0.6 gather_fusion
  70.3 0.3 join.4.rest_2_
  70.5 0.4 join.3.rest_1_
  71.0 0.7 copy-done.15
  71.7 0.7 collective-permute-start.5
  72.4 0.3 collective-permute-start.25
  72.7 1.3 collective-permute-start.9
  74.0 0.9 add.107.refs_2_
  75.0 0.4 join.5.rest_3_
  75.4 0.3 collective-permute-start.18
  75.7 0.7 copy-done.6
  76.3 0.8 collective-permute-start.24
  77.1 0.9 collective-permute-done.5.rest_0_
  78.0 0.9 collective-permute-start.12
  79.1 0.7 copy-done.2
  79.8 1.6 %collective-permute-start.26 = (bf16[2,1024,128]{2,1,0:T(8,128)(2,1)S(1)}, bf16[2,1024,128]{2,1,0:T(8,128)(2,1)}, u32[]{:S(2)}, u32[]{:S(2)}) collective-permute-start(bf16[2,1024,128]{2,1,0:T(8,128)(2,1)S(1)} %join.5.rest_3_), channel_id=1, source_target_pairs={{0,1},{1,0},{2,3},{3,2},{4,5},{5,4},{6,7},{7,6},{8,9},{9,8},{10,11... | collective-permute-start | bytes 1572872 | tf_op jit(solution)/shard_map/ppermute | solution.py:440
  81.4 9.2 %collective-permute-done.9.rest_1_ = bf16[2,1152,128]{2,1,0:T(8,128)(2,1)S(1)} collective-permute-done((bf16[2,1152,128]{2,1,0:T(8,128)(2,1)S(1)}, bf16[2,1152,128]{2,1,0:T(8,128)(2,1)S(1)}, u32[]{:S(2)}, u32[]{:S(2)}) %collective-permute-start.9) | collective-permute-done | bytes 589856 | tf_op jit(solution)/shard_map/ppermute | solution.py:440
  90.6 2.0 %collective-permute-start.20 = (bf16[2,1152,128]{2,1,0:T(8,128)(2,1)S(1)}, bf16[2,1152,128]{2,1,0:T(8,128)(2,1)S(1)}, u32[]{:S(2)}, u32[]{:S(2)}) collective-permute-start(bf16[2,1152,128]{2,1,0:T(8,128)(2,1)S(1)} %collective-permute-done.9.rest_1_), channel_id=1, source_target_pairs={{0,1},{1,0},{2,3},{3,2},{4,5},{5,4},{6,7},{7,6},{8,9},{9,8},{10,11... | collective-permute-start | bytes 1769480 | tf_op jit(solution)/shard_map/ppermute | solution.py:440
  92.6 0.6 add_convert_fusion
  93.4 0.7 reshape.206.flags
  94.1 7.8 %collective-permute-done.18.rest_3_ = bf16[2,1024,128]{2,1,0:T(8,128)(2,1)} collective-permute-done((bf16[2,1024,128]{2,1,0:T(8,128)(2,1)S(1)}, bf16[2,1024,128]{2,1,0:T(8,128)(2,1)}, u32[]{:S(2)}, u32[]{:S(2)}) %collective-permute-start.18) | collective-permute-done | bytes 524320 | tf_op jit(solution)/shard_map/ppermute | solution.py:440
  101.9 2.0 %collective-permute-start.22 = (bf16[2,1024,128]{2,1,0:T(8,128)(2,1)}, bf16[2,1024,128]{2,1,0:T(8,128)(2,1)S(1)}, u32[]{:S(2)}, u32[]{:S(2)}) collective-permute-start(bf16[2,1024,128]{2,1,0:T(8,128)(2,1)} %collective-permute-done.18.rest_3_), channel_id=1, source_target_pairs={{0,1},{1,0},{2,3},{3,2},{4,5},{5,4},{6,7},{7,6},{8,9},{9,8},{10,11... | collective-permute-start | bytes 1572872 | tf_op jit(solution)/shard_map/ppermute | solution.py:440
  104.0 0.9 copy-done.14
  104.9 0.9 copy-done.16
  105.9 8.6 %window.3 = (f32[2,512,1024]{2,1,0:T(8,128)}, f32[2,512,1024]{2,1,0:T(8,128)}) custom-call(s32[4]{0:T(128)S(1)} %iota_xor_fusion.order, s32[8]{0:T(128)S(1)} %reshape.206.flags, bf16[512,4096]{1,0:T(8,128)(2,1)} %query_ref.7, bf16[2,512,128]{2,1,0:T(8,128)(2,1)S(1)} %get-tuple-element.30.rest_0_, bf16[2,512,128]{2,1,0:T(8,128)(2,1)S(1)} %copy-done.14, ...), custom_call_target="tpu_custom_call" | custom-call | flops 1610612736 | bytes 8388608 | tf_op jit(solution)/shard_map/window/pallas_call | solution.py:270
  114.6 9.1 %window.2 = (f32[2,512,1024]{2,1,0:T(8,128)}, f32[2,512,1024]{2,1,0:T(8,128)}) custom-call(s32[4]{0:T(128)} %copy-done.8, s32[8]{0:T(128)} %copy-done.10, bf16[512,4096]{1,0:T(8,128)(2,1)} %query_ref.7, bf16[2,512,128]{2,1,0:T(8,128)(2,1)} %copy-done.11, bf16[2,512,128]{2,1,0:T(8,128)(2,1)} %copy-done.12, bf16[2,128,512]{2,1,0:T(8,128)(2,1)} %copy-done.15, ...), custom_call_target="tpu_custom_call" | custom-call | flops 1610612736 | bytes 8388608 | tf_op jit(solution)/shard_map/window/pallas_call | solution.py:270
  123.7 0.5 collective-permute-start.19
  124.3 1.0 copy-done.3
  125.3 0.9 copy-done.7
  126.2 12.6 %finish.2.rest_8_ = bf16[512,4096]{1,0:T(8,128)(2,1)} custom-call(s32[4]{0:T(128)S(1)} %copy-done.9, s32[80]{0:T(128)S(1)} %reshape.204.table, bf16[512,4096]{1,0:T(8,128)(2,1)} %query_ref.7, f32[2,512,1024]{2,1,0:T(8,128)} %get-tuple-element.41.mixed_ref, f32[2,512,1024]{2,1,0:T(8,128)} %get-tuple-element.42.level_ref, bf16[2,384,128]{2,1,0:T(8,128)(2,1)S(1)} %copy-done.5, ...), custom_call_target="tpu_custom_call" | custom-call | flops 2684354560 | bytes 8388608 | tf_op jit(solution)/shard_map/finish/pallas_call | solution.py:374
  138.8 13.2 %finish.3 = bf16[512,4096]{1,0:T(8,128)(2,1)} custom-call(s32[4]{0:T(128)S(1)} %copy-done.9, s32[80]{0:T(128)S(1)} %reshape.204.table, bf16[512,4096]{1,0:T(8,128)(2,1)} %query_ref.7, f32[2,512,1024]{2,1,0:T(8,128)} %get-tuple-element.28.mixed_ref, f32[2,512,1024]{2,1,0:T(8,128)} %get-tuple-element.29.level_ref, ...), custom_call_target="tpu_custom_call", output_to_operand_aliasing={{}: (13, {})} | custom-call | flops 2684354560 | bytes 8388608 | tf_op jit(solution)/shard_map/finish/pallas_call | solution.py:374
  (84 shorter events, 1.9 us)
Async XLA Ops:
  0.0 1.0 copy-start
  1.0 1.0 copy-start.1
  2.1 112.4 %copy-start.8 = (s32[4]{0:T(128)}, s32[4]{0:T(128)S(1)}, u32[]{:S(2)}) copy-start(s32[4]{0:T(128)S(1)} %iota_xor_fusion.order) | copy-start | bytes 52
  4.5 15.0 %copy-start.11 = (bf16[2,512,128]{2,1,0:T(8,128)(2,1)}, bf16[2,512,128]{2,1,0:T(8,128)(2,1)S(1)}, u32[]{:S(2)}) copy-start(bf16[2,512,128]{2,1,0:T(8,128)(2,1)S(1)} %get-tuple-element.24.rest_0_) | copy-start | bytes 786436
  4.5 15.0 %copy-start.12 = (bf16[2,512,128]{2,1,0:T(8,128)(2,1)}, bf16[2,512,128]{2,1,0:T(8,128)(2,1)S(1)}, u32[]{:S(2)}) copy-start(bf16[2,512,128]{2,1,0:T(8,128)(2,1)S(1)} %get-tuple-element.25.rest_1_) | copy-start | bytes 786436
  4.5 65.7 %copy-start.13 = (bf16[2,512,128]{2,1,0:T(8,128)(2,1)}, bf16[2,512,128]{2,1,0:T(8,128)(2,1)S(1)}, u32[]{:S(2)}) copy-start(bf16[2,512,128]{2,1,0:T(8,128)(2,1)S(1)} %get-tuple-element.31.rest_1_) | copy-start | bytes 786436
  4.5 9.8 %collective-permute-start.2 = (bf16[2,512,128]{2,1,0:T(8,128)(2,1)S(1)}, bf16[2,512,128]{2,1,0:T(8,128)(2,1)S(1)}, u32[]{:S(2)}, u32[]{:S(2)}) collective-permute-start(bf16[2,512,128]{2,1,0:T(8,128)(2,1)S(1)} %get-tuple-element.31.rest_1_), channel_id=1, source_target_pairs={{0,1},{1,0},{2,3},{3,2},{4,5},{5,4},{6,7},{7,6},{8,9},{9,8},{10,11... | collective-permute-start | bytes 786440 | tf_op jit(solution)/shard_map/ppermute | solution.py:440
  5.2 9.0 %collective-permute-start.3 = (bf16[2,512,128]{2,1,0:T(8,128)(2,1)S(1)}, bf16[2,512,128]{2,1,0:T(8,128)(2,1)S(1)}, u32[]{:S(2)}, u32[]{:S(2)}) collective-permute-start(bf16[2,512,128]{2,1,0:T(8,128)(2,1)S(1)} %get-tuple-element.24.rest_0_), channel_id=1, source_target_pairs={{0,2},{1,3},{2,0},{3,1},{4,6},{5,7},{6,4},{7,5},{8,10},{9,11},{10,... | collective-permute-start | bytes 786440 | tf_op jit(solution)/shard_map/ppermute | solution.py:440
  6.4 13.0 %collective-permute-start.4 = (bf16[2,512,128]{2,1,0:T(8,128)(2,1)S(1)}, bf16[2,512,128]{2,1,0:T(8,128)(2,1)S(1)}, u32[]{:S(2)}, u32[]{:S(2)}) collective-permute-start(bf16[2,512,128]{2,1,0:T(8,128)(2,1)S(1)} %get-tuple-element.25.rest_1_), channel_id=1, source_target_pairs={{0,3},{1,2},{2,1},{3,0},{4,7},{5,6},{6,5},{7,4},{8,11},{9,10},{10,... | collective-permute-start | bytes 786440 | tf_op jit(solution)/shard_map/ppermute | solution.py:440
  6.9 64.0 %collective-permute-start = (bf16[2,128,512]{2,1,0:T(8,128)(2,1)S(1)}, bf16[2,128,512]{2,1,0:T(8,128)(2,1)S(1)}, u32[]{:S(2)}, u32[]{:S(2)}) collective-permute-start(bf16[2,128,512]{2,1,0:T(8,128)(2,1)S(1)} %get-tuple-element.26), channel_id=1, source_target_pairs={{0,1},{1,2},{2,3},{3,4},{4,5},{5,6},{6,7},{7,8},{8,9},{9,10},{10,1... | collective-permute-start | bytes 786440 | tf_op jit(solution)/shard_map/ppermute | solution.py:446
  21.9 59.5 %copy-start.4 = (bf16[2,384,128]{2,1,0:T(8,128)(2,1)}, bf16[2,384,128]{2,1,0:T(8,128)(2,1)S(1)}, u32[]{:S(2)}) copy-start(bf16[2,384,128]{2,1,0:T(8,128)(2,1)S(1)} %get-tuple-element.32.rest_0_) | copy-start | bytes 589828
  21.9 13.4 %collective-permute-start.15 = (bf16[2,256,128]{2,1,0:T(8,128)(2,1)S(1)}, bf16[2,256,128]{2,1,0:T(8,128)(2,1)S(1)}, u32[]{:S(2)}, u32[]{:S(2)}) collective-permute-start(bf16[2,256,128]{2,1,0:T(8,128)(2,1)S(1)} %get-tuple-element.40), channel_id=1, source_target_pairs={{0,16},{4,20},{8,24},{12,28},{16,0},{20,4},{24,8},{28,12},{1,17},{... | collective-permute-start | bytes 393224 | tf_op jit(solution)/shard_map/ppermute | solution.py:440
  22.3 17.7 %collective-permute-start.10 = (bf16[2,384,128]{2,1,0:T(8,128)(2,1)S(1)}, bf16[2,384,128]{2,1,0:T(8,128)(2,1)S(1)}, u32[]{:S(2)}, u32[]{:S(2)}) collective-permute-start(bf16[2,384,128]{2,1,0:T(8,128)(2,1)S(1)} %get-tuple-element.36), channel_id=1, source_target_pairs={{0,16},{4,20},{8,24},{12,28},{16,0},{20,4},{24,8},{28,12},{1,17},{... | collective-permute-start | bytes 589832 | tf_op jit(solution)/shard_map/ppermute | solution.py:440
  35.4 6.9 %collective-permute-start.16 = (bf16[2,256,128]{2,1,0:T(8,128)(2,1)S(1)}, bf16[2,256,128]{2,1,0:T(8,128)(2,1)S(1)}, u32[]{:S(2)}, u32[]{:S(2)}) collective-permute-start(bf16[2,256,128]{2,1,0:T(8,128)(2,1)S(1)} %add.105), channel_id=1, source_target_pairs={{0,8},{4,12},{8,0},{12,4},{16,24},{20,28},{24,16},{28,20},{1,9},{5... | collective-permute-start | bytes 393224 | tf_op jit(solution)/shard_map/ppermute | solution.py:440
  36.2 15.3 %collective-permute-start.11 = (bf16[2,384,128]{2,1,0:T(8,128)(2,1)S(1)}, bf16[2,384,128]{2,1,0:T(8,128)(2,1)S(1)}, u32[]{:S(2)}, u32[]{:S(2)}) collective-permute-start(bf16[2,384,128]{2,1,0:T(8,128)(2,1)S(1)} %get-tuple-element.37), channel_id=1, source_target_pairs={{0,20},{4,16},{8,28},{12,24},{16,4},{20,0},{24,12},{28,8},{1,21},{... | collective-permute-start | bytes 589832 | tf_op jit(solution)/shard_map/ppermute | solution.py:440
  39.8 12.1 %collective-permute-start.6 = (bf16[2,384,128]{2,1,0:T(8,128)(2,1)S(1)}, bf16[2,384,128]{2,1,0:T(8,128)(2,1)S(1)}, u32[]{:S(2)}, u32[]{:S(2)}) collective-permute-start(bf16[2,384,128]{2,1,0:T(8,128)(2,1)S(1)} %get-tuple-element.33), channel_id=1, source_target_pairs={{0,4},{4,0},{8,12},{12,8},{16,20},{20,16},{24,28},{28,24},{1,5},{5... | collective-permute-start | bytes 589832 | tf_op jit(solution)/shard_map/ppermute | solution.py:440
  40.0 15.0 %collective-permute-start.7 = (bf16[2,384,128]{2,1,0:T(8,128)(2,1)}, bf16[2,384,128]{2,1,0:T(8,128)(2,1)S(1)}, u32[]{:S(2)}, u32[]{:S(2)}) collective-permute-start(bf16[2,384,128]{2,1,0:T(8,128)(2,1)} %get-tuple-element.34), channel_id=1, source_target_pairs={{0,8},{4,12},{8,0},{12,4},{16,24},{20,28},{24,16},{28,20},{1,9},{5... | collective-permute-start | bytes 589832 | tf_op jit(solution)/shard_map/ppermute | solution.py:440
  42.3 24.1 %collective-permute-start.8 = (bf16[2,384,128]{2,1,0:T(8,128)(2,1)S(1)}, bf16[2,384,128]{2,1,0:T(8,128)(2,1)S(1)}, u32[]{:S(2)}, u32[]{:S(2)}) collective-permute-start(bf16[2,384,128]{2,1,0:T(8,128)(2,1)S(1)} %get-tuple-element.35), channel_id=1, source_target_pairs={{0,12},{4,8},{8,4},{12,0},{16,28},{20,24},{24,20},{28,16},{1,13},{... | collective-permute-start | bytes 589832 | tf_op jit(solution)/shard_map/ppermute | solution.py:440
  51.4 20.3 %collective-permute-start.13 = (bf16[2,384,128]{2,1,0:T(8,128)(2,1)}, bf16[2,384,128]{2,1,0:T(8,128)(2,1)S(1)}, u32[]{:S(2)}, u32[]{:S(2)}) collective-permute-start(bf16[2,384,128]{2,1,0:T(8,128)(2,1)} %get-tuple-element.38), channel_id=1, source_target_pairs={{0,24},{4,28},{8,16},{12,20},{16,8},{20,12},{24,0},{28,4},{1,25},{... | collective-permute-start | bytes 589832 | tf_op jit(solution)/shard_map/ppermute | solution.py:440
  52.0 20.5 %collective-permute-start.14 = (bf16[2,384,128]{2,1,0:T(8,128)(2,1)}, bf16[2,384,128]{2,1,0:T(8,128)(2,1)S(1)}, u32[]{:S(2)}, u32[]{:S(2)}) collective-permute-start(bf16[2,384,128]{2,1,0:T(8,128)(2,1)} %get-tuple-element.39), channel_id=1, source_target_pairs={{0,28},{4,24},{8,20},{12,16},{16,12},{20,8},{24,4},{28,0},{1,29},{... | collective-permute-start | bytes 589832 | tf_op jit(solution)/shard_map/ppermute | solution.py:440
  55.0 17.7 %collective-permute-start.17 = (bf16[2,256,128]{2,1,0:T(8,128)(2,1)S(1)}, bf16[2,256,128]{2,1,0:T(8,128)(2,1)}, u32[]{:S(2)}, u32[]{:S(2)}) collective-permute-start(bf16[2,256,128]{2,1,0:T(8,128)(2,1)S(1)} %add.106), channel_id=1, source_target_pairs={{0,4},{4,0},{8,12},{12,8},{16,20},{20,16},{24,28},{28,24},{1,5},{5... | collective-permute-start | bytes 393224 | tf_op jit(solution)/shard_map/ppermute | solution.py:440
  66.4 9.0 %collective-permute-start.1 = (bf16[2,128,512]{2,1,0:T(8,128)(2,1)}, bf16[2,128,512]{2,1,0:T(8,128)(2,1)}, u32[]{:S(2)}, u32[]{:S(2)}) collective-permute-start(bf16[2,128,512]{2,1,0:T(8,128)(2,1)} %get-tuple-element.27), channel_id=1, source_target_pairs={{1,0},{2,1},{3,2},{4,3},{5,4},{6,5},{7,6},{8,7},{9,8},{10,9},{11,1... | collective-permute-start | bytes 786440 | tf_op jit(solution)/shard_map/ppermute | solution.py:447
  71.0 0.7 copy-start.15
  71.7 4.0 %collective-permute-start.23 = (bf16[2,384,128]{2,1,0:T(8,128)(2,1)S(1)}, bf16[2,384,128]{2,1,0:T(8,128)(2,1)S(1)}, u32[]{:S(2)}, u32[]{:S(2)}) collective-permute-start(bf16[2,384,128]{2,1,0:T(8,128)(2,1)S(1)} %get-tuple-element.32.rest_0_), channel_id=1, source_target_pairs={{0,1},{1,0},{2,3},{3,2},{4,5},{5,4},{6,7},{7,6},{8,9},{9,8},{10,11... | collective-permute-start | bytes 589832 | tf_op jit(solution)/shard_map/ppermute | solution.py:440
  71.7 6.3 %collective-permute-start.5 = (bf16[2,384,128]{2,1,0:T(8,128)(2,1)S(1)}, bf16[2,384,128]{2,1,0:T(8,128)(2,1)}, u32[]{:S(2)}, u32[]{:S(2)}) collective-permute-start(bf16[2,384,128]{2,1,0:T(8,128)(2,1)S(1)} %get-tuple-element.32.rest_0_), channel_id=1, source_target_pairs={{0,2},{1,3},{2,0},{3,1},{4,6},{5,7},{6,4},{7,5},{8,10},{9,11},{10,... | collective-permute-start | bytes 589832 | tf_op jit(solution)/shard_map/ppermute | solution.py:440
  72.4 6.6 %collective-permute-start.25 = (bf16[2,768,128]{2,1,0:T(8,128)(2,1)S(1)}, bf16[2,768,128]{2,1,0:T(8,128)(2,1)S(1)}, u32[]{:S(2)}, u32[]{:S(2)}) collective-permute-start(bf16[2,768,128]{2,1,0:T(8,128)(2,1)S(1)} %join.4.rest_2_), channel_id=1, source_target_pairs={{0,1},{1,0},{2,3},{3,2},{4,5},{5,4},{6,7},{7,6},{8,9},{9,8},{10,11... | collective-permute-start | bytes 1179656 | tf_op jit(solution)/shard_map/ppermute | solution.py:440
  72.7 17.9 %collective-permute-start.9 = (bf16[2,1152,128]{2,1,0:T(8,128)(2,1)S(1)}, bf16[2,1152,128]{2,1,0:T(8,128)(2,1)S(1)}, u32[]{:S(2)}, u32[]{:S(2)}) collective-permute-start(bf16[2,1152,128]{2,1,0:T(8,128)(2,1)S(1)} %join.3.rest_1_), channel_id=1, source_target_pairs={{0,2},{1,3},{2,0},{3,1},{4,6},{5,7},{6,4},{7,5},{8,10},{9,11},{10,... | collective-permute-start | bytes 1769480 | tf_op jit(solution)/shard_map/ppermute | solution.py:440
  75.4 26.5 %collective-permute-start.18 = (bf16[2,1024,128]{2,1,0:T(8,128)(2,1)S(1)}, bf16[2,1024,128]{2,1,0:T(8,128)(2,1)}, u32[]{:S(2)}, u32[]{:S(2)}) collective-permute-start(bf16[2,1024,128]{2,1,0:T(8,128)(2,1)S(1)} %join.5.rest_3_), channel_id=1, source_target_pairs={{0,2},{1,3},{2,0},{3,1},{4,6},{5,7},{6,4},{7,5},{8,10},{9,11},{10,... | collective-permute-start | bytes 1572872 | tf_op jit(solution)/shard_map/ppermute | solution.py:440
  75.7 0.7 copy-start.6
  76.3 47.4 %collective-permute-start.24 = (bf16[2,1152,128]{2,1,0:T(8,128)(2,1)S(1)}, bf16[2,1152,128]{2,1,0:T(8,128)(2,1)S(1)}, u32[]{:S(2)}, u32[]{:S(2)}) collective-permute-start(bf16[2,1152,128]{2,1,0:T(8,128)(2,1)S(1)} %join.3.rest_1_), channel_id=1, source_target_pairs={{0,1},{1,0},{2,3},{3,2},{4,5},{5,4},{6,7},{7,6},{8,9},{9,8},{10,11... | collective-permute-start | bytes 1769480 | tf_op jit(solution)/shard_map/ppermute | solution.py:440
  78.0 36.4 %collective-permute-start.12 = (bf16[2,768,128]{2,1,0:T(8,128)(2,1)S(1)}, bf16[2,768,128]{2,1,0:T(8,128)(2,1)}, u32[]{:S(2)}, u32[]{:S(2)}) collective-permute-start(bf16[2,768,128]{2,1,0:T(8,128)(2,1)S(1)} %join.4.rest_2_), channel_id=1, source_target_pairs={{0,2},{1,3},{2,0},{3,1},{4,6},{5,7},{6,4},{7,5},{8,10},{9,11},{10,... | collective-permute-start | bytes 1179656 | tf_op jit(solution)/shard_map/ppermute | solution.py:440
  79.0 0.7 copy-start.2
  79.8 44.5 %collective-permute-start.26 = (bf16[2,1024,128]{2,1,0:T(8,128)(2,1)S(1)}, bf16[2,1024,128]{2,1,0:T(8,128)(2,1)}, u32[]{:S(2)}, u32[]{:S(2)}) collective-permute-start(bf16[2,1024,128]{2,1,0:T(8,128)(2,1)S(1)} %join.5.rest_3_), channel_id=1, source_target_pairs={{0,1},{1,0},{2,3},{3,2},{4,5},{5,4},{6,7},{7,6},{8,9},{9,8},{10,11... | collective-permute-start | bytes 1572872 | tf_op jit(solution)/shard_map/ppermute | solution.py:440
  90.6 48.2 %collective-permute-start.20 = (bf16[2,1152,128]{2,1,0:T(8,128)(2,1)S(1)}, bf16[2,1152,128]{2,1,0:T(8,128)(2,1)S(1)}, u32[]{:S(2)}, u32[]{:S(2)}) collective-permute-start(bf16[2,1152,128]{2,1,0:T(8,128)(2,1)S(1)} %collective-permute-done.9.rest_1_), channel_id=1, source_target_pairs={{0,1},{1,0},{2,3},{3,2},{4,5},{5,4},{6,7},{7,6},{8,9},{9,8},{10,11... | collective-permute-start | bytes 1769480 | tf_op jit(solution)/shard_map/ppermute | solution.py:440
  94.1 20.5 %copy-start.10 = (s32[8]{0:T(128)}, s32[8]{0:T(128)S(1)}, u32[]{:S(2)}) copy-start(s32[8]{0:T(128)S(1)} %reshape.206.flags) | copy-start | bytes 100
  101.9 36.9 %collective-permute-start.22 = (bf16[2,1024,128]{2,1,0:T(8,128)(2,1)}, bf16[2,1024,128]{2,1,0:T(8,128)(2,1)S(1)}, u32[]{:S(2)}, u32[]{:S(2)}) collective-permute-start(bf16[2,1024,128]{2,1,0:T(8,128)(2,1)} %collective-permute-done.18.rest_3_), channel_id=1, source_target_pairs={{0,1},{1,0},{2,3},{3,2},{4,5},{5,4},{6,7},{7,6},{8,9},{9,8},{10,11... | collective-permute-start | bytes 1572872 | tf_op jit(solution)/shard_map/ppermute | solution.py:440
  104.0 0.9 copy-start.14
  104.9 0.9 copy-start.16
  114.5 9.8 %copy-start.5 = (bf16[2,384,128]{2,1,0:T(8,128)(2,1)S(1)}, bf16[2,384,128]{2,1,0:T(8,128)(2,1)}, u32[]{:S(2)}) copy-start(bf16[2,384,128]{2,1,0:T(8,128)(2,1)} %copy-done.4) | copy-start | bytes 589828
  114.5 9.8 %copy-start.9 = (s32[4]{0:T(128)S(1)}, s32[4]{0:T(128)}, u32[]{:S(2)}) copy-start(s32[4]{0:T(128)} %copy-done.8) | copy-start | bytes 52
  114.5 24.3 %collective-permute-start.21 = (bf16[2,768,128]{2,1,0:T(8,128)(2,1)}, bf16[2,768,128]{2,1,0:T(8,128)(2,1)}, u32[]{:S(2)}, u32[]{:S(2)}) collective-permute-start(bf16[2,768,128]{2,1,0:T(8,128)(2,1)} %collective-permute-done.12.rest_2_), channel_id=1, source_target_pairs={{0,1},{1,0},{2,3},{3,2},{4,5},{5,4},{6,7},{7,6},{8,9},{9,8},{10,11... | collective-permute-start | bytes 1179656 | tf_op jit(solution)/shard_map/ppermute | solution.py:440
  123.7 15.1 %collective-permute-start.19 = (bf16[2,384,128]{2,1,0:T(8,128)(2,1)}, bf16[2,384,128]{2,1,0:T(8,128)(2,1)S(1)}, u32[]{:S(2)}, u32[]{:S(2)}) collective-permute-start(bf16[2,384,128]{2,1,0:T(8,128)(2,1)} %collective-permute-done.5.rest_0_), channel_id=1, source_target_pairs={{0,1},{1,0},{2,3},{3,2},{4,5},{5,4},{6,7},{7,6},{8,9},{9,8},{10,11... | collective-permute-start | bytes 589832 | tf_op jit(solution)/shard_map/ppermute | solution.py:440
  124.3 1.0 copy-start.3
  125.3 0.9 copy-start.7
